TPU v7x, 768 devices: a whole 4x8x12 slice. The times are simulated.
768 devices in a mesh: dc: 64 (over x, y, core), tp: 12 (over z).
Axes of the slice: x: 4, y: 8, z: 12, core: 2. Of those that a mesh axis runs over, the one named last changes fastest.
Arguments:
- queries: bfloat16 [12288, 3072], P('dc', 'tp'), may hold values from -15 to 15
- keys: bfloat16 [12288, 768], P('dc'), may hold values from -4.5 to 4.5
- values: bfloat16 [12288, 768], P('dc'), may hold values from -5 to 5
- lengths: int32 [24], replicated, may hold values from 1 to 9216, 12288 in all
- mlp_owner: int32 [12288], replicated, may hold values from 0 to 63, as said below
- out_weight: bfloat16 [3072, 4096], P('tp'), may hold values from -0.109375 to 0.109375
- residual: bfloat16 [12288, 4096], P(('dc', 'tp')), may hold values from -3 to 3
Outputs:
- hidden: bfloat16 [12288, 4096], P(('dc', 'tp'))
Inputs may be any that keep to these rules, and one draw needn't show every extreme that they name: `mlp_owner`: the tokens of any one slab of 192 positions send at most 6 tokens to one owner, and every owner receives exactly 192 tokens.
All inputs are finite; a program needn't handle non-finite values.
Results may differ from a plain program's by a relative error of at most 0.013.
Values may be sent and summed in bfloat16 or wider, within the bound.
No kernel may reach another device: no remote copies, remote signals or barrier semaphores. Data moves between devices by JAX's collectives and lax.ppermute only.
A program may use at most 128 MiB of HBM per device.

v0:
```python
import jax
import jax.numpy as jnp
from jax import lax
from jax.experimental import pallas as pl
from jax.experimental.pallas import tpu as pltpu
from jax.sharding import Mesh, PartitionSpec as P

HEAD = 128
GROUP = 4
NX, NY, NC, NQ, NJ = 4, 8, 2, 4, 3
TOK = 192
DOCS = 24
HEADS_HERE = 2
COLS = HEADS_HERE * HEAD
QROWS = HEADS_HERE * TOK
SLOTS = 6
N_DC = NX * NY * NC
SLOT_TOTAL = N_DC * SLOTS
CHUNK_SLABS = 4
CHUNK = CHUNK_SLABS * TOK
PART = HEAD + 16
LOG2E = 1.4426950408889634
SCALE2 = HEAD**-0.5 * LOG2E
NEG = -1e30
FLOOR = -1e9


NT = (((1,), (1,)), ((), ()))
TN = (((0,), (0,)), ((), ()))


def round_up(v):
    return (v + jnp.abs(v) * 0.0079).astype(jnp.bfloat16).astype(jnp.float32)


def attend_kernel(place, lengths, q_ref, own_ref, peer_ref, out_ref, q_s, m_s, l_s, acc_s):
    x, y, c = place[0], place[1], place[2]

    def empty(xs, carry):
        out_ref[xs, :HEAD, :] = jnp.zeros((HEAD, QROWS), jnp.bfloat16)
        rows = lax.broadcasted_iota(jnp.int32, (PART - HEAD, QROWS), 0)
        out_ref[xs, HEAD:, :] = jnp.where(rows == 0, FLOOR, 0.0).astype(jnp.bfloat16)
        return carry

    lax.fori_loop(0, x, empty, 0)

    def slab(xs, carry):
        p0 = (xs * (NY * NC) + y * NC + c) * TOK
        last = p0 + TOK - 1
        lane = lax.broadcasted_iota(jnp.int32, (1, QROWS), 1)
        pos = p0 + jnp.where(lane >= TOK, lane - TOK, lane)
        start = jnp.zeros((1, QROWS), jnp.int32)
        first_start = jnp.int32(0)
        last_start = jnp.int32(0)
        end = jnp.int32(0)
        for k in range(DOCS):
            end = end + lengths[k]
            start = jnp.where(pos >= end, end, start)
            first_start = jnp.where(p0 >= end, end, first_start)
            last_start = jnp.where(last >= end, end, last_start)
        q_s[:TOK, :] = q_ref[xs, :, :HEAD]
        q_s[TOK:, :] = q_ref[xs, :, HEAD:]
        m_s[...] = jnp.full((1, QROWS), FLOOR, jnp.float32)
        l_s[...] = jnp.zeros((1, QROWS), jnp.float32)
        acc_s[...] = jnp.zeros((HEAD, QROWS), jnp.float32)

        for ref, core in ((own_ref, c), (peer_ref, 1 - c)):

            def chunk(ch, carry, ref=ref, core=core):
                low = ((x * NY + ch * CHUNK_SLABS) * NC + core) * TOK
                high = low + (CHUNK_SLABS - 1) * NC * TOK + TOK - 1
                rows = pl.ds(pl.multiple_of(ch * CHUNK, CHUNK), CHUNK)

                def update(masked):
                    s = lax.dot_general(
                        ref[rows, :HEAD], q_s[...], NT, preferred_element_type=jnp.float32
                    )
                    s = s * SCALE2
                    if masked:
                        at = lax.broadcasted_iota(jnp.int32, (CHUNK, 1), 0)
                        slab_at = jnp.zeros((CHUNK, 1), jnp.int32)
                        for n in range(1, CHUNK_SLABS):
                            slab_at += (at >= n * TOK).astype(jnp.int32)
                        key_pos = low + at + slab_at * ((NC - 1) * TOK)
                        s = jnp.where((key_pos >= start) & (key_pos <= pos), s, NEG)
                    m_old = m_s[...]
                    m_new = jnp.maximum(m_old, round_up(jnp.max(s, axis=0, keepdims=True)))
                    w = jnp.exp2(s - m_new)
                    fix = jnp.exp2(m_old - m_new)
                    m_s[...] = m_new
                    l_s[...] = l_s[...] * fix + jnp.sum(w, axis=0, keepdims=True)
                    acc_s[...] = acc_s[...] * fix + lax.dot_general(
                        ref[rows, HEAD:],
                        w.astype(jnp.bfloat16),
                        TN,
                        preferred_element_type=jnp.float32,
                    )

                needed = (low <= last) & (high >= first_start)
                whole = (high <= p0) & (low >= last_start)

                @pl.when(needed & whole)
                def _():
                    update(False)

                @pl.when(needed & jnp.logical_not(whole))
                def _():
                    update(True)

                return carry

            lax.fori_loop(0, NY // CHUNK_SLABS, chunk, 0)

        out_ref[xs, :HEAD, :] = acc_s[...].astype(jnp.bfloat16)
        total = l_s[...]
        high_part = total.astype(jnp.bfloat16).astype(jnp.float32)
        rows = lax.broadcasted_iota(jnp.int32, (PART - HEAD, QROWS), 0)
        stats = jnp.where(rows == 0, m_s[...], jnp.where(rows == 1, high_part, total - high_part))
        out_ref[xs, HEAD:, :] = stats.astype(jnp.bfloat16)
        return carry

    lax.fori_loop(x, NX, slab, 0)


def merge_kernel(part_ref, row_ref, col_ref, out_ref):
    m = [part_ref[i, HEAD : HEAD + 1, :].astype(jnp.float32) for i in range(NX)]
    top = jnp.maximum(jnp.maximum(m[0], m[1]), jnp.maximum(m[2], m[3]))
    total = jnp.zeros((1, QROWS), jnp.float32)
    mixed = jnp.zeros((HEAD, QROWS), jnp.float32)
    for i in range(NX):
        w = jnp.exp2(m[i] - top)
        part = part_ref[i, HEAD + 1 : HEAD + 2, :].astype(jnp.float32)
        part = part + part_ref[i, HEAD + 2 : HEAD + 3, :].astype(jnp.float32)
        total = total + w * part
        mixed = mixed + w * part_ref[i, :HEAD, :].astype(jnp.float32)
    attention = (mixed / total).astype(jnp.bfloat16)
    target = row_ref[...]
    earlier = lax.broadcasted_iota(jnp.int32, (TOK, TOK), 0) < lax.broadcasted_iota(
        jnp.int32, (TOK, TOK), 1
    )
    same = (col_ref[...] == target) & earlier
    rank = jnp.sum(same.astype(jnp.int32), axis=0, keepdims=True)
    slot = target * SLOTS + rank
    ids = lax.broadcasted_iota(jnp.int32, (SLOT_TOTAL, TOK), 0)
    placement = (ids == slot).astype(jnp.float32).astype(jnp.bfloat16)
    for h in range(HEADS_HERE):
        out_ref[:, h * HEAD : (h + 1) * HEAD] = lax.dot_general(
            placement,
            attention[:, h * TOK : (h + 1) * TOK],
            NT,
            preferred_element_type=jnp.float32,
        ).astype(jnp.bfloat16)


def collect_kernel(me, owner_ref, in_ref, out_ref):
    mine = (owner_ref[...] == me[0]).astype(jnp.float32).astype(jnp.bfloat16)
    count = lax.dot_general(
        jnp.ones((8, TOK), jnp.bfloat16), mine, NT, preferred_element_type=jnp.float32
    ).astype(jnp.bfloat16)
    before = lax.broadcasted_iota(jnp.int32, (N_DC, N_DC), 0) < lax.broadcasted_iota(
        jnp.int32, (N_DC, N_DC), 1
    )
    first = jnp.dot(
        count, before.astype(jnp.float32).astype(jnp.bfloat16), preferred_element_type=jnp.float32
    ).astype(jnp.bfloat16)
    src = lax.broadcasted_iota(jnp.int32, (N_DC, SLOT_TOTAL), 0)
    slot = lax.broadcasted_iota(jnp.int32, (N_DC, SLOT_TOTAL), 1)
    inside = (slot >= src * SLOTS) & (slot < (src + 1) * SLOTS)
    spread = inside.astype(jnp.float32).astype(jnp.bfloat16)
    count = jnp.dot(count, spread, preferred_element_type=jnp.float32)[:1]
    first = jnp.dot(first, spread, preferred_element_type=jnp.float32)[:1]
    k = (slot[:1] % SLOTS).astype(jnp.float32)
    g = jnp.where(k < count, first + k, -1.0).astype(jnp.int32)
    at = lax.broadcasted_iota(jnp.int32, (TOK, 1), 0)
    part = (at >= 64).astype(jnp.int32) + (at >= 128).astype(jnp.int32)
    within = at - 64 * part
    wanted = ((within // 16) * NJ + part) * 16 + within % 16
    chooser = (g == wanted).astype(jnp.float32).astype(jnp.bfloat16)
    out_ref[...] = jnp.dot(chooser, in_ref[...], preferred_element_type=jnp.float32).astype(
        jnp.bfloat16
    )


def project_kernel(place, x_ref, w0, a1, a2, b1, b2, out_ref):
    c, j = place[0], place[1]
    total = jnp.dot(x_ref[j], w0[...], preferred_element_type=jnp.float32)
    for step, near, far in ((1, a1, b1), (2, a2, b2)):
        rows = x_ref[lax.rem(j + NJ - step, NJ)]
        left, right = rows[:, :HEAD], rows[:, HEAD:]
        lo = jnp.where(c == 0, left, right)
        hi = jnp.where(c == 0, right, left)
        total += jnp.dot(lo, near[...], preferred_element_type=jnp.float32)
        total += jnp.dot(hi, far[...], preferred_element_type=jnp.float32)
    rows = TOK // NJ // NQ
    for n in range(NQ):
        out_ref[n] = total[n * rows : (n + 1) * rows].astype(jnp.bfloat16)


def vmem():
    return pl.BlockSpec(memory_space=pltpu.VMEM)


def near_core(array):
    return pltpu.with_memory_space_constraint(array, pltpu.VMEM)


def far_off(array):
    return pltpu.with_memory_space_constraint(array, pltpu.HBM)


def out_here(*shape):
    return pltpu.VMEM(shape, jnp.bfloat16)


def smem():
    return pl.BlockSpec(memory_space=pltpu.SMEM)


def per_device(queries, keys, values, lengths, mlp_owner, out_weight, residual):
    x, y, c = lax.axis_index("x"), lax.axis_index("y"), lax.axis_index("c")
    j = lax.axis_index("j")
    tp = lax.axis_index("q") * NJ + j
    dc = (x * NY + y) * NC + c
    place = jnp.stack([x, y, c]).astype(jnp.int32)
    peer = [(0, 1), (1, 0)]

    kv_at = tp * HEADS_HERE // GROUP * HEAD
    kv = jnp.concatenate(
        [
            lax.dynamic_slice_in_dim(keys, kv_at, HEAD, 1),
            lax.dynamic_slice_in_dim(values, kv_at, HEAD, 1),
        ],
        axis=1,
    )
    copies = jnp.broadcast_to(queries[None], (NX, TOK, COLS))
    q_all = lax.all_to_all(copies, "x", 0, 0, tiled=True)
    own = lax.all_gather(kv, "y", axis=0, tiled=True)
    other = lax.ppermute(own, "c", peer)
    half = lax.dynamic_slice_in_dim(out_weight, c * HEAD, HEAD, 0)
    half, _ = lax.optimization_barrier((half, own))
    near = [lax.ppermute(half, "j", [(i, (i + s) % NJ) for i in range(NJ)]) for s in (1, 2)]

    partial = pl.pallas_call(
        attend_kernel,
        out_shape=out_here(NX, PART, QROWS),
        in_specs=[smem(), smem(), vmem(), vmem(), vmem()],
        out_specs=vmem(),
        scratch_shapes=[
            pltpu.VMEM((QROWS, HEAD), jnp.bfloat16),
            pltpu.VMEM((1, QROWS), jnp.float32),
            pltpu.VMEM((1, QROWS), jnp.float32),
            pltpu.VMEM((HEAD, QROWS), jnp.float32),
        ],
        name="attend",
    )(place, lengths, near_core(q_all), near_core(own), near_core(other))
    parts = lax.all_to_all(partial, "x", 0, 0, tiled=True)

    targets = lax.dynamic_slice_in_dim(mlp_owner, dc * TOK, TOK, 0)
    outgoing = pl.pallas_call(
        merge_kernel,
        out_shape=out_here(SLOT_TOTAL, COLS),
        in_specs=[vmem(), vmem(), vmem()],
        out_specs=vmem(),
        name="merge",
    )(near_core(parts), targets.reshape(1, TOK), targets.reshape(TOK, 1))
    near, _ = lax.optimization_barrier((near, outgoing))
    far = [lax.ppermute(w, "c", peer) for w in near]
    incoming = lax.all_to_all(
        outgoing.reshape(N_DC, SLOTS, COLS), ("x", "y", "c"), 0, 0, tiled=True
    )
    owned = pl.pallas_call(
        collect_kernel,
        out_shape=out_here(TOK, COLS),
        in_specs=[smem(), vmem(), vmem()],
        out_specs=vmem(),
        name="collect",
    )(
        dc.reshape(1).astype(jnp.int32),
        mlp_owner.reshape(N_DC, TOK),
        near_core(incoming.reshape(SLOT_TOTAL, COLS)),
    )
    shared = lax.all_to_all(owned.reshape(NJ, TOK // NJ, COLS), "j", 0, 0, tiled=True)

    width = out_weight.shape[1]
    rows = TOK // NJ
    tile = 1024
    projected = pl.pallas_call(
        project_kernel,
        out_shape=jax.ShapeDtypeStruct((NQ, rows // NQ, width), jnp.bfloat16),
        grid=(width // tile,),
        in_specs=[smem(), vmem(), pl.BlockSpec((COLS, tile), lambda n: (0, n))]
        + [pl.BlockSpec((HEAD, tile), lambda n: (0, n))] * 4,
        out_specs=pl.BlockSpec((NQ, rows // NQ, tile), lambda n: (0, 0, n)),
        name="project",
    )(jnp.stack([c, j]).astype(jnp.int32), near_core(shared), out_weight, *map(far_off, (*near, *far)))
    q = lax.axis_index("q")
    total = lax.dynamic_index_in_dim(projected, q, 0, keepdims=False).astype(jnp.float32)
    for s in (2, 1, 3):
        block = lax.dynamic_index_in_dim(projected, (q + s) % NQ, 0, keepdims=False)
        moved = lax.ppermute(block, "q", [(i, (i + s) % NQ) for i in range(NQ)])
        total += moved.astype(jnp.float32)
    return (total + residual.astype(jnp.float32)).astype(jnp.bfloat16)


def solution(mesh):
    fine = Mesh(mesh.devices.reshape(NX, NY, NC, NQ, NJ), ("x", "y", "c", "q", "j"))
    dcs, tps = ("x", "y", "c"), ("q", "j")
    return jax.shard_map(
        per_device,
        mesh=fine,
        in_specs=(
            P(dcs, tps),
            P(dcs, None),
            P(dcs, None),
            P(),
            P(),
            P(tps, None),
            P(dcs + tps, None),
        ),
        out_specs=P(dcs + tps, None),
        check_vma=False,
    )
```

profile of v0, /device:TPU:6, one launch (start us, length us, event | category | flops | bytes accessed | tf_op | source)
XLA Modules:
  0.0 160.4 jit_solution(12504452895354237977)
XLA Ops:
  0.0 0.9 constant_dynamic-slice_fusion.1
  0.9 27.7 %all_gather.3.own_ref = bf16[1536,256]{1,0:T(8,128)(2,1)S(1)} all-gather(bf16[192,256]{1,0:T(8,128)(2,1)S(1)} %pad_maximum_fusion), channel_id=1, replica_groups=mesh['x'=4,'y'=8,'c'=2,'q'=4,'j'=3] {'y'}, dimensions={0}, use_global_device_ids=true | all-gather | bytes 884736 | tf_op jit(solution)/shard_map/all_gather | solution.py:237
  28.6 1.9 %collective-permute-start = (bf16[1536,256]{1,0:T(8,128)(2,1)S(1)}, bf16[1536,256]{1,0:T(8,128)(2,1)S(1)}, u32[]{:S(2)}, u32[]{:S(2)}) collective-permute-start(bf16[1536,256]{1,0:T(8,128)(2,1)S(1)} %all_gather.3.own_ref), channel_id=1, source_target_pairs={{0,12},{12,0},{1,13},{13,1},{2,14},{14,2},{3,15},{15,3},{4,16},{16... | collective-permute-start | bytes 2359304 | tf_op jit(solution)/shard_map/ppermute | solution.py:238
  30.5 1.3 constant_dynamic-slice_fusion
  31.9 4.3 %collective-permute-start.1 = (bf16[128,4096]{1,0:T(8,128)(2,1)S(1)}, bf16[128,4096]{1,0:T(8,128)(2,1)}, u32[]{:S(2)}, u32[]{:S(2)}) collective-permute-start(bf16[128,4096]{1,0:T(8,128)(2,1)S(1)} %constant_dynamic-slice_fusion), channel_id=1, source_target_pairs={{0,1},{1,2},{2,0},{3,4},{4,5},{5,3},{6,7},{7,8},{8,6},{9,10},{10,1... | collective-permute-start | bytes 3145736 | tf_op jit(solution)/shard_map/ppermute | solution.py:241
  36.2 3.7 %collective-permute-start.2 = (bf16[128,4096]{1,0:T(8,128)(2,1)S(1)}, bf16[128,4096]{1,0:T(8,128)(2,1)}, u32[]{:S(2)}, u32[]{:S(2)}) collective-permute-start(bf16[128,4096]{1,0:T(8,128)(2,1)S(1)} %constant_dynamic-slice_fusion), channel_id=1, source_target_pairs={{0,2},{1,0},{2,1},{3,5},{4,3},{5,4},{6,8},{7,6},{8,7},{9,11},{10,9... | collective-permute-start | bytes 3145736 | tf_op jit(solution)/shard_map/ppermute | solution.py:241
  39.9 0.8 broadcast_in_dim.2
  40.7 9.8 %all-to-all-start = ((bf16[4,192,256]{2,1,0:T(8,128)(2,1)}), bf16[4,192,256]{2,1,0:T(8,128)(2,1)S(1)}, u32[]{:S(2)}, u32[]{:S(2)}) async-start(bf16[4,192,256]{2,1,0:T(8,128)(2,1)} %broadcast_in_dim.2), calls=%async_computation | async-start | bytes 786432 | tf_op jit(solution)/shard_map/all_to_all | solution.py:236
  51.1 5.8 %all-to-all-done.q_ref = bf16[4,192,256]{2,1,0:T(8,128)(2,1)S(1)} async-done(((bf16[4,192,256]{2,1,0:T(8,128)(2,1)}), bf16[4,192,256]{2,1,0:T(8,128)(2,1)S(1)}, u32[]{:S(2)}, u32[]{:S(2)}) %all-to-all-start) | async-done | bytes 393248 | tf_op jit(solution)/shard_map/all_to_all | solution.py:236
  56.9 2.5 %attend.1 = bf16[4,144,384]{2,1,0:T(8,128)(2,1)} custom-call(s32[3]{0:T(128)} %pad_add_fusion.1.place, s32[24]{0:T(128)} %lengths.1, bf16[4,192,256]{2,1,0:T(8,128)(2,1)S(1)} %all-to-all-done.q_ref, bf16[1536,256]{1,0:T(8,128)(2,1)S(1)} %all_gather.3.own_ref, bf16[1536,256]{1,0:T(8,128)(2,1)S(1)} %collective-permute-done.peer_ref), custom_call_target="tpu_custom_call" | custom-call | tf_op jit(solution)/shard_map/attend/pallas_call | solution.py:243
  59.4 11.3 %all-to-all-start.1 = ((bf16[4,144,384]{2,1,0:T(8,128)(2,1)}), bf16[4,144,384]{2,1,0:T(8,128)(2,1)S(1)}, u32[]{:S(2)}, u32[]{:S(2)}) async-start(bf16[4,144,384]{2,1,0:T(8,128)(2,1)} %attend.1), calls=%async_computation.1 | async-start | bytes 884736 | tf_op jit(solution)/shard_map/all_to_all | solution.py:256
  70.8 0.8 copy.8.col_ref
  71.5 6.1 %all-to-all-done.1.part_ref = bf16[4,144,384]{2,1,0:T(8,128)(2,1)S(1)} async-done(((bf16[4,144,384]{2,1,0:T(8,128)(2,1)}), bf16[4,144,384]{2,1,0:T(8,128)(2,1)S(1)}, u32[]{:S(2)}, u32[]{:S(2)}) %all-to-all-start.1) | async-done | bytes 442400 | tf_op jit(solution)/shard_map/all_to_all | solution.py:256
  77.6 1.3 merge.1
  78.9 5.4 %collective-permute-done.2.a2 = bf16[128,4096]{1,0:T(8,128)(2,1)} collective-permute-done((bf16[128,4096]{1,0:T(8,128)(2,1)S(1)}, bf16[128,4096]{1,0:T(8,128)(2,1)}, u32[]{:S(2)}, u32[]{:S(2)}) %collective-permute-start.2) | collective-permute-done | bytes 1048608 | tf_op jit(solution)/shard_map/ppermute | solution.py:241
  84.3 2.0 %collective-permute-start.3 = (bf16[128,4096]{1,0:T(8,128)(2,1)}, bf16[128,4096]{1,0:T(8,128)(2,1)S(1)}, u32[]{:S(2)}, u32[]{:S(2)}) collective-permute-start(bf16[128,4096]{1,0:T(8,128)(2,1)} %collective-permute-done.1.a1), channel_id=1, source_target_pairs={{0,12},{12,0},{1,13},{13,1},{2,14},{14,2},{3,15},{15,3},{4,16},{16... | collective-permute-start | bytes 3145736 | tf_op jit(solution)/shard_map/ppermute | solution.py:267
  86.3 2.3 %collective-permute-start.4 = (bf16[128,4096]{1,0:T(8,128)(2,1)}, bf16[128,4096]{1,0:T(8,128)(2,1)S(1)}, u32[]{:S(2)}, u32[]{:S(2)}) collective-permute-start(bf16[128,4096]{1,0:T(8,128)(2,1)} %collective-permute-done.2.a2), channel_id=1, source_target_pairs={{0,12},{12,0},{1,13},{13,1},{2,14},{14,2},{3,15},{15,3},{4,16},{16... | collective-permute-start | bytes 3145736 | tf_op jit(solution)/shard_map/ppermute | solution.py:267
  88.7 0.8 reshape.28
  89.4 10.4 %all-to-all-start.2 = ((bf16[64,6,256]{2,1,0:T(8,128)(2,1)}), bf16[64,6,256]{2,1,0:T(8,128)(2,1)S(1)}, u32[]{:S(2)}, u32[]{:S(2)}) async-start(bf16[64,6,256]{2,1,0:T(8,128)(2,1)} %reshape.28), calls=%async_computation.2 | async-start | bytes 524288 | tf_op jit(solution)/shard_map/all_to_all | solution.py:268
  100.5 10.8 %all-to-all-done.2 = bf16[64,6,256]{2,1,0:T(8,128)(2,1)S(1)} async-done(((bf16[64,6,256]{2,1,0:T(8,128)(2,1)}), bf16[64,6,256]{2,1,0:T(8,128)(2,1)S(1)}, u32[]{:S(2)}, u32[]{:S(2)}) %all-to-all-start.2) | async-done | bytes 196640 | tf_op jit(solution)/shard_map/all_to_all | solution.py:268
  111.4 2.0 %collect.1 = bf16[192,256]{1,0:T(8,128)(2,1)} custom-call(s32[1]{0:T(128)} %bitcast.2.me, s32[64,192]{1,0:T(8,128)} %reshape.25.owner_ref, bf16[384,256]{1,0:T(8,128)(2,1)S(1)} %reshape.29.in_ref), custom_call_target="tpu_custom_call" | custom-call | tf_op jit(solution)/shard_map/collect/pallas_call | solution.py:271
  113.5 3.3 %all-to-all-start.3 = ((bf16[3,64,256]{2,1,0:T(8,128)(2,1)}), bf16[3,64,256]{2,1,0:T(8,128)(2,1)S(1)}, u32[]{:S(2)}, u32[]{:S(2)}) async-start(bf16[3,64,256]{2,1,0:T(8,128)(2,1)} %bitcast.7), calls=%async_computation.3 | async-start | bytes 196608 | tf_op jit(solution)/shard_map/all_to_all | solution.py:282
  117.4 4.3 %all-to-all-done.3.x_ref = bf16[3,64,256]{2,1,0:T(8,128)(2,1)S(1)} async-done(((bf16[3,64,256]{2,1,0:T(8,128)(2,1)}), bf16[3,64,256]{2,1,0:T(8,128)(2,1)S(1)}, u32[]{:S(2)}, u32[]{:S(2)}) %all-to-all-start.3) | async-done | bytes 98336 | tf_op jit(solution)/shard_map/all_to_all | solution.py:282
  121.8 1.0 copy-done
  122.8 1.0 copy-done.1
  123.7 4.9 %project.1 = bf16[4,16,4096]{2,1,0:T(8,128)(2,1)} custom-call(s32[2]{0:T(128)} %pad_add_fusion.place, bf16[3,64,256]{2,1,0:T(8,128)(2,1)S(1)} %all-to-all-done.3.x_ref, bf16[256,4096]{1,0:T(8,128)(2,1)} %w0.1, bf16[128,4096]{1,0:T(8,128)(2,1)} %collective-permute-done.1.a1, bf16[128,4096]{1,0:T(8,128)(2,1)} %collective-permute-done.2.a2, ...), custom_call_target="tpu_custom_call" | custom-call | tf_op jit(solution)/shard_map/project/pallas_call | solution.py:287
  128.7 1.1 dynamic-slice_bitcast_fusion.2
  129.7 14.9 %collective-permute-start.5 = (bf16[16,4096]{1,0:T(8,128)(2,1)S(1)}, bf16[16,4096]{1,0:T(8,128)(2,1)S(1)}, u32[]{:S(2)}, u32[]{:S(2)}) collective-permute-start(bf16[16,4096]{1,0:T(8,128)(2,1)S(1)} %get-tuple-element.11), channel_id=1, source_target_pairs={{0,6},{3,9},{6,0},{9,3},{1,7},{4,10},{7,1},{10,4},{2,8},{5,11},{8,... | collective-permute-start | bytes 393224 | tf_op jit(solution)/shard_map/ppermute | solution.py:300
  144.6 2.7 %collective-permute-start.6 = (bf16[16,4096]{1,0:T(8,128)(2,1)S(1)}, bf16[16,4096]{1,0:T(8,128)(2,1)S(1)}, u32[]{:S(2)}, u32[]{:S(2)}) collective-permute-start(bf16[16,4096]{1,0:T(8,128)(2,1)S(1)} %get-tuple-element.13), channel_id=1, source_target_pairs={{0,3},{3,6},{6,9},{9,0},{1,4},{4,7},{7,10},{10,1},{2,5},{5,8},{8,1... | collective-permute-start | bytes 393224 | tf_op jit(solution)/shard_map/ppermute | solution.py:300
  147.3 6.1 %collective-permute-start.7 = (bf16[16,4096]{1,0:T(8,128)(2,1)S(1)}, bf16[16,4096]{1,0:T(8,128)(2,1)S(1)}, u32[]{:S(2)}, u32[]{:S(2)}) collective-permute-start(bf16[16,4096]{1,0:T(8,128)(2,1)S(1)} %get-tuple-element.12), channel_id=1, source_target_pairs={{0,9},{3,0},{6,3},{9,6},{1,10},{4,1},{7,4},{10,7},{2,11},{5,2},{8,... | collective-permute-start | bytes 393224 | tf_op jit(solution)/shard_map/ppermute | solution.py:300
  153.5 4.7 %collective-permute-done.6 = bf16[16,4096]{1,0:T(8,128)(2,1)S(1)} collective-permute-done((bf16[16,4096]{1,0:T(8,128)(2,1)S(1)}, bf16[16,4096]{1,0:T(8,128)(2,1)S(1)}, u32[]{:S(2)}, u32[]{:S(2)}) %collective-permute-start.6) | collective-permute-done | bytes 131104 | tf_op jit(solution)/shard_map/ppermute | solution.py:300
  158.8 1.6 %fusion.3 = bf16[16,4096]{1,0:T(8,128)(2,1)} fusion(bf16[16,4096]{1,0:T(8,128)(2,1)S(1)} %copy-done.2, bf16[16,4096]{1,0:T(8,128)(2,1)S(1)} %collective-permute-done.7, bf16[16,4096]{1,0:T(8,128)(2,1)S(1)} %collective-permute-done.6, bf16[16,4096]{1,0:T(8,128)(2,1)S(1)} %collective-permute-done.5, bf16[4,16,4096]{2,1,0:T(8,128)(2,1)} %project.1, s32[]{:T(128)S(6)} %select_n.46), kind=kLoop, calls=%fused_computation.4 | loop fusion | flops 655360 | bytes 786436 | tf_op jit(solution)/shard_map/convert_element_type | solution.py:302
  (22 shorter events, 2.7 us)
Async XLA Ops:
  0.0 39.9 %copy-start.3 = (bf16[192,256]{1,0:T(8,128)(2,1)S(1)}, bf16[192,256]{1,0:T(8,128)(2,1)}, u32[]{:S(2)}) copy-start(bf16[192,256]{1,0:T(8,128)(2,1)} %param.7) | copy-start | bytes 294916
  28.6 28.3 %collective-permute-start = (bf16[1536,256]{1,0:T(8,128)(2,1)S(1)}, bf16[1536,256]{1,0:T(8,128)(2,1)S(1)}, u32[]{:S(2)}, u32[]{:S(2)}) collective-permute-start(bf16[1536,256]{1,0:T(8,128)(2,1)S(1)} %all_gather.3.own_ref), channel_id=1, source_target_pairs={{0,12},{12,0},{1,13},{13,1},{2,14},{14,2},{3,15},{15,3},{4,16},{16... | collective-permute-start | bytes 2359304 | tf_op jit(solution)/shard_map/ppermute | solution.py:238
  31.9 47.0 %collective-permute-start.1 = (bf16[128,4096]{1,0:T(8,128)(2,1)S(1)}, bf16[128,4096]{1,0:T(8,128)(2,1)}, u32[]{:S(2)}, u32[]{:S(2)}) collective-permute-start(bf16[128,4096]{1,0:T(8,128)(2,1)S(1)} %constant_dynamic-slice_fusion), channel_id=1, source_target_pairs={{0,1},{1,2},{2,0},{3,4},{4,5},{5,3},{6,7},{7,8},{8,6},{9,10},{10,1... | collective-permute-start | bytes 3145736 | tf_op jit(solution)/shard_map/ppermute | solution.py:241
  36.2 48.2 %collective-permute-start.2 = (bf16[128,4096]{1,0:T(8,128)(2,1)S(1)}, bf16[128,4096]{1,0:T(8,128)(2,1)}, u32[]{:S(2)}, u32[]{:S(2)}) collective-permute-start(bf16[128,4096]{1,0:T(8,128)(2,1)S(1)} %constant_dynamic-slice_fusion), channel_id=1, source_target_pairs={{0,2},{1,0},{2,1},{3,5},{4,3},{5,4},{6,8},{7,6},{8,7},{9,11},{10,9... | collective-permute-start | bytes 3145736 | tf_op jit(solution)/shard_map/ppermute | solution.py:241
  40.7 30.0 %copy-start.4 = (s32[12288]{0:T(1024)S(1)}, s32[12288]{0:T(1024)}, u32[]{:S(2)}) copy-start(s32[12288]{0:T(1024)} %param.11) | copy-start | bytes 147460
  40.7 16.2 %all-to-all-start = ((bf16[4,192,256]{2,1,0:T(8,128)(2,1)}), bf16[4,192,256]{2,1,0:T(8,128)(2,1)S(1)}, u32[]{:S(2)}, u32[]{:S(2)}) async-start(bf16[4,192,256]{2,1,0:T(8,128)(2,1)} %broadcast_in_dim.2), calls=%async_computation | async-start | bytes 786432 | tf_op jit(solution)/shard_map/all_to_all | solution.py:236
  59.4 18.2 %all-to-all-start.1 = ((bf16[4,144,384]{2,1,0:T(8,128)(2,1)}), bf16[4,144,384]{2,1,0:T(8,128)(2,1)S(1)}, u32[]{:S(2)}, u32[]{:S(2)}) async-start(bf16[4,144,384]{2,1,0:T(8,128)(2,1)} %attend.1), calls=%async_computation.1 | async-start | bytes 884736 | tf_op jit(solution)/shard_map/all_to_all | solution.py:256
  70.8 6.9 %copy-start.5 = (s32[192]{0:T(256)}, s32[192]{0:T(256)S(1)}, u32[]{:S(2)}) copy-start(s32[192]{0:T(256)S(1)} %dynamic_slice.27) | copy-start | bytes 2308
  84.3 37.4 %collective-permute-start.3 = (bf16[128,4096]{1,0:T(8,128)(2,1)}, bf16[128,4096]{1,0:T(8,128)(2,1)S(1)}, u32[]{:S(2)}, u32[]{:S(2)}) collective-permute-start(bf16[128,4096]{1,0:T(8,128)(2,1)} %collective-permute-done.1.a1), channel_id=1, source_target_pairs={{0,12},{12,0},{1,13},{13,1},{2,14},{14,2},{3,15},{15,3},{4,16},{16... | collective-permute-start | bytes 3145736 | tf_op jit(solution)/shard_map/ppermute | solution.py:267
  86.3 35.5 %collective-permute-start.4 = (bf16[128,4096]{1,0:T(8,128)(2,1)}, bf16[128,4096]{1,0:T(8,128)(2,1)S(1)}, u32[]{:S(2)}, u32[]{:S(2)}) collective-permute-start(bf16[128,4096]{1,0:T(8,128)(2,1)} %collective-permute-done.2.a2), channel_id=1, source_target_pairs={{0,12},{12,0},{1,13},{13,1},{2,14},{14,2},{3,15},{15,3},{4,16},{16... | collective-permute-start | bytes 3145736 | tf_op jit(solution)/shard_map/ppermute | solution.py:267
  89.4 21.9 %all-to-all-start.2 = ((bf16[64,6,256]{2,1,0:T(8,128)(2,1)}), bf16[64,6,256]{2,1,0:T(8,128)(2,1)S(1)}, u32[]{:S(2)}, u32[]{:S(2)}) async-start(bf16[64,6,256]{2,1,0:T(8,128)(2,1)} %reshape.28), calls=%async_computation.2 | async-start | bytes 524288 | tf_op jit(solution)/shard_map/all_to_all | solution.py:268
  113.5 8.3 %all-to-all-start.3 = ((bf16[3,64,256]{2,1,0:T(8,128)(2,1)}), bf16[3,64,256]{2,1,0:T(8,128)(2,1)S(1)}, u32[]{:S(2)}, u32[]{:S(2)}) async-start(bf16[3,64,256]{2,1,0:T(8,128)(2,1)} %bitcast.7), calls=%async_computation.3 | async-start | bytes 196608 | tf_op jit(solution)/shard_map/all_to_all | solution.py:282
  117.4 41.4 %copy-start.2 = (bf16[16,4096]{1,0:T(8,128)(2,1)S(1)}, bf16[16,4096]{1,0:T(8,128)(2,1)}, u32[]{:S(2)}) copy-start(bf16[16,4096]{1,0:T(8,128)(2,1)} %param.13) | copy-start | bytes 393220
  121.8 1.0 copy-start
  122.8 1.0 copy-start.1
  129.7 23.8 %collective-permute-start.5 = (bf16[16,4096]{1,0:T(8,128)(2,1)S(1)}, bf16[16,4096]{1,0:T(8,128)(2,1)S(1)}, u32[]{:S(2)}, u32[]{:S(2)}) collective-permute-start(bf16[16,4096]{1,0:T(8,128)(2,1)S(1)} %get-tuple-element.11), channel_id=1, source_target_pairs={{0,6},{3,9},{6,0},{9,3},{1,7},{4,10},{7,1},{10,4},{2,8},{5,11},{8,... | collective-permute-start | bytes 393224 | tf_op jit(solution)/shard_map/ppermute | solution.py:300
  144.6 13.5 %collective-permute-start.6 = (bf16[16,4096]{1,0:T(8,128)(2,1)S(1)}, bf16[16,4096]{1,0:T(8,128)(2,1)S(1)}, u32[]{:S(2)}, u32[]{:S(2)}) collective-permute-start(bf16[16,4096]{1,0:T(8,128)(2,1)S(1)} %get-tuple-element.13), channel_id=1, source_target_pairs={{0,3},{3,6},{6,9},{9,0},{1,4},{4,7},{7,10},{10,1},{2,5},{5,8},{8,1... | collective-permute-start | bytes 393224 | tf_op jit(solution)/shard_map/ppermute | solution.py:300
  147.3 11.4 %collective-permute-start.7 = (bf16[16,4096]{1,0:T(8,128)(2,1)S(1)}, bf16[16,4096]{1,0:T(8,128)(2,1)S(1)}, u32[]{:S(2)}, u32[]{:S(2)}) collective-permute-start(bf16[16,4096]{1,0:T(8,128)(2,1)S(1)} %get-tuple-element.12), channel_id=1, source_target_pairs={{0,9},{3,0},{6,3},{9,6},{1,10},{4,1},{7,4},{10,7},{2,11},{5,2},{8,... | collective-permute-start | bytes 393224 | tf_op jit(solution)/shard_map/ppermute | solution.py:300
where the time goes:
time: 163 us; the launch traced here: 160 us
  starting transfers between devices  72.7 us (45%)
  waiting for transfers between devices  37.8 us (23%)
  blocking collectives  27.7 us (17%)
  Pallas kernels  10.8 us (7%)
  local copies, waits for them, and re-layouts  8.34 us (5%)
  other arithmetic  2.82 us (2%)
    all_gather x1, blocking collectives, per_device(): own = lax.all_gather(kv, 'y', axis=0, tiled=True)  27.7 us
    ppermute x3, starting transfers between devices, per_device(): moved = lax.ppermute(block, 'q', [(i, (i + s) % NQ) for i in range(NQ)])  23.7 us
    all_to_all x1, starting transfers between devices, per_device(): parts = lax.all_to_all(partial, 'x', 0, 0, tiled=True)  11.3 us
    all_to_all x1, waiting for transfers between devices, per_device(): lax.all_to_all(outgoing.reshape(N_DC, SLOTS, COLS), ('x', 'y', 'c'), 0, 0...  10.8 us
    all_to_all x1, starting transfers between devices, per_device(): lax.all_to_all(outgoing.reshape(N_DC, SLOTS, COLS), ('x', 'y', 'c'), 0, 0...  10.4 us
    all_to_all x1, starting transfers between devices, per_device(): q_all = lax.all_to_all(copies, 'x', 0, 0, tiled=True)  9.82 us
    ppermute x2, starting transfers between devices, per_device(): lax.ppermute(half, 'j', [(i, (i + s) % NJ) for i in range(NJ)])  8.01 us
    all_to_all x1, waiting for transfers between devices, per_device(): parts = lax.all_to_all(partial, 'x', 0, 0, tiled=True)  6.09 us
  transfers between devices with their start and end apart: 12, of which 7 were waited for; matrix products, arithmetic and copies ran while one was open for 4% of the time, Pallas kernels for 4%

commit v1 on v0

--- a/solution.py
+++ b/solution.py
@@ -14,6 +14,8 @@
 COLS = HEADS_HERE * HEAD
 QROWS = HEADS_HERE * TOK
 SLOTS = 6
+PADDED = 8
+OUT = TOK // (NQ * NJ)
 N_DC = NX * NY * NC
 SLOT_TOTAL = N_DC * SLOTS
 CHUNK_SLABS = 4
@@ -122,7 +124,19 @@
     lax.fori_loop(x, NX, slab, 0)
 
 
-def merge_kernel(part_ref, row_ref, col_ref, out_ref):
+def place_kernel(row_ref, col_ref, out_ref):
+    target = row_ref[...]
+    earlier = lax.broadcasted_iota(jnp.int32, (TOK, TOK), 0) < lax.broadcasted_iota(
+        jnp.int32, (TOK, TOK), 1
+    )
+    same = (col_ref[...] == target) & earlier
+    rank = jnp.sum(same.astype(jnp.int32), axis=0, keepdims=True)
+    slot = target * PADDED + rank
+    ids = lax.broadcasted_iota(jnp.int32, (N_DC * PADDED, TOK), 0)
+    out_ref[...] = (ids == slot).astype(jnp.float32).astype(jnp.bfloat16)
+
+
+def merge_kernel(placement, part_ref, out_ref):
     m = [part_ref[i, HEAD : HEAD + 1, :].astype(jnp.float32) for i in range(NX)]
     top = jnp.maximum(jnp.maximum(m[0], m[1]), jnp.maximum(m[2], m[3]))
     total = jnp.zeros((1, QROWS), jnp.float32)
@@ -134,25 +148,18 @@
         total = total + w * part
         mixed = mixed + w * part_ref[i, :HEAD, :].astype(jnp.float32)
     attention = (mixed / total).astype(jnp.bfloat16)
-    target = row_ref[...]
-    earlier = lax.broadcasted_iota(jnp.int32, (TOK, TOK), 0) < lax.broadcasted_iota(
-        jnp.int32, (TOK, TOK), 1
-    )
-    same = (col_ref[...] == target) & earlier
-    rank = jnp.sum(same.astype(jnp.int32), axis=0, keepdims=True)
-    slot = target * SLOTS + rank
-    ids = lax.broadcasted_iota(jnp.int32, (SLOT_TOTAL, TOK), 0)
-    placement = (ids == slot).astype(jnp.float32).astype(jnp.bfloat16)
     for h in range(HEADS_HERE):
-        out_ref[:, h * HEAD : (h + 1) * HEAD] = lax.dot_general(
-            placement,
+        rows = lax.dot_general(
+            placement[...],
             attention[:, h * TOK : (h + 1) * TOK],
             NT,
             preferred_element_type=jnp.float32,
-        ).astype(jnp.bfloat16)
-
-
-def collect_kernel(me, owner_ref, in_ref, out_ref):
+        )
+        rows = rows.reshape(N_DC, PADDED, HEAD)[:, :SLOTS, :]
+        out_ref[:, :, h * HEAD : (h + 1) * HEAD] = rows.astype(jnp.bfloat16)
+
+
+def choose_kernel(me, owner_ref, out_ref):
     mine = (owner_ref[...] == me[0]).astype(jnp.float32).astype(jnp.bfloat16)
     count = lax.dot_general(
         jnp.ones((8, TOK), jnp.bfloat16), mine, NT, preferred_element_type=jnp.float32
@@ -175,25 +182,38 @@
     part = (at >= 64).astype(jnp.int32) + (at >= 128).astype(jnp.int32)
     within = at - 64 * part
     wanted = ((within // 16) * NJ + part) * 16 + within % 16
-    chooser = (g == wanted).astype(jnp.float32).astype(jnp.bfloat16)
-    out_ref[...] = jnp.dot(chooser, in_ref[...], preferred_element_type=jnp.float32).astype(
+    out_ref[...] = (g == wanted).astype(jnp.float32).astype(jnp.bfloat16)
+
+
+def collect_kernel(chooser, in_ref, out_ref):
+    out_ref[...] = jnp.dot(chooser[...], in_ref[...], preferred_element_type=jnp.float32).astype(
         jnp.bfloat16
     )
 
 
-def project_kernel(place, x_ref, w0, a1, a2, b1, b2, out_ref):
-    c, j = place[0], place[1]
-    total = jnp.dot(x_ref[j], w0[...], preferred_element_type=jnp.float32)
+def project_kernel(place, x_ref, w0, a1, a2, b1, b2, own_ref, next_ref, prev_ref, c1_ref, c2_ref):
+    c, j, q = place[0], place[1], place[2]
+
+    def rows_of(member):
+        turned = [
+            x_ref[member, pl.ds(pl.multiple_of(lax.rem(q + s, NQ) * OUT, OUT), OUT), :]
+            for s in range(NQ)
+        ]
+        return jnp.concatenate(turned, axis=0)
+
+    total = jnp.dot(rows_of(j), w0[...], preferred_element_type=jnp.float32)
     for step, near, far in ((1, a1, b1), (2, a2, b2)):
-        rows = x_ref[lax.rem(j + NJ - step, NJ)]
+        rows = rows_of(lax.rem(j + NJ - step, NJ))
         left, right = rows[:, :HEAD], rows[:, HEAD:]
         lo = jnp.where(c == 0, left, right)
         hi = jnp.where(c == 0, right, left)
         total += jnp.dot(lo, near[...], preferred_element_type=jnp.float32)
         total += jnp.dot(hi, far[...], preferred_element_type=jnp.float32)
-    rows = TOK // NJ // NQ
-    for n in range(NQ):
-        out_ref[n] = total[n * rows : (n + 1) * rows].astype(jnp.bfloat16)
+    own_ref[...] = total[:OUT]
+    next_ref[...] = total[OUT : 2 * OUT]
+    c1_ref[...] = total[2 * OUT : 2 * OUT + OUT // 2].astype(jnp.bfloat16)
+    c2_ref[...] = total[2 * OUT + OUT // 2 : 3 * OUT].astype(jnp.bfloat16)
+    prev_ref[...] = total[3 * OUT :]
 
 
 def vmem():
@@ -216,13 +236,20 @@
     return pl.BlockSpec(memory_space=pltpu.SMEM)
 
 
+def kernel(body, shapes, in_specs, **more):
+    return pl.pallas_call(body, out_shape=shapes, in_specs=in_specs, out_specs=vmem(), **more)
+
+
 def per_device(queries, keys, values, lengths, mlp_owner, out_weight, residual):
     x, y, c = lax.axis_index("x"), lax.axis_index("y"), lax.axis_index("c")
-    j = lax.axis_index("j")
-    tp = lax.axis_index("q") * NJ + j
+    q, j = lax.axis_index("q"), lax.axis_index("j")
+    tp = q * NJ + j
     dc = (x * NY + y) * NC + c
     place = jnp.stack([x, y, c]).astype(jnp.int32)
     peer = [(0, 1), (1, 0)]
+
+    def turn(size, step):
+        return [(i, (i + step) % size) for i in range(size)]
 
     kv_at = tp * HEADS_HERE // GROUP * HEAD
     kv = jnp.concatenate(
@@ -236,75 +263,78 @@
     q_all = lax.all_to_all(copies, "x", 0, 0, tiled=True)
     own = lax.all_gather(kv, "y", axis=0, tiled=True)
     other = lax.ppermute(own, "c", peer)
+
     half = lax.dynamic_slice_in_dim(out_weight, c * HEAD, HEAD, 0)
     half, _ = lax.optimization_barrier((half, own))
-    near = [lax.ppermute(half, "j", [(i, (i + s) % NJ) for i in range(NJ)]) for s in (1, 2)]
-
-    partial = pl.pallas_call(
+    near2 = lax.ppermute(half, "j", turn(NJ, 2))
+
+    partial = kernel(
         attend_kernel,
-        out_shape=out_here(NX, PART, QROWS),
-        in_specs=[smem(), smem(), vmem(), vmem(), vmem()],
-        out_specs=vmem(),
+        out_here(NX, PART, QROWS),
+        [smem(), smem(), vmem(), vmem(), vmem()],
         scratch_shapes=[
             pltpu.VMEM((QROWS, HEAD), jnp.bfloat16),
             pltpu.VMEM((1, QROWS), jnp.float32),
             pltpu.VMEM((1, QROWS), jnp.float32),
             pltpu.VMEM((HEAD, QROWS), jnp.float32),
         ],
-        name="attend",
     )(place, lengths, near_core(q_all), near_core(own), near_core(other))
+    half, _ = lax.optimization_barrier((half, partial))
+    near1 = lax.ppermute(half, "j", turn(NJ, 1))
     parts = lax.all_to_all(partial, "x", 0, 0, tiled=True)
 
     targets = lax.dynamic_slice_in_dim(mlp_owner, dc * TOK, TOK, 0)
-    outgoing = pl.pallas_call(
-        merge_kernel,
-        out_shape=out_here(SLOT_TOTAL, COLS),
-        in_specs=[vmem(), vmem(), vmem()],
-        out_specs=vmem(),
-        name="merge",
-    )(near_core(parts), targets.reshape(1, TOK), targets.reshape(TOK, 1))
-    near, _ = lax.optimization_barrier((near, outgoing))
-    far = [lax.ppermute(w, "c", peer) for w in near]
-    incoming = lax.all_to_all(
-        outgoing.reshape(N_DC, SLOTS, COLS), ("x", "y", "c"), 0, 0, tiled=True
-    )
-    owned = pl.pallas_call(
-        collect_kernel,
-        out_shape=out_here(TOK, COLS),
-        in_specs=[smem(), vmem(), vmem()],
-        out_specs=vmem(),
-        name="collect",
-    )(
-        dc.reshape(1).astype(jnp.int32),
-        mlp_owner.reshape(N_DC, TOK),
-        near_core(incoming.reshape(SLOT_TOTAL, COLS)),
-    )
+    placement = kernel(place_kernel, out_here(N_DC * PADDED, TOK), [vmem(), vmem()])(
+        targets.reshape(1, TOK), targets.reshape(TOK, 1)
+    )
+    outgoing = kernel(
+        merge_kernel, out_here(N_DC, SLOTS, COLS), [vmem(), vmem()]
+    )(near_core(placement), near_core(parts))
+    incoming = lax.all_to_all(outgoing, ("x", "y", "c"), 0, 0, tiled=True)
+    chooser = kernel(choose_kernel, out_here(TOK, SLOT_TOTAL), [smem(), vmem()])(
+        dc.reshape(1).astype(jnp.int32), mlp_owner.reshape(N_DC, TOK)
+    )
+    owned = kernel(collect_kernel, out_here(TOK, COLS), [vmem(), vmem()])(
+        near_core(chooser), near_core(incoming.reshape(SLOT_TOTAL, COLS))
+    )
+    near2, _ = lax.optimization_barrier((near2, outgoing))
+    far2 = lax.ppermute(near2, "c", peer)
+    near1, _ = lax.optimization_barrier((near1, owned))
+    far1 = lax.ppermute(near1, "c", peer)
     shared = lax.all_to_all(owned.reshape(NJ, TOK // NJ, COLS), "j", 0, 0, tiled=True)
 
     width = out_weight.shape[1]
-    rows = TOK // NJ
     tile = 1024
-    projected = pl.pallas_call(
+    blocks = [(OUT, jnp.float32)] * 3 + [(OUT // 2, jnp.bfloat16)] * 2
+    mine, ahead, behind, c1, c2 = pl.pallas_call(
         project_kernel,
-        out_shape=jax.ShapeDtypeStruct((NQ, rows // NQ, width), jnp.bfloat16),
+        out_shape=[jax.ShapeDtypeStruct((n, width), t) for n, t in blocks],
         grid=(width // tile,),
         in_specs=[smem(), vmem(), pl.BlockSpec((COLS, tile), lambda n: (0, n))]
         + [pl.BlockSpec((HEAD, tile), lambda n: (0, n))] * 4,
-        out_specs=pl.BlockSpec((NQ, rows // NQ, tile), lambda n: (0, 0, n)),
+        out_specs=[pl.BlockSpec((n, tile), lambda n: (0, n)) for n, _ in blocks],
         name="project",
-    )(jnp.stack([c, j]).astype(jnp.int32), near_core(shared), out_weight, *map(far_off, (*near, *far)))
-    q = lax.axis_index("q")
-    total = lax.dynamic_index_in_dim(projected, q, 0, keepdims=False).astype(jnp.float32)
-    for s in (2, 1, 3):
-        block = lax.dynamic_index_in_dim(projected, (q + s) % NQ, 0, keepdims=False)
-        moved = lax.ppermute(block, "q", [(i, (i + s) % NQ) for i in range(NQ)])
-        total += moved.astype(jnp.float32)
+    )(
+        jnp.stack([c, j, q]).astype(jnp.int32),
+        near_core(shared),
+        out_weight,
+        *map(far_off, (near1, near2, far1, far2)),
+    )
+    c1 = lax.ppermute(c1, "q", turn(NQ, 1))
+    c2 = lax.ppermute(c2, "q", turn(NQ, 3))
+    h = OUT // 2
+    ahead = jnp.concatenate([ahead[:h] + c1.astype(jnp.float32), ahead[h:]]).astype(jnp.bfloat16)
+    behind = jnp.concatenate([behind[:h], behind[h:] + c2.astype(jnp.float32)]).astype(jnp.bfloat16)
+    ahead = lax.ppermute(ahead, "q", turn(NQ, 1))
+    behind = lax.ppermute(behind, "q", turn(NQ, 3))
+    total = mine + ahead.astype(jnp.float32) + behind.astype(jnp.float32)
     return (total + residual.astype(jnp.float32)).astype(jnp.bfloat16)
 
 
 def solution(mesh):
     fine = Mesh(mesh.devices.reshape(NX, NY, NC, NQ, NJ), ("x", "y", "c", "q", "j"))
     dcs, tps = ("x", "y", "c"), ("q", "j")
+
     return jax.shard_map(
         per_device,
         mesh=fine,

time: 163 us -> 149 us (0.914)
  starting transfers between devices: 72.7 us -> 61.7 us
  waiting for transfers between devices: 37.8 us -> 33.1 us
  other arithmetic: 2.82 us -> 4.86 us
    all_to_all x1, waiting for transfers between devices: 10.8 us -> 0.01 us  [per_device(): incoming = lax.all_to_all(outgoing, ('x', 'y', 'c'), 0, 0, tiled=True)]
    ppermute x7 -> x8, waiting for transfers between devices: 10.7 us -> 21.3 us  [the longest x1 11.6 us: per_device(): near2 = lax.ppermute(half, 'j', turn(NJ, 2))]
    ppermute x7 -> x8, starting transfers between devices: 36.1 us -> 26.9 us  [the longest x1 7.43 us: per_device(): c2 = lax.ppermute(c2, 'q', turn(NQ, 3))]
    all_to_all x1, waiting for transfers between devices: 5.83 us -> 1.92 us  [per_device(): q_all = lax.all_to_all(copies, 'x', 0, 0, tiled=True)]
    all_to_all x1, starting transfers between devices: 10.4 us -> 7.45 us  [per_device(): incoming = lax.all_to_all(outgoing, ('x', 'y', 'c'), 0, 0, tiled=True)]
    unnamed x12 -> x10, local copies, waits for them, and re-layouts: 1.95 us -> 0.02 us
    another operation x1 -> x3, other arithmetic: 0.61 us -> 2.5 us  [per_device(): jnp.stack([c, j]).astype(jnp.int32)]
    slice x0 -> x2, local copies, waits for them, and re-layouts: none -> 1.82 us  [the longest x1 0.91 us: per_device(): ahead[h:]]
  transfers between devices with their start and end apart: 12 -> 13, of which waited for: 7 -> 7; matrix products, arithmetic and copies ran while one was open for 4% -> 7% of each run, Pallas kernels for 4% -> 5%
where the time goes in v1:
time: 149 us; the launch traced here: 148 us
  starting transfers between devices  61.7 us (41%)
  waiting for transfers between devices  33.1 us (22%)
  blocking collectives  27.7 us (19%)
  Pallas kernels  11.8 us (8%)
  local copies, waits for them, and re-layouts  8.29 us (6%)
  other arithmetic  4.86 us (3%)
    all_gather x1, blocking collectives, per_device(): own = lax.all_gather(kv, 'y', axis=0, tiled=True)  27.7 us
    ppermute x1, waiting for transfers between devices, per_device(): near2 = lax.ppermute(half, 'j', turn(NJ, 2))  11.6 us
    all_to_all x1, starting transfers between devices, per_device(): parts = lax.all_to_all(partial, 'x', 0, 0, tiled=True)  11.2 us
    all_to_all x1, starting transfers between devices, per_device(): q_all = lax.all_to_all(copies, 'x', 0, 0, tiled=True)  11 us
    all_to_all x1, starting transfers between devices, per_device(): incoming = lax.all_to_all(outgoing, ('x', 'y', 'c'), 0, 0, tiled=True)  7.45 us
    ppermute x1, starting transfers between devices, per_device(): c2 = lax.ppermute(c2, 'q', turn(NQ, 3))  7.43 us
    ppermute x1, starting transfers between devices, per_device(): behind = lax.ppermute(behind, 'q', turn(NQ, 3))  7.26 us
    all_to_all x1, waiting for transfers between devices, per_device(): parts = lax.all_to_all(partial, 'x', 0, 0, tiled=True)  5.53 us
  transfers between devices with their start and end apart: 13, of which 7 were waited for; matrix products, arithmetic and copies ran while one was open for 7% of the time, Pallas kernels for 5%

profile of v1, /device:TPU:6, one launch (start us, length us, event | category | flops | bytes accessed | tf_op | source)
XLA Modules:
  0.0 147.7 jit_solution(7027900834255117473)
XLA Ops:
  0.8 27.7 %all_gather.3.own_ref = bf16[1536,256]{1,0:T(8,128)(2,1)S(1)} all-gather(bf16[192,256]{1,0:T(8,128)(2,1)S(1)} %pad_maximum_fusion.2), channel_id=1, replica_groups=mesh['x'=4,'y'=8,'c'=2,'q'=4,'j'=3] {'y'}, dimensions={0}, use_global_device_ids=true | all-gather | bytes 884736 | tf_op jit(solution)/shard_map/all_gather | solution.py:264
  28.6 1.9 %collective-permute-start = (bf16[1536,256]{1,0:T(8,128)(2,1)S(1)}, bf16[1536,256]{1,0:T(8,128)(2,1)S(1)}, u32[]{:S(2)}, u32[]{:S(2)}) collective-permute-start(bf16[1536,256]{1,0:T(8,128)(2,1)S(1)} %all_gather.3.own_ref), channel_id=1, source_target_pairs={{0,12},{12,0},{1,13},{13,1},{2,14},{14,2},{3,15},{15,3},{4,16},{16... | collective-permute-start | bytes 2359304 | tf_op jit(solution)/shard_map/ppermute | solution.py:265
  30.5 1.7 %broadcast_in_dim.2 = bf16[4,192,256]{2,1,0:T(8,128)(2,1)} broadcast(bf16[192,256]{1,0:T(8,128)(2,1)} %param.7), dimensions={1,2} | broadcast | bytes 491520 | tf_op jit(solution)/shard_map/broadcast_in_dim | solution.py:262
  32.2 11.0 %all-to-all-start = ((bf16[4,192,256]{2,1,0:T(8,128)(2,1)}), bf16[4,192,256]{2,1,0:T(8,128)(2,1)S(1)}, u32[]{:S(2)}, u32[]{:S(2)}) async-start(bf16[4,192,256]{2,1,0:T(8,128)(2,1)} %broadcast_in_dim.2), calls=%async_computation | async-start | bytes 786432 | tf_op jit(solution)/shard_map/all_to_all | solution.py:263
  43.1 2.3 %constant_dynamic-slice_fusion = bf16[128,4096]{1,0:T(8,128)(2,1)} fusion(bf16[256,4096]{1,0:T(8,128)(2,1)} %w0.1, s32[]{:T(128)S(6)} %select_n.18), kind=kLoop, calls=%fused_computation.8 | loop fusion | bytes 2097156 | tf_op jit(solution)/shard_map/dynamic_slice | solution.py:267
  45.5 2.0 %collective-permute-start.2 = (bf16[128,4096]{1,0:T(8,128)(2,1)}, bf16[128,4096]{1,0:T(8,128)(2,1)S(1)}, u32[]{:S(2)}, u32[]{:S(2)}) collective-permute-start(bf16[128,4096]{1,0:T(8,128)(2,1)} %constant_dynamic-slice_fusion), channel_id=1, source_target_pairs={{0,2},{1,0},{2,1},{3,5},{4,3},{5,4},{6,8},{7,6},{8,7},{9,11},{10,9... | collective-permute-start | bytes 3145736 | tf_op jit(solution)/shard_map/ppermute | solution.py:269
  48.2 1.9 %all-to-all-done.q_ref = bf16[4,192,256]{2,1,0:T(8,128)(2,1)S(1)} async-done(((bf16[4,192,256]{2,1,0:T(8,128)(2,1)}), bf16[4,192,256]{2,1,0:T(8,128)(2,1)S(1)}, u32[]{:S(2)}, u32[]{:S(2)}) %all-to-all-start) | async-done | bytes 393248 | tf_op jit(solution)/shard_map/all_to_all | solution.py:263
  50.1 2.5 %shard_map.75 = bf16[4,144,384]{2,1,0:T(8,128)(2,1)} custom-call(s32[3]{0:T(128)} %pad_add_fusion.1.place, s32[24]{0:T(128)} %lengths.1, bf16[4,192,256]{2,1,0:T(8,128)(2,1)S(1)} %all-to-all-done.q_ref, bf16[1536,256]{1,0:T(8,128)(2,1)S(1)} %all_gather.3.own_ref, bf16[1536,256]{1,0:T(8,128)(2,1)S(1)} %collective-permute-done.peer_ref), custom_call_target="tpu_custom_call" | custom-call | tf_op jit(solution)/shard_map/pallas_call | solution.py:271
  52.6 2.0 %collective-permute-start.1 = (bf16[128,4096]{1,0:T(8,128)(2,1)}, bf16[128,4096]{1,0:T(8,128)(2,1)S(1)}, u32[]{:S(2)}, u32[]{:S(2)}) collective-permute-start(bf16[128,4096]{1,0:T(8,128)(2,1)} %constant_dynamic-slice_fusion), channel_id=1, source_target_pairs={{0,1},{1,2},{2,0},{3,4},{4,5},{5,3},{6,7},{7,8},{8,6},{9,10},{10,1... | collective-permute-start | bytes 3145736 | tf_op jit(solution)/shard_map/ppermute | solution.py:283
  54.6 11.2 %all-to-all-start.1 = ((bf16[4,144,384]{2,1,0:T(8,128)(2,1)}), bf16[4,144,384]{2,1,0:T(8,128)(2,1)S(1)}, u32[]{:S(2)}, u32[]{:S(2)}) async-start(bf16[4,144,384]{2,1,0:T(8,128)(2,1)} %shard_map.75), calls=%async_computation.1 | async-start | bytes 884736 | tf_op jit(solution)/shard_map/all_to_all | solution.py:284
  66.7 1.1 shard_map.74.placement
  67.8 5.5 %all-to-all-done.1.part_ref = bf16[4,144,384]{2,1,0:T(8,128)(2,1)S(1)} async-done(((bf16[4,144,384]{2,1,0:T(8,128)(2,1)}), bf16[4,144,384]{2,1,0:T(8,128)(2,1)S(1)}, u32[]{:S(2)}, u32[]{:S(2)}) %all-to-all-start.1) | async-done | bytes 442400 | tf_op jit(solution)/shard_map/all_to_all | solution.py:284
  73.3 1.1 shard_map.76
  74.4 7.4 %all-to-all-start.2 = ((bf16[64,6,256]{2,1,0:T(8,128)(2,1)}), bf16[64,6,256]{2,1,0:T(8,128)(2,1)S(1)}, u32[]{:S(2)}, u32[]{:S(2)}) async-start(bf16[64,6,256]{2,1,0:T(8,128)(2,1)} %shard_map.76), calls=%async_computation.2 | async-start | bytes 524288 | tf_op jit(solution)/shard_map/all_to_all | solution.py:293
  82.6 1.2 shard_map.73.chooser
  83.8 11.6 %collective-permute-done.2.a2 = bf16[128,4096]{1,0:T(8,128)(2,1)S(1)} collective-permute-done((bf16[128,4096]{1,0:T(8,128)(2,1)}, bf16[128,4096]{1,0:T(8,128)(2,1)S(1)}, u32[]{:S(2)}, u32[]{:S(2)}) %collective-permute-start.2) | collective-permute-done | bytes 1048608 | tf_op jit(solution)/shard_map/ppermute | solution.py:269
  95.4 1.9 %collective-permute-start.4 = (bf16[128,4096]{1,0:T(8,128)(2,1)S(1)}, bf16[128,4096]{1,0:T(8,128)(2,1)}, u32[]{:S(2)}, u32[]{:S(2)}) collective-permute-start(bf16[128,4096]{1,0:T(8,128)(2,1)S(1)} %collective-permute-done.2.a2), channel_id=1, source_target_pairs={{0,12},{12,0},{1,13},{13,1},{2,14},{14,2},{3,15},{15,3},{4,16},{16... | collective-permute-start | bytes 3145736 | tf_op jit(solution)/shard_map/ppermute | solution.py:301
  98.3 2.4 %collective-permute-start.3 = (bf16[128,4096]{1,0:T(8,128)(2,1)S(1)}, bf16[128,4096]{1,0:T(8,128)(2,1)}, u32[]{:S(2)}, u32[]{:S(2)}) collective-permute-start(bf16[128,4096]{1,0:T(8,128)(2,1)S(1)} %collective-permute-done.1.a1), channel_id=1, source_target_pairs={{0,12},{12,0},{1,13},{13,1},{2,14},{14,2},{3,15},{15,3},{4,16},{16... | collective-permute-start | bytes 3145736 | tf_op jit(solution)/shard_map/ppermute | solution.py:303
  100.7 3.3 %all-to-all-start.3 = ((bf16[3,64,256]{2,1,0:T(8,128)(2,1)}), bf16[3,64,256]{2,1,0:T(8,128)(2,1)S(1)}, u32[]{:S(2)}, u32[]{:S(2)}) async-start(bf16[3,64,256]{2,1,0:T(8,128)(2,1)} %bitcast.8), calls=%async_computation.3 | async-start | bytes 196608 | tf_op jit(solution)/shard_map/all_to_all | solution.py:304
  104.7 4.3 %all-to-all-done.3.x_ref = bf16[3,64,256]{2,1,0:T(8,128)(2,1)S(1)} async-done(((bf16[3,64,256]{2,1,0:T(8,128)(2,1)}), bf16[3,64,256]{2,1,0:T(8,128)(2,1)S(1)}, u32[]{:S(2)}, u32[]{:S(2)}) %all-to-all-start.3) | async-done | bytes 98336 | tf_op jit(solution)/shard_map/all_to_all | solution.py:304
  109.1 5.0 %project.1 = (f32[16,4096]{1,0:T(8,128)}, f32[16,4096]{1,0:T(8,128)}, f32[16,4096]{1,0:T(8,128)}, bf16[8,4096]{1,0:T(8,128)(2,1)}, bf16[8,4096]{1,0:T(8,128)(2,1)}) custom-call(s32[3]{0:T(128)} %pad_add_fusion.place, bf16[3,64,256]{2,1,0:T(8,128)(2,1)S(1)} %all-to-all-done.3.x_ref, bf16[256,4096]{1,0:T(8,128)(2,1)} %w0.1, bf16[128,4096]{1,0:T(8,128)(2,1)} %copy-done.1, ...), custom_call_target="tpu_custom_call" | custom-call | tf_op jit(solution)/shard_map/project/pallas_call | solution.py:309
  114.0 7.4 %collective-permute-start.7 = (bf16[8,4096]{1,0:T(8,128)(2,1)}, bf16[8,4096]{1,0:T(8,128)(2,1)S(1)}, u32[]{:S(2)}, u32[]{:S(2)}) collective-permute-start(bf16[8,4096]{1,0:T(8,128)(2,1)} %get-tuple-element.22), channel_id=1, source_target_pairs={{0,9},{3,0},{6,3},{9,6},{1,10},{4,1},{7,4},{10,7},{2,11},{5,2},{8,... | collective-permute-start | bytes 196616 | tf_op jit(solution)/shard_map/ppermute | solution.py:324
  121.5 0.9 slice.25
  122.4 0.9 slice.24
  123.3 1.9 %collective-permute-start.5 = (bf16[8,4096]{1,0:T(8,128)(2,1)}, bf16[8,4096]{1,0:T(8,128)(2,1)S(1)}, u32[]{:S(2)}, u32[]{:S(2)}) collective-permute-start(bf16[8,4096]{1,0:T(8,128)(2,1)} %get-tuple-element.20), channel_id=1, source_target_pairs={{0,3},{3,6},{6,9},{9,0},{1,4},{4,7},{7,10},{10,1},{2,5},{5,8},{8,1... | collective-permute-start | bytes 196616 | tf_op jit(solution)/shard_map/ppermute | solution.py:323
  125.5 0.9 add_convert_fusion.1
  126.5 7.3 %collective-permute-start.8 = (bf16[16,4096]{1,0:T(8,128)(2,1)S(1)}, bf16[16,4096]{1,0:T(8,128)(2,1)S(1)}, u32[]{:S(2)}, u32[]{:S(2)}) collective-permute-start(bf16[16,4096]{1,0:T(8,128)(2,1)S(1)} %pad_maximum_fusion.1), channel_id=1, source_target_pairs={{0,9},{3,0},{6,3},{9,6},{1,10},{4,1},{7,4},{10,7},{2,11},{5,2},{8,... | collective-permute-start | bytes 393224 | tf_op jit(solution)/shard_map/ppermute | solution.py:329
  133.8 0.9 add_convert_fusion.2
  134.7 1.9 %collective-permute-start.6 = (bf16[16,4096]{1,0:T(8,128)(2,1)S(1)}, bf16[16,4096]{1,0:T(8,128)(2,1)S(1)}, u32[]{:S(2)}, u32[]{:S(2)}) collective-permute-start(bf16[16,4096]{1,0:T(8,128)(2,1)S(1)} %pad_maximum_fusion), channel_id=1, source_target_pairs={{0,3},{3,6},{6,9},{9,0},{1,4},{4,7},{7,10},{10,1},{2,5},{5,8},{8,1... | collective-permute-start | bytes 393224 | tf_op jit(solution)/shard_map/ppermute | solution.py:328
  136.6 4.3 %collective-permute-done.8 = bf16[16,4096]{1,0:T(8,128)(2,1)S(1)} collective-permute-done((bf16[16,4096]{1,0:T(8,128)(2,1)S(1)}, bf16[16,4096]{1,0:T(8,128)(2,1)S(1)}, u32[]{:S(2)}, u32[]{:S(2)}) %collective-permute-start.8) | collective-permute-done | bytes 131104 | tf_op jit(solution)/shard_map/ppermute | solution.py:329
  140.9 5.1 %collective-permute-done.6 = bf16[16,4096]{1,0:T(8,128)(2,1)S(1)} collective-permute-done((bf16[16,4096]{1,0:T(8,128)(2,1)S(1)}, bf16[16,4096]{1,0:T(8,128)(2,1)S(1)}, u32[]{:S(2)}, u32[]{:S(2)}) %collective-permute-start.6) | collective-permute-done | bytes 131104 | tf_op jit(solution)/shard_map/ppermute | solution.py:328
  146.0 1.7 %add_convert_fusion = bf16[16,4096]{1,0:T(8,128)(2,1)} fusion(bf16[16,4096]{1,0:T(8,128)(2,1)S(1)} %copy-done.2, bf16[16,4096]{1,0:T(8,128)(2,1)S(1)} %collective-permute-done.8, f32[16,4096]{1,0:T(8,128)} %get-tuple-element.18, bf16[16,4096]{1,0:T(8,128)(2,1)S(1)} %collective-permute-done.6), kind=kLoop, calls=%fused_computation | loop fusion | flops 458752 | bytes 786432 | tf_op jit(solution)/shard_map/convert_element_type | solution.py:331
  (28 shorter events, 5.0 us)
Async XLA Ops:
  28.6 21.5 %collective-permute-start = (bf16[1536,256]{1,0:T(8,128)(2,1)S(1)}, bf16[1536,256]{1,0:T(8,128)(2,1)S(1)}, u32[]{:S(2)}, u32[]{:S(2)}) collective-permute-start(bf16[1536,256]{1,0:T(8,128)(2,1)S(1)} %all_gather.3.own_ref), channel_id=1, source_target_pairs={{0,12},{12,0},{1,13},{13,1},{2,14},{14,2},{3,15},{15,3},{4,16},{16... | collective-permute-start | bytes 2359304 | tf_op jit(solution)/shard_map/ppermute | solution.py:265
  32.2 17.9 %all-to-all-start = ((bf16[4,192,256]{2,1,0:T(8,128)(2,1)}), bf16[4,192,256]{2,1,0:T(8,128)(2,1)S(1)}, u32[]{:S(2)}, u32[]{:S(2)}) async-start(bf16[4,192,256]{2,1,0:T(8,128)(2,1)} %broadcast_in_dim.2), calls=%async_computation | async-start | bytes 786432 | tf_op jit(solution)/shard_map/all_to_all | solution.py:263
  45.5 20.4 %copy-start.3 = (s32[12288]{0:T(1024)S(1)}, s32[12288]{0:T(1024)}, u32[]{:S(2)}) copy-start(s32[12288]{0:T(1024)} %param.11) | copy-start | bytes 147460
  45.5 50.0 %collective-permute-start.2 = (bf16[128,4096]{1,0:T(8,128)(2,1)}, bf16[128,4096]{1,0:T(8,128)(2,1)S(1)}, u32[]{:S(2)}, u32[]{:S(2)}) collective-permute-start(bf16[128,4096]{1,0:T(8,128)(2,1)} %constant_dynamic-slice_fusion), channel_id=1, source_target_pairs={{0,2},{1,0},{2,1},{3,5},{4,3},{5,4},{6,8},{7,6},{8,7},{9,11},{10,9... | collective-permute-start | bytes 3145736 | tf_op jit(solution)/shard_map/ppermute | solution.py:269
  52.6 45.7 %collective-permute-start.1 = (bf16[128,4096]{1,0:T(8,128)(2,1)}, bf16[128,4096]{1,0:T(8,128)(2,1)S(1)}, u32[]{:S(2)}, u32[]{:S(2)}) collective-permute-start(bf16[128,4096]{1,0:T(8,128)(2,1)} %constant_dynamic-slice_fusion), channel_id=1, source_target_pairs={{0,1},{1,2},{2,0},{3,4},{4,5},{5,3},{6,7},{7,8},{8,6},{9,10},{10,1... | collective-permute-start | bytes 3145736 | tf_op jit(solution)/shard_map/ppermute | solution.py:283
  54.6 18.7 %all-to-all-start.1 = ((bf16[4,144,384]{2,1,0:T(8,128)(2,1)}), bf16[4,144,384]{2,1,0:T(8,128)(2,1)S(1)}, u32[]{:S(2)}, u32[]{:S(2)}) async-start(bf16[4,144,384]{2,1,0:T(8,128)(2,1)} %shard_map.75), calls=%async_computation.1 | async-start | bytes 884736 | tf_op jit(solution)/shard_map/all_to_all | solution.py:284
  65.9 0.8 copy-start.4
  74.4 22.9 %all-to-all-start.2 = ((bf16[64,6,256]{2,1,0:T(8,128)(2,1)}), bf16[64,6,256]{2,1,0:T(8,128)(2,1)S(1)}, u32[]{:S(2)}, u32[]{:S(2)}) async-start(bf16[64,6,256]{2,1,0:T(8,128)(2,1)} %shard_map.76), calls=%async_computation.2 | async-start | bytes 524288 | tf_op jit(solution)/shard_map/all_to_all | solution.py:293
  95.4 13.6 %copy-start = (bf16[128,4096]{1,0:T(8,128)(2,1)}, bf16[128,4096]{1,0:T(8,128)(2,1)S(1)}, u32[]{:S(2)}) copy-start(bf16[128,4096]{1,0:T(8,128)(2,1)S(1)} %collective-permute-done.2.a2) | copy-start | bytes 3145732
  95.4 13.6 %collective-permute-start.4 = (bf16[128,4096]{1,0:T(8,128)(2,1)S(1)}, bf16[128,4096]{1,0:T(8,128)(2,1)}, u32[]{:S(2)}, u32[]{:S(2)}) collective-permute-start(bf16[128,4096]{1,0:T(8,128)(2,1)S(1)} %collective-permute-done.2.a2), channel_id=1, source_target_pairs={{0,12},{12,0},{1,13},{13,1},{2,14},{14,2},{3,15},{15,3},{4,16},{16... | collective-permute-start | bytes 3145736 | tf_op jit(solution)/shard_map/ppermute | solution.py:301
  98.3 10.8 %copy-start.1 = (bf16[128,4096]{1,0:T(8,128)(2,1)}, bf16[128,4096]{1,0:T(8,128)(2,1)S(1)}, u32[]{:S(2)}) copy-start(bf16[128,4096]{1,0:T(8,128)(2,1)S(1)} %collective-permute-done.1.a1) | copy-start | bytes 3145732
  98.3 10.8 %collective-permute-start.3 = (bf16[128,4096]{1,0:T(8,128)(2,1)S(1)}, bf16[128,4096]{1,0:T(8,128)(2,1)}, u32[]{:S(2)}, u32[]{:S(2)}) collective-permute-start(bf16[128,4096]{1,0:T(8,128)(2,1)S(1)} %collective-permute-done.1.a1), channel_id=1, source_target_pairs={{0,12},{12,0},{1,13},{13,1},{2,14},{14,2},{3,15},{15,3},{4,16},{16... | collective-permute-start | bytes 3145736 | tf_op jit(solution)/shard_map/ppermute | solution.py:303
  100.7 8.3 %all-to-all-start.3 = ((bf16[3,64,256]{2,1,0:T(8,128)(2,1)}), bf16[3,64,256]{2,1,0:T(8,128)(2,1)S(1)}, u32[]{:S(2)}, u32[]{:S(2)}) async-start(bf16[3,64,256]{2,1,0:T(8,128)(2,1)} %bitcast.8), calls=%async_computation.3 | async-start | bytes 196608 | tf_op jit(solution)/shard_map/all_to_all | solution.py:304
  104.7 41.3 %copy-start.2 = (bf16[16,4096]{1,0:T(8,128)(2,1)S(1)}, bf16[16,4096]{1,0:T(8,128)(2,1)}, u32[]{:S(2)}) copy-start(bf16[16,4096]{1,0:T(8,128)(2,1)} %param.13) | copy-start | bytes 393220
  114.0 11.5 %collective-permute-start.7 = (bf16[8,4096]{1,0:T(8,128)(2,1)}, bf16[8,4096]{1,0:T(8,128)(2,1)S(1)}, u32[]{:S(2)}, u32[]{:S(2)}) collective-permute-start(bf16[8,4096]{1,0:T(8,128)(2,1)} %get-tuple-element.22), channel_id=1, source_target_pairs={{0,9},{3,0},{6,3},{9,6},{1,10},{4,1},{7,4},{10,7},{2,11},{5,2},{8,... | collective-permute-start | bytes 196616 | tf_op jit(solution)/shard_map/ppermute | solution.py:324
  123.3 10.5 %collective-permute-start.5 = (bf16[8,4096]{1,0:T(8,128)(2,1)}, bf16[8,4096]{1,0:T(8,128)(2,1)S(1)}, u32[]{:S(2)}, u32[]{:S(2)}) collective-permute-start(bf16[8,4096]{1,0:T(8,128)(2,1)} %get-tuple-element.20), channel_id=1, source_target_pairs={{0,3},{3,6},{6,9},{9,0},{1,4},{4,7},{7,10},{10,1},{2,5},{5,8},{8,1... | collective-permute-start | bytes 196616 | tf_op jit(solution)/shard_map/ppermute | solution.py:323
  126.5 14.4 %collective-permute-start.8 = (bf16[16,4096]{1,0:T(8,128)(2,1)S(1)}, bf16[16,4096]{1,0:T(8,128)(2,1)S(1)}, u32[]{:S(2)}, u32[]{:S(2)}) collective-permute-start(bf16[16,4096]{1,0:T(8,128)(2,1)S(1)} %pad_maximum_fusion.1), channel_id=1, source_target_pairs={{0,9},{3,0},{6,3},{9,6},{1,10},{4,1},{7,4},{10,7},{2,11},{5,2},{8,... | collective-permute-start | bytes 393224 | tf_op jit(solution)/shard_map/ppermute | solution.py:329
  134.7 11.3 %collective-permute-start.6 = (bf16[16,4096]{1,0:T(8,128)(2,1)S(1)}, bf16[16,4096]{1,0:T(8,128)(2,1)S(1)}, u32[]{:S(2)}, u32[]{:S(2)}) collective-permute-start(bf16[16,4096]{1,0:T(8,128)(2,1)S(1)} %pad_maximum_fusion), channel_id=1, source_target_pairs={{0,3},{3,6},{6,9},{9,0},{1,4},{4,7},{7,10},{10,1},{2,5},{5,8},{8,1... | collective-permute-start | bytes 393224 | tf_op jit(solution)/shard_map/ppermute | solution.py:328

commit v2 on v1

--- a/solution.py
+++ b/solution.py
@@ -35,8 +35,8 @@
     return (v + jnp.abs(v) * 0.0079).astype(jnp.bfloat16).astype(jnp.float32)
 
 
-def attend_kernel(place, lengths, q_ref, own_ref, peer_ref, out_ref, q_s, m_s, l_s, acc_s):
-    x, y, c = place[0], place[1], place[2]
+def attend_kernel(lengths, q_ref, own_ref, peer_ref, out_ref, q_s, m_s, l_s, acc_s):
+    x, y, c = (lax.axis_index(a) for a in ("x", "y", "c"))
 
     def empty(xs, carry):
         out_ref[xs, :HEAD, :] = jnp.zeros((HEAD, QROWS), jnp.bfloat16)
@@ -159,8 +159,9 @@
         out_ref[:, :, h * HEAD : (h + 1) * HEAD] = rows.astype(jnp.bfloat16)
 
 
-def choose_kernel(me, owner_ref, out_ref):
-    mine = (owner_ref[...] == me[0]).astype(jnp.float32).astype(jnp.bfloat16)
+def choose_kernel(owner_ref, out_ref):
+    x, y, c = (lax.axis_index(a) for a in ("x", "y", "c"))
+    mine = (owner_ref[...] == (x * NY + y) * NC + c).astype(jnp.float32).astype(jnp.bfloat16)
     count = lax.dot_general(
         jnp.ones((8, TOK), jnp.bfloat16), mine, NT, preferred_element_type=jnp.float32
     ).astype(jnp.bfloat16)
@@ -191,10 +192,11 @@
     )
 
 
-def project_kernel(place, x_ref, w0, a1, a2, b1, b2, own_ref, next_ref, prev_ref, c1_ref, c2_ref):
-    c, j, q = place[0], place[1], place[2]
+def project_kernel(x_ref, w0, w1, w2, own_ref, *piece_refs):
+    c, j, q = (lax.axis_index(a) for a in ("c", "j", "q"))
 
     def rows_of(member):
+        member = lax.rem(member, NJ)
         turned = [
             x_ref[member, pl.ds(pl.multiple_of(lax.rem(q + s, NQ) * OUT, OUT), OUT), :]
             for s in range(NQ)
@@ -202,18 +204,27 @@
         return jnp.concatenate(turned, axis=0)
 
     total = jnp.dot(rows_of(j), w0[...], preferred_element_type=jnp.float32)
-    for step, near, far in ((1, a1, b1), (2, a2, b2)):
-        rows = rows_of(lax.rem(j + NJ - step, NJ))
-        left, right = rows[:, :HEAD], rows[:, HEAD:]
-        lo = jnp.where(c == 0, left, right)
-        hi = jnp.where(c == 0, right, left)
-        total += jnp.dot(lo, near[...], preferred_element_type=jnp.float32)
-        total += jnp.dot(hi, far[...], preferred_element_type=jnp.float32)
+    total += jnp.dot(rows_of(j + 2 - c), w1[...], preferred_element_type=jnp.float32)
+    total += jnp.dot(rows_of(j + 1 + c), w2[...], preferred_element_type=jnp.float32)
     own_ref[...] = total[:OUT]
-    next_ref[...] = total[OUT : 2 * OUT]
-    c1_ref[...] = total[2 * OUT : 2 * OUT + OUT // 2].astype(jnp.bfloat16)
-    c2_ref[...] = total[2 * OUT + OUT // 2 : 3 * OUT].astype(jnp.bfloat16)
-    prev_ref[...] = total[3 * OUT :]
+    half = OUT // 2
+    for n, ref in enumerate(piece_refs):
+        ref[...] = total[OUT + n * half : OUT + (n + 1) * half].astype(ref.dtype)
+
+
+def fold_kernel(near_ref, near_add, near_rest, far_rest, far_ref, far_add, ahead_ref, behind_ref):
+    half = OUT // 2
+    ahead_ref[:half] = (near_ref[...] + near_add[...].astype(jnp.float32)).astype(jnp.bfloat16)
+    ahead_ref[half:] = near_rest[...]
+    behind_ref[:half] = far_rest[...]
+    behind_ref[half:] = (far_ref[...] + far_add[...].astype(jnp.float32)).astype(jnp.bfloat16)
+
+
+def prepare_kernel(head, q_ref, k_ref, v_ref, copies_ref, kv_ref):
+    for i in range(NX):
+        copies_ref[i] = q_ref[...]
+    kv_ref[:, :HEAD] = k_ref[...]
+    kv_ref[:, HEAD:] = v_ref[...]
 
 
 def vmem():
@@ -224,10 +235,6 @@
     return pltpu.with_memory_space_constraint(array, pltpu.VMEM)
 
 
-def far_off(array):
-    return pltpu.with_memory_space_constraint(array, pltpu.HBM)
-
-
 def out_here(*shape):
     return pltpu.VMEM(shape, jnp.bfloat16)
 
@@ -237,50 +244,56 @@
 
 
 def kernel(body, shapes, in_specs, **more):
-    return pl.pallas_call(body, out_shape=shapes, in_specs=in_specs, out_specs=vmem(), **more)
+    outs = [vmem() for _ in shapes] if isinstance(shapes, list) else vmem()
+    return pl.pallas_call(body, out_shape=shapes, in_specs=in_specs, out_specs=outs, **more)
 
 
 def per_device(queries, keys, values, lengths, mlp_owner, out_weight, residual):
     x, y, c = lax.axis_index("x"), lax.axis_index("y"), lax.axis_index("c")
-    q, j = lax.axis_index("q"), lax.axis_index("j")
-    tp = q * NJ + j
+    tp = lax.axis_index("q") * NJ + lax.axis_index("j")
     dc = (x * NY + y) * NC + c
-    place = jnp.stack([x, y, c]).astype(jnp.int32)
     peer = [(0, 1), (1, 0)]
 
     def turn(size, step):
         return [(i, (i + step) % size) for i in range(size)]
 
-    kv_at = tp * HEADS_HERE // GROUP * HEAD
-    kv = jnp.concatenate(
-        [
-            lax.dynamic_slice_in_dim(keys, kv_at, HEAD, 1),
-            lax.dynamic_slice_in_dim(values, kv_at, HEAD, 1),
+    around = [
+        (k * NJ + i, k * NJ + (i + 1 + k) % NJ) for k in range(NC) for i in range(NJ)
+    ]
+    turned = lax.ppermute(out_weight, ("c", "j"), around)
+    block = pl.BlockSpec((TOK, HEAD), lambda i, head: (0, head[0]))
+    copies, kv = pl.pallas_call(
+        prepare_kernel,
+        out_shape=[
+            jax.ShapeDtypeStruct((NX, TOK, COLS), jnp.bfloat16),
+            out_here(TOK, COLS),
         ],
-        axis=1,
-    )
-    copies = jnp.broadcast_to(queries[None], (NX, TOK, COLS))
+        grid_spec=pltpu.PrefetchScalarGridSpec(
+            num_scalar_prefetch=1,
+            grid=(1,),
+            in_specs=[pl.BlockSpec((TOK, COLS), lambda i, head: (0, 0)), block, block],
+            out_specs=[
+                pl.BlockSpec((NX, TOK, COLS), lambda i, head: (0, 0, 0)),
+                pl.BlockSpec((TOK, COLS), lambda i, head: (0, 0)),
+            ],
+        ),
+        name="prepare",
+    )((tp * HEADS_HERE // GROUP).reshape(1).astype(jnp.int32), queries, keys, values)
     q_all = lax.all_to_all(copies, "x", 0, 0, tiled=True)
     own = lax.all_gather(kv, "y", axis=0, tiled=True)
     other = lax.ppermute(own, "c", peer)
 
-    half = lax.dynamic_slice_in_dim(out_weight, c * HEAD, HEAD, 0)
-    half, _ = lax.optimization_barrier((half, own))
-    near2 = lax.ppermute(half, "j", turn(NJ, 2))
-
     partial = kernel(
         attend_kernel,
         out_here(NX, PART, QROWS),
-        [smem(), smem(), vmem(), vmem(), vmem()],
+        [smem(), vmem(), vmem(), vmem()],
         scratch_shapes=[
             pltpu.VMEM((QROWS, HEAD), jnp.bfloat16),
             pltpu.VMEM((1, QROWS), jnp.float32),
             pltpu.VMEM((1, QROWS), jnp.float32),
             pltpu.VMEM((HEAD, QROWS), jnp.float32),
         ],
-    )(place, lengths, near_core(q_all), near_core(own), near_core(other))
-    half, _ = lax.optimization_barrier((half, partial))
-    near1 = lax.ppermute(half, "j", turn(NJ, 1))
+    )(lengths, near_core(q_all), near_core(own), near_core(other))
     parts = lax.all_to_all(partial, "x", 0, 0, tiled=True)
 
     targets = lax.dynamic_slice_in_dim(mlp_owner, dc * TOK, TOK, 0)
@@ -291,40 +304,36 @@
         merge_kernel, out_here(N_DC, SLOTS, COLS), [vmem(), vmem()]
     )(near_core(placement), near_core(parts))
     incoming = lax.all_to_all(outgoing, ("x", "y", "c"), 0, 0, tiled=True)
-    chooser = kernel(choose_kernel, out_here(TOK, SLOT_TOTAL), [smem(), vmem()])(
-        dc.reshape(1).astype(jnp.int32), mlp_owner.reshape(N_DC, TOK)
+    chooser = kernel(choose_kernel, out_here(TOK, SLOT_TOTAL), [vmem()])(
+        mlp_owner.reshape(N_DC, TOK)
     )
     owned = kernel(collect_kernel, out_here(TOK, COLS), [vmem(), vmem()])(
         near_core(chooser), near_core(incoming.reshape(SLOT_TOTAL, COLS))
     )
-    near2, _ = lax.optimization_barrier((near2, outgoing))
-    far2 = lax.ppermute(near2, "c", peer)
-    near1, _ = lax.optimization_barrier((near1, owned))
-    far1 = lax.ppermute(near1, "c", peer)
+    turned, _ = lax.optimization_barrier((turned, partial))
+    swapped = lax.ppermute(turned, "c", peer)
+    owned, swapped = lax.optimization_barrier((owned, swapped))
     shared = lax.all_to_all(owned.reshape(NJ, TOK // NJ, COLS), "j", 0, 0, tiled=True)
 
     width = out_weight.shape[1]
     tile = 1024
-    blocks = [(OUT, jnp.float32)] * 3 + [(OUT // 2, jnp.bfloat16)] * 2
-    mine, ahead, behind, c1, c2 = pl.pallas_call(
+    half = OUT // 2
+    f32, bf16 = jnp.float32, jnp.bfloat16
+    blocks = [(OUT, f32), (half, f32), (half, bf16), (half, bf16), (half, bf16)]
+    blocks += [(half, bf16), (half, f32)]
+    mine, near, near_rest, c1, c2, far_rest, far = pl.pallas_call(
         project_kernel,
         out_shape=[jax.ShapeDtypeStruct((n, width), t) for n, t in blocks],
         grid=(width // tile,),
-        in_specs=[smem(), vmem(), pl.BlockSpec((COLS, tile), lambda n: (0, n))]
-        + [pl.BlockSpec((HEAD, tile), lambda n: (0, n))] * 4,
+        in_specs=[vmem()] + [pl.BlockSpec((COLS, tile), lambda n: (0, n))] * 3,
         out_specs=[pl.BlockSpec((n, tile), lambda n: (0, n)) for n, _ in blocks],
         name="project",
-    )(
-        jnp.stack([c, j, q]).astype(jnp.int32),
-        near_core(shared),
-        out_weight,
-        *map(far_off, (near1, near2, far1, far2)),
-    )
+    )(near_core(shared), out_weight, turned, swapped)
     c1 = lax.ppermute(c1, "q", turn(NQ, 1))
     c2 = lax.ppermute(c2, "q", turn(NQ, 3))
-    h = OUT // 2
-    ahead = jnp.concatenate([ahead[:h] + c1.astype(jnp.float32), ahead[h:]]).astype(jnp.bfloat16)
-    behind = jnp.concatenate([behind[:h], behind[h:] + c2.astype(jnp.float32)]).astype(jnp.bfloat16)
+    ahead, behind = kernel(fold_kernel, [out_here(OUT, width)] * 2, [vmem()] * 6)(
+        near, near_core(c1), near_rest, far_rest, far, near_core(c2)
+    )
     ahead = lax.ppermute(ahead, "q", turn(NQ, 1))
     behind = lax.ppermute(behind, "q", turn(NQ, 3))
     total = mine + ahead.astype(jnp.float32) + behind.astype(jnp.float32)

time: 149 us -> 149 us (level)
  blocking collectives: 27.7 us -> 52.3 us
  starting transfers between devices: 61.7 us -> 48.7 us
  local copies, waits for them, and re-layouts: 8.29 us -> 1.64 us
  waiting for transfers between devices: 33.1 us -> 29.9 us
  other arithmetic: 4.86 us -> 1.67 us
  Pallas kernels: 11.8 us -> 13.9 us
    all_to_all x0 -> x2, blocking collectives: none -> 24.5 us  [the longest x1 15.8 us: per_device(): q_all = lax.all_to_all(copies, 'x', 0, 0, tiled=True)]
    all_to_all x2 -> x0, starting transfers between devices: 14.3 us -> none  [the longest x1 11 us: per_device(): q_all = lax.all_to_all(copies, 'x', 0, 0, tiled=True)]
    ppermute x4 -> x2, waiting for transfers between devices: 11.6 us -> 0.01 us  [the longest x1 0.01 us: per_device(): turned = lax.ppermute(out_weight, ('c', 'j'), around)]
    all_to_all x1, waiting for transfers between devices: 0.01 us -> 9.58 us  [per_device(): incoming = lax.all_to_all(outgoing, ('x', 'y', 'c'), 0, 0, tiled=True)]
    all_to_all x2 -> x0, waiting for transfers between devices: 6.25 us -> none  [the longest x1 4.34 us: per_device(): lax.all_to_all(owned.reshape(NJ, TOK // NJ, COLS), 'j', 0, 0, tiled=True)]
    ppermute x1, starting transfers between devices: 1.91 us -> 7.97 us  [per_device(): c1 = lax.ppermute(c1, 'q', turn(NQ, 1))]
    ppermute x1, waiting for transfers between devices: 0.34 us -> 5.42 us  [per_device(): c2 = lax.ppermute(c2, 'q', turn(NQ, 3))]
    ppermute x1, starting transfers between devices: 7.26 us -> 2.62 us  [per_device(): behind = lax.ppermute(behind, 'q', turn(NQ, 3))]
  transfers between devices with their start and end apart: 13 -> 9, of which waited for: 7 -> 6; matrix products, arithmetic and copies ran while one was open for 7% -> 1% of each run, Pallas kernels for 5% -> 5%
where the time goes in v2:
time: 149 us; the launch traced here: 148 us
  blocking collectives  52.3 us (35%)
  starting transfers between devices  48.7 us (33%)
  waiting for transfers between devices  29.9 us (20%)
  Pallas kernels  13.9 us (9%)
  other arithmetic  1.67 us (1%)
  local copies, waits for them, and re-layouts  1.64 us (1%)
    all_gather x1, blocking collectives, per_device(): own = lax.all_gather(kv, 'y', axis=0, tiled=True)  27.8 us
    all_to_all x1, blocking collectives, per_device(): q_all = lax.all_to_all(copies, 'x', 0, 0, tiled=True)  15.8 us
    all_to_all x1, starting transfers between devices, per_device(): parts = lax.all_to_all(partial, 'x', 0, 0, tiled=True)  11.3 us
    all_to_all x1, waiting for transfers between devices, per_device(): incoming = lax.all_to_all(outgoing, ('x', 'y', 'c'), 0, 0, tiled=True)  9.58 us
    all_to_all x1, blocking collectives, per_device(): lax.all_to_all(owned.reshape(NJ, TOK // NJ, COLS), 'j', 0, 0, tiled=True)  8.73 us
    ppermute x1, starting transfers between devices, per_device(): c1 = lax.ppermute(c1, 'q', turn(NQ, 1))  7.97 us
    all_to_all x1, starting transfers between devices, per_device(): incoming = lax.all_to_all(outgoing, ('x', 'y', 'c'), 0, 0, tiled=True)  7.44 us
    ppermute x1, starting transfers between devices, per_device(): ahead = lax.ppermute(ahead, 'q', turn(NQ, 1))  6.23 us
  transfers between devices with their start and end apart: 9, of which 6 were waited for; matrix products, arithmetic and copies ran while one was open for 1% of the time, Pallas kernels for 5%

profile of v2, /device:TPU:6, one launch (start us, length us, event | category | flops | bytes accessed | tf_op | source)
XLA Modules:
  0.0 148.3 jit_solution(7455874523763424741)
XLA Ops:
  0.0 4.3 %collective-permute-start.1 = (bf16[256,4096]{1,0:T(8,128)(2,1)}, bf16[256,4096]{1,0:T(8,128)(2,1)}, u32[]{:S(2)}, u32[]{:S(2)}) collective-permute-start(bf16[256,4096]{1,0:T(8,128)(2,1)} %w0.1), channel_id=1, source_target_pairs={{0,1},{1,2},{2,0},{12,14},{13,12},{14,13},{3,4},{4,5},{5,3},{15,17... | collective-permute-start | bytes 6291464 | tf_op jit(solution)/shard_map/ppermute | solution.py:263
  4.3 1.7 %prepare.1 = (bf16[4,192,256]{2,1,0:T(8,128)(2,1)}, bf16[192,256]{1,0:T(8,128)(2,1)S(1)}) custom-call(s32[1]{0:T(128)} %bitcast.2.head, bf16[192,256]{1,0:T(8,128)(2,1)} %q_ref.1, bf16[192,768]{1,0:T(8,128)(2,1)} %k_ref.1, bf16[192,768]{1,0:T(8,128)(2,1)} %v_ref.1), custom_call_target="tpu_custom_call" | custom-call | tf_op jit(solution)/shard_map/prepare/pallas_call | solution.py:265
  6.0 27.8 %all_gather.3.own_ref = bf16[1536,256]{1,0:T(8,128)(2,1)S(1)} all-gather(bf16[192,256]{1,0:T(8,128)(2,1)S(1)} %get-tuple-element.20), channel_id=1, replica_groups=mesh['x'=4,'y'=8,'c'=2,'q'=4,'j'=3] {'y'}, dimensions={0}, use_global_device_ids=true | all-gather | bytes 884736 | tf_op jit(solution)/shard_map/all_gather | solution.py:283
  33.8 2.0 %collective-permute-start = (bf16[1536,256]{1,0:T(8,128)(2,1)S(1)}, bf16[1536,256]{1,0:T(8,128)(2,1)S(1)}, u32[]{:S(2)}, u32[]{:S(2)}) collective-permute-start(bf16[1536,256]{1,0:T(8,128)(2,1)S(1)} %all_gather.3.own_ref), channel_id=1, source_target_pairs={{0,12},{12,0},{1,13},{13,1},{2,14},{14,2},{3,15},{15,3},{4,16},{16... | collective-permute-start | bytes 2359304 | tf_op jit(solution)/shard_map/ppermute | solution.py:284
  35.9 15.8 %all_to_all.20.q_ref = bf16[4,192,256]{2,1,0:T(8,128)(2,1)S(1)} all-to-all(bf16[4,192,256]{2,1,0:T(8,128)(2,1)} %get-tuple-element.19), channel_id=1, replica_groups=mesh['x'=4,'y'=8,'c'=2,'q'=4,'j'=3] {'x'}, dimensions={0} | all-to-all | bytes 786432 | tf_op jit(solution)/shard_map/all_to_all | solution.py:282
  51.6 0.0 collective-permute-done.peer_ref
  51.6 2.5 %shard_map.75 = bf16[4,144,384]{2,1,0:T(8,128)(2,1)} custom-call(s32[24]{0:T(128)} %lengths.1, bf16[4,192,256]{2,1,0:T(8,128)(2,1)S(1)} %all_to_all.20.q_ref, bf16[1536,256]{1,0:T(8,128)(2,1)S(1)} %all_gather.3.own_ref, bf16[1536,256]{1,0:T(8,128)(2,1)S(1)} %collective-permute-done.peer_ref), custom_call_target="tpu_custom_call" | custom-call | tf_op jit(solution)/shard_map/pallas_call | solution.py:286
  54.2 2.1 %collective-permute-start.2 = (bf16[256,4096]{1,0:T(8,128)(2,1)}, bf16[256,4096]{1,0:T(8,128)(2,1)S(1)}, u32[]{:S(2)}, u32[]{:S(2)}) collective-permute-start(bf16[256,4096]{1,0:T(8,128)(2,1)} %collective-permute-done.1.w1), channel_id=1, source_target_pairs={{0,12},{12,0},{1,13},{13,1},{2,14},{14,2},{3,15},{15,3},{4,16},{16... | collective-permute-start | bytes 6291464 | tf_op jit(solution)/shard_map/ppermute | solution.py:314
  56.3 11.3 %all-to-all-start.1 = ((bf16[4,144,384]{2,1,0:T(8,128)(2,1)}), bf16[4,144,384]{2,1,0:T(8,128)(2,1)S(1)}, u32[]{:S(2)}, u32[]{:S(2)}) async-start(bf16[4,144,384]{2,1,0:T(8,128)(2,1)} %shard_map.75), calls=%async_computation.1 | async-start | bytes 884736 | tf_op jit(solution)/shard_map/all_to_all | solution.py:297
  67.6 0.1 dynamic_slice.3
  67.7 0.8 copy.8.col_ref
  68.4 1.1 shard_map.74.placement
  69.5 5.3 %all-to-all-done.1.part_ref = bf16[4,144,384]{2,1,0:T(8,128)(2,1)S(1)} async-done(((bf16[4,144,384]{2,1,0:T(8,128)(2,1)}), bf16[4,144,384]{2,1,0:T(8,128)(2,1)S(1)}, u32[]{:S(2)}, u32[]{:S(2)}) %all-to-all-start.1) | async-done | bytes 442400 | tf_op jit(solution)/shard_map/all_to_all | solution.py:297
  74.8 1.1 shard_map.76
  76.0 7.4 %all-to-all-start.2 = ((bf16[64,6,256]{2,1,0:T(8,128)(2,1)}), bf16[64,6,256]{2,1,0:T(8,128)(2,1)S(1)}, u32[]{:S(2)}, u32[]{:S(2)}) async-start(bf16[64,6,256]{2,1,0:T(8,128)(2,1)} %shard_map.76), calls=%async_computation.2 | async-start | bytes 524288 | tf_op jit(solution)/shard_map/all_to_all | solution.py:306
  83.4 0.7 reshape.18.owner_ref
  84.1 1.2 shard_map.73.chooser
  85.4 9.6 %all-to-all-done.2 = bf16[64,6,256]{2,1,0:T(8,128)(2,1)S(1)} async-done(((bf16[64,6,256]{2,1,0:T(8,128)(2,1)}), bf16[64,6,256]{2,1,0:T(8,128)(2,1)S(1)}, u32[]{:S(2)}, u32[]{:S(2)}) %all-to-all-start.2) | async-done | bytes 196640 | tf_op jit(solution)/shard_map/all_to_all | solution.py:306
  94.9 0.1 reshape.22.in_ref
  95.0 0.2 shard_map.77
  95.2 8.7 %all_to_all.21.x_ref = bf16[3,64,256]{2,1,0:T(8,128)(2,1)S(1)} all-to-all(bf16[3,64,256]{2,1,0:T(8,128)(2,1)S(1)} %bitcast.4), channel_id=1, replica_groups=mesh['x'=4,'y'=8,'c'=2,'q'=4,'j'=3] {'j'}, dimensions={0} | all-to-all | bytes 196608 | tf_op jit(solution)/shard_map/all_to_all | solution.py:316
  104.0 5.0 %project.1 = (f32[16,4096]{1,0:T(8,128)}, f32[8,4096]{1,0:T(8,128)}, bf16[8,4096]{1,0:T(8,128)(2,1)}, bf16[8,4096]{1,0:T(8,128)(2,1)}, bf16[8,4096]{1,0:T(8,128)...) custom-call(bf16[3,64,256]{2,1,0:T(8,128)(2,1)S(1)} %all_to_all.21.x_ref, bf16[256,4096]{1,0:T(8,128)(2,1)} %w0.1, ...), custom_call_target="tpu_custom_call" | custom-call | tf_op jit(solution)/shard_map/project/pallas_call | solution.py:324
  108.9 8.0 %collective-permute-start.3 = (bf16[8,4096]{1,0:T(8,128)(2,1)}, bf16[8,4096]{1,0:T(8,128)(2,1)S(1)}, u32[]{:S(2)}, u32[]{:S(2)}) collective-permute-start(bf16[8,4096]{1,0:T(8,128)(2,1)} %get-tuple-element.26), channel_id=1, source_target_pairs={{0,3},{3,6},{6,9},{9,0},{1,4},{4,7},{7,10},{10,1},{2,5},{5,8},{8,1... | collective-permute-start | bytes 196616 | tf_op jit(solution)/shard_map/ppermute | solution.py:332
  116.9 4.7 %collective-permute-start.4 = (bf16[8,4096]{1,0:T(8,128)(2,1)}, bf16[8,4096]{1,0:T(8,128)(2,1)S(1)}, u32[]{:S(2)}, u32[]{:S(2)}) collective-permute-start(bf16[8,4096]{1,0:T(8,128)(2,1)} %get-tuple-element.30), channel_id=1, source_target_pairs={{0,9},{3,0},{6,3},{9,6},{1,10},{4,1},{7,4},{10,7},{2,11},{5,2},{8,... | collective-permute-start | bytes 196616 | tf_op jit(solution)/shard_map/ppermute | solution.py:333
  121.6 1.3 collective-permute-done.3.near_add
  123.0 5.4 %collective-permute-done.4.far_add = bf16[8,4096]{1,0:T(8,128)(2,1)S(1)} collective-permute-done((bf16[8,4096]{1,0:T(8,128)(2,1)}, bf16[8,4096]{1,0:T(8,128)(2,1)S(1)}, u32[]{:S(2)}, u32[]{:S(2)}) %collective-permute-start.4) | collective-permute-done | bytes 65568 | tf_op jit(solution)/shard_map/ppermute | solution.py:333
  128.4 1.1 shard_map.78
  129.4 6.2 %collective-permute-start.5 = (bf16[16,4096]{1,0:T(8,128)(2,1)S(1)}, bf16[16,4096]{1,0:T(8,128)(2,1)S(1)}, u32[]{:S(2)}, u32[]{:S(2)}) collective-permute-start(bf16[16,4096]{1,0:T(8,128)(2,1)S(1)} %get-tuple-element.31), channel_id=1, source_target_pairs={{0,3},{3,6},{6,9},{9,0},{1,4},{4,7},{7,10},{10,1},{2,5},{5,8},{8,1... | collective-permute-start | bytes 393224 | tf_op jit(solution)/shard_map/ppermute | solution.py:337
  135.7 2.6 %collective-permute-start.6 = (bf16[16,4096]{1,0:T(8,128)(2,1)S(1)}, bf16[16,4096]{1,0:T(8,128)(2,1)S(1)}, u32[]{:S(2)}, u32[]{:S(2)}) collective-permute-start(bf16[16,4096]{1,0:T(8,128)(2,1)S(1)} %get-tuple-element.32), channel_id=1, source_target_pairs={{0,9},{3,0},{6,3},{9,6},{1,10},{4,1},{7,4},{10,7},{2,11},{5,2},{8,... | collective-permute-start | bytes 393224 | tf_op jit(solution)/shard_map/ppermute | solution.py:338
  138.3 2.7 %collective-permute-done.5 = bf16[16,4096]{1,0:T(8,128)(2,1)S(1)} collective-permute-done((bf16[16,4096]{1,0:T(8,128)(2,1)S(1)}, bf16[16,4096]{1,0:T(8,128)(2,1)S(1)}, u32[]{:S(2)}, u32[]{:S(2)}) %collective-permute-start.5) | collective-permute-done | bytes 131104 | tf_op jit(solution)/shard_map/ppermute | solution.py:337
  141.1 5.5 %collective-permute-done.6 = bf16[16,4096]{1,0:T(8,128)(2,1)S(1)} collective-permute-done((bf16[16,4096]{1,0:T(8,128)(2,1)S(1)}, bf16[16,4096]{1,0:T(8,128)(2,1)S(1)}, u32[]{:S(2)}, u32[]{:S(2)}) %collective-permute-start.6) | collective-permute-done | bytes 131104 | tf_op jit(solution)/shard_map/ppermute | solution.py:338
  146.6 1.7 %add_convert_fusion = bf16[16,4096]{1,0:T(8,128)(2,1)} fusion(bf16[16,4096]{1,0:T(8,128)(2,1)S(1)} %copy-done.1, bf16[16,4096]{1,0:T(8,128)(2,1)S(1)} %collective-permute-done.6, f32[16,4096]{1,0:T(8,128)} %get-tuple-element.24, bf16[16,4096]{1,0:T(8,128)(2,1)S(1)} %collective-permute-done.5), kind=kLoop, calls=%fused_computation | loop fusion | flops 458752 | bytes 786432 | tf_op jit(solution)/shard_map/convert_element_type | solution.py:340
  (10 shorter events, 0.0 us)
Async XLA Ops:
  0.0 54.2 %collective-permute-start.1 = (bf16[256,4096]{1,0:T(8,128)(2,1)}, bf16[256,4096]{1,0:T(8,128)(2,1)}, u32[]{:S(2)}, u32[]{:S(2)}) collective-permute-start(bf16[256,4096]{1,0:T(8,128)(2,1)} %w0.1), channel_id=1, source_target_pairs={{0,1},{1,2},{2,0},{12,14},{13,12},{14,13},{3,4},{4,5},{5,3},{15,17... | collective-permute-start | bytes 6291464 | tf_op jit(solution)/shard_map/ppermute | solution.py:263
  33.8 33.8 %copy-start.2 = (s32[12288]{0:T(1024)S(1)}, s32[12288]{0:T(1024)}, u32[]{:S(2)}) copy-start(s32[12288]{0:T(1024)} %param.11) | copy-start | bytes 147460
  33.8 17.8 %collective-permute-start = (bf16[1536,256]{1,0:T(8,128)(2,1)S(1)}, bf16[1536,256]{1,0:T(8,128)(2,1)S(1)}, u32[]{:S(2)}, u32[]{:S(2)}) collective-permute-start(bf16[1536,256]{1,0:T(8,128)(2,1)S(1)} %all_gather.3.own_ref), channel_id=1, source_target_pairs={{0,12},{12,0},{1,13},{13,1},{2,14},{14,2},{3,15},{15,3},{4,16},{16... | collective-permute-start | bytes 2359304 | tf_op jit(solution)/shard_map/ppermute | solution.py:284
  54.2 41.1 %collective-permute-start.2 = (bf16[256,4096]{1,0:T(8,128)(2,1)}, bf16[256,4096]{1,0:T(8,128)(2,1)S(1)}, u32[]{:S(2)}, u32[]{:S(2)}) collective-permute-start(bf16[256,4096]{1,0:T(8,128)(2,1)} %collective-permute-done.1.w1), channel_id=1, source_target_pairs={{0,12},{12,0},{1,13},{13,1},{2,14},{14,2},{3,15},{15,3},{4,16},{16... | collective-permute-start | bytes 6291464 | tf_op jit(solution)/shard_map/ppermute | solution.py:314
  56.3 18.5 %all-to-all-start.1 = ((bf16[4,144,384]{2,1,0:T(8,128)(2,1)}), bf16[4,144,384]{2,1,0:T(8,128)(2,1)S(1)}, u32[]{:S(2)}, u32[]{:S(2)}) async-start(bf16[4,144,384]{2,1,0:T(8,128)(2,1)} %shard_map.75), calls=%async_computation.1 | async-start | bytes 884736 | tf_op jit(solution)/shard_map/all_to_all | solution.py:297
  67.7 0.8 copy-start.3
  76.0 19.0 %all-to-all-start.2 = ((bf16[64,6,256]{2,1,0:T(8,128)(2,1)}), bf16[64,6,256]{2,1,0:T(8,128)(2,1)S(1)}, u32[]{:S(2)}, u32[]{:S(2)}) async-start(bf16[64,6,256]{2,1,0:T(8,128)(2,1)} %shard_map.76), calls=%async_computation.2 | async-start | bytes 524288 | tf_op jit(solution)/shard_map/all_to_all | solution.py:306
  95.2 8.7 %copy-start = (bf16[256,4096]{1,0:T(8,128)(2,1)}, bf16[256,4096]{1,0:T(8,128)(2,1)S(1)}, u32[]{:S(2)}) copy-start(bf16[256,4096]{1,0:T(8,128)(2,1)S(1)} %collective-permute-done.2.w2) | copy-start | bytes 6291460
  104.0 42.6 %copy-start.1 = (bf16[16,4096]{1,0:T(8,128)(2,1)S(1)}, bf16[16,4096]{1,0:T(8,128)(2,1)}, u32[]{:S(2)}) copy-start(bf16[16,4096]{1,0:T(8,128)(2,1)} %param.13) | copy-start | bytes 393220
  108.9 14.0 %collective-permute-start.3 = (bf16[8,4096]{1,0:T(8,128)(2,1)}, bf16[8,4096]{1,0:T(8,128)(2,1)S(1)}, u32[]{:S(2)}, u32[]{:S(2)}) collective-permute-start(bf16[8,4096]{1,0:T(8,128)(2,1)} %get-tuple-element.26), channel_id=1, source_target_pairs={{0,3},{3,6},{6,9},{9,0},{1,4},{4,7},{7,10},{10,1},{2,5},{5,8},{8,1... | collective-permute-start | bytes 196616 | tf_op jit(solution)/shard_map/ppermute | solution.py:332
  116.9 11.5 %collective-permute-start.4 = (bf16[8,4096]{1,0:T(8,128)(2,1)}, bf16[8,4096]{1,0:T(8,128)(2,1)S(1)}, u32[]{:S(2)}, u32[]{:S(2)}) collective-permute-start(bf16[8,4096]{1,0:T(8,128)(2,1)} %get-tuple-element.30), channel_id=1, source_target_pairs={{0,9},{3,0},{6,3},{9,6},{1,10},{4,1},{7,4},{10,7},{2,11},{5,2},{8,... | collective-permute-start | bytes 196616 | tf_op jit(solution)/shard_map/ppermute | solution.py:333
  129.4 11.6 %collective-permute-start.5 = (bf16[16,4096]{1,0:T(8,128)(2,1)S(1)}, bf16[16,4096]{1,0:T(8,128)(2,1)S(1)}, u32[]{:S(2)}, u32[]{:S(2)}) collective-permute-start(bf16[16,4096]{1,0:T(8,128)(2,1)S(1)} %get-tuple-element.31), channel_id=1, source_target_pairs={{0,3},{3,6},{6,9},{9,0},{1,4},{4,7},{7,10},{10,1},{2,5},{5,8},{8,1... | collective-permute-start | bytes 393224 | tf_op jit(solution)/shard_map/ppermute | solution.py:337
  135.7 10.9 %collective-permute-start.6 = (bf16[16,4096]{1,0:T(8,128)(2,1)S(1)}, bf16[16,4096]{1,0:T(8,128)(2,1)S(1)}, u32[]{:S(2)}, u32[]{:S(2)}) collective-permute-start(bf16[16,4096]{1,0:T(8,128)(2,1)S(1)} %get-tuple-element.32), channel_id=1, source_target_pairs={{0,9},{3,0},{6,3},{9,6},{1,10},{4,1},{7,4},{10,7},{2,11},{5,2},{8,... | collective-permute-start | bytes 393224 | tf_op jit(solution)/shard_map/ppermute | solution.py:338

commit v3 on v2

--- a/solution.py
+++ b/solution.py
@@ -35,7 +35,10 @@
     return (v + jnp.abs(v) * 0.0079).astype(jnp.bfloat16).astype(jnp.float32)
 
 
-def attend_kernel(lengths, q_ref, own_ref, peer_ref, out_ref, q_s, m_s, l_s, acc_s):
+def attend_kernel(lengths, *refs):
+    q_refs, (own_ref, peer_ref, out_ref, q_all, q_s, m_s, l_s, acc_s) = refs[:NX], refs[NX:]
+    for s, q_ref in enumerate(q_refs):
+        q_all[s] = q_ref[...]
     x, y, c = (lax.axis_index(a) for a in ("x", "y", "c"))
 
     def empty(xs, carry):
@@ -60,8 +63,8 @@
             start = jnp.where(pos >= end, end, start)
             first_start = jnp.where(p0 >= end, end, first_start)
             last_start = jnp.where(last >= end, end, last_start)
-        q_s[:TOK, :] = q_ref[xs, :, :HEAD]
-        q_s[TOK:, :] = q_ref[xs, :, HEAD:]
+        q_s[:TOK, :] = q_all[xs - x, :, :HEAD]
+        q_s[TOK:, :] = q_all[xs - x, :, HEAD:]
         m_s[...] = jnp.full((1, QROWS), FLOOR, jnp.float32)
         l_s[...] = jnp.zeros((1, QROWS), jnp.float32)
         acc_s[...] = jnp.zeros((HEAD, QROWS), jnp.float32)
@@ -192,39 +195,20 @@
     )
 
 
-def project_kernel(x_ref, w0, w1, w2, own_ref, *piece_refs):
-    c, j, q = (lax.axis_index(a) for a in ("c", "j", "q"))
-
-    def rows_of(member):
-        member = lax.rem(member, NJ)
-        turned = [
-            x_ref[member, pl.ds(pl.multiple_of(lax.rem(q + s, NQ) * OUT, OUT), OUT), :]
-            for s in range(NQ)
-        ]
-        return jnp.concatenate(turned, axis=0)
-
-    total = jnp.dot(rows_of(j), w0[...], preferred_element_type=jnp.float32)
-    total += jnp.dot(rows_of(j + 2 - c), w1[...], preferred_element_type=jnp.float32)
-    total += jnp.dot(rows_of(j + 1 + c), w2[...], preferred_element_type=jnp.float32)
-    own_ref[...] = total[:OUT]
-    half = OUT // 2
-    for n, ref in enumerate(piece_refs):
-        ref[...] = total[OUT + n * half : OUT + (n + 1) * half].astype(ref.dtype)
-
-
-def fold_kernel(near_ref, near_add, near_rest, far_rest, far_ref, far_add, ahead_ref, behind_ref):
-    half = OUT // 2
-    ahead_ref[:half] = (near_ref[...] + near_add[...].astype(jnp.float32)).astype(jnp.bfloat16)
-    ahead_ref[half:] = near_rest[...]
-    behind_ref[:half] = far_rest[...]
-    behind_ref[half:] = (far_ref[...] + far_add[...].astype(jnp.float32)).astype(jnp.bfloat16)
-
-
-def prepare_kernel(head, q_ref, k_ref, v_ref, copies_ref, kv_ref):
-    for i in range(NX):
-        copies_ref[i] = q_ref[...]
-    kv_ref[:, :HEAD] = k_ref[...]
-    kv_ref[:, HEAD:] = v_ref[...]
+def project_kernel(x_ref, w0, w1, w2, out_ref):
+    c, j = lax.axis_index("c"), lax.axis_index("j")
+    total = jnp.dot(x_ref[j], w0[...], preferred_element_type=jnp.float32)
+    for w, step in ((w1, 2 - c), (w2, 1 + c)):
+        rows = x_ref[lax.rem(j + step, NJ)]
+        total += jnp.dot(rows, w[...], preferred_element_type=jnp.float32)
+    for n in range(NQ):
+        out_ref[n] = total[n * OUT : (n + 1) * OUT].astype(jnp.bfloat16)
+
+
+def prepare_kernel(head, k_ref, v_ref, kv_ref):
+    for i in range(NY):
+        kv_ref[i, :, :HEAD] = k_ref[...]
+        kv_ref[i, :, HEAD:] = v_ref[...]
 
 
 def vmem():
@@ -254,46 +238,38 @@
     dc = (x * NY + y) * NC + c
     peer = [(0, 1), (1, 0)]
 
-    def turn(size, step):
-        return [(i, (i + step) % size) for i in range(size)]
-
     around = [
         (k * NJ + i, k * NJ + (i + 1 + k) % NJ) for k in range(NC) for i in range(NJ)
     ]
     turned = lax.ppermute(out_weight, ("c", "j"), around)
     block = pl.BlockSpec((TOK, HEAD), lambda i, head: (0, head[0]))
-    copies, kv = pl.pallas_call(
+    kv = pl.pallas_call(
         prepare_kernel,
-        out_shape=[
-            jax.ShapeDtypeStruct((NX, TOK, COLS), jnp.bfloat16),
-            out_here(TOK, COLS),
-        ],
+        out_shape=jax.ShapeDtypeStruct((NY, TOK, COLS), jnp.bfloat16),
         grid_spec=pltpu.PrefetchScalarGridSpec(
             num_scalar_prefetch=1,
             grid=(1,),
-            in_specs=[pl.BlockSpec((TOK, COLS), lambda i, head: (0, 0)), block, block],
-            out_specs=[
-                pl.BlockSpec((NX, TOK, COLS), lambda i, head: (0, 0, 0)),
-                pl.BlockSpec((TOK, COLS), lambda i, head: (0, 0)),
-            ],
+            in_specs=[block, block],
+            out_specs=pl.BlockSpec((NY, TOK, COLS), lambda i, head: (0, 0, 0)),
         ),
         name="prepare",
-    )((tp * HEADS_HERE // GROUP).reshape(1).astype(jnp.int32), queries, keys, values)
-    q_all = lax.all_to_all(copies, "x", 0, 0, tiled=True)
-    own = lax.all_gather(kv, "y", axis=0, tiled=True)
+    )((tp * HEADS_HERE // GROUP).reshape(1).astype(jnp.int32), keys, values)
+    own = lax.all_to_all(kv, "y", 0, 0, tiled=True).reshape(NY * TOK, COLS)
+    moved = [lax.ppermute(queries, "x", [(i, i - s) for i in range(s, NX)]) for s in range(1, NX)]
     other = lax.ppermute(own, "c", peer)
 
     partial = kernel(
         attend_kernel,
         out_here(NX, PART, QROWS),
-        [smem(), vmem(), vmem(), vmem()],
+        [smem()] + [vmem()] * (NX + 2),
         scratch_shapes=[
+            pltpu.VMEM((NX, TOK, COLS), jnp.bfloat16),
             pltpu.VMEM((QROWS, HEAD), jnp.bfloat16),
             pltpu.VMEM((1, QROWS), jnp.float32),
             pltpu.VMEM((1, QROWS), jnp.float32),
             pltpu.VMEM((HEAD, QROWS), jnp.float32),
         ],
-    )(lengths, near_core(q_all), near_core(own), near_core(other))
+    )(lengths, queries, *map(near_core, moved), near_core(own), near_core(other))
     parts = lax.all_to_all(partial, "x", 0, 0, tiled=True)
 
     targets = lax.dynamic_slice_in_dim(mlp_owner, dc * TOK, TOK, 0)
@@ -317,27 +293,19 @@
 
     width = out_weight.shape[1]
     tile = 1024
-    half = OUT // 2
-    f32, bf16 = jnp.float32, jnp.bfloat16
-    blocks = [(OUT, f32), (half, f32), (half, bf16), (half, bf16), (half, bf16)]
-    blocks += [(half, bf16), (half, f32)]
-    mine, near, near_rest, c1, c2, far_rest, far = pl.pallas_call(
+    projected = pl.pallas_call(
         project_kernel,
-        out_shape=[jax.ShapeDtypeStruct((n, width), t) for n, t in blocks],
+        out_shape=jax.ShapeDtypeStruct((NQ, OUT, width), jnp.bfloat16),
         grid=(width // tile,),
         in_specs=[vmem()] + [pl.BlockSpec((COLS, tile), lambda n: (0, n))] * 3,
-        out_specs=[pl.BlockSpec((n, tile), lambda n: (0, n)) for n, _ in blocks],
+        out_specs=pl.BlockSpec((NQ, OUT, tile), lambda n: (0, 0, n)),
         name="project",
     )(near_core(shared), out_weight, turned, swapped)
-    c1 = lax.ppermute(c1, "q", turn(NQ, 1))
-    c2 = lax.ppermute(c2, "q", turn(NQ, 3))
-    ahead, behind = kernel(fold_kernel, [out_here(OUT, width)] * 2, [vmem()] * 6)(
-        near, near_core(c1), near_rest, far_rest, far, near_core(c2)
-    )
-    ahead = lax.ppermute(ahead, "q", turn(NQ, 1))
-    behind = lax.ppermute(behind, "q", turn(NQ, 3))
-    total = mine + ahead.astype(jnp.float32) + behind.astype(jnp.float32)
-    return (total + residual.astype(jnp.float32)).astype(jnp.bfloat16)
+    blocks = lax.all_to_all(projected, "q", 0, 0, tiled=True)
+    total = residual.astype(jnp.float32)
+    for n in range(NQ):
+        total += blocks[n].astype(jnp.float32)
+    return total.astype(jnp.bfloat16)
 
 
 def solution(mesh):

time: 149 us -> 151 us (1.013)
  waiting for transfers between devices: 29.9 us -> 51 us
  starting transfers between devices: 48.7 us -> 37 us
  blocking collectives: 52.3 us -> 46.1 us
    all_gather x1 -> x0, blocking collectives: 27.8 us -> none  [per_device(): own = lax.all_gather(kv, 'y', axis=0, tiled=True)]
    all_to_all x1, blocking collectives: 15.8 us -> 37 us  [per_device(): blocks = lax.all_to_all(projected, 'q', 0, 0, tiled=True)]
    all_to_all x0 -> x1, waiting for transfers between devices: none -> 18.8 us  [per_device(): own = lax.all_to_all(kv, 'y', 0, 0, tiled=True).reshape(NY * TOK, COLS)]
    ppermute x4 -> x3, starting transfers between devices: 21.5 us -> 6.49 us  [per_device(): lax.ppermute(queries, 'x', [(i, i - s) for i in range(s, NX)])]
    ppermute x1, waiting for transfers between devices: 0.01 us -> 15 us  [per_device(): turned = lax.ppermute(out_weight, ('c', 'j'), around)]
    ppermute x4 -> x3, waiting for transfers between devices: 15 us -> 2.4 us  [per_device(): lax.ppermute(queries, 'x', [(i, i - s) for i in range(s, NX)])]
    all_to_all x0 -> x1, starting transfers between devices: none -> 7.23 us  [per_device(): own = lax.all_to_all(kv, 'y', 0, 0, tiled=True).reshape(NY * TOK, COLS)]
    all_to_all x1, starting transfers between devices: 11.3 us -> 4.78 us  [per_device(): parts = lax.all_to_all(partial, 'x', 0, 0, tiled=True)]
  transfers between devices with their start and end apart: 9 -> 9, of which waited for: 6 -> 6; matrix products, arithmetic and copies ran while one was open for 1% -> 1% of each run, Pallas kernels for 5% -> 4%
where the time goes in v3:
time: 151 us; the launch traced here: 150 us
  waiting for transfers between devices  51 us (34%)
  blocking collectives  46.1 us (31%)
  starting transfers between devices  37 us (25%)
  Pallas kernels  13.3 us (9%)
  local copies, waits for them, and re-layouts  1.64 us (1%)
    all_to_all x1, blocking collectives, per_device(): blocks = lax.all_to_all(projected, 'q', 0, 0, tiled=True)  37 us
    all_to_all x1, waiting for transfers between devices, per_device(): own = lax.all_to_all(kv, 'y', 0, 0, tiled=True).reshape(NY * TOK, COLS)  18.8 us
    ppermute x1, waiting for transfers between devices, per_device(): turned = lax.ppermute(out_weight, ('c', 'j'), around)  15 us
    all_to_all x1, starting transfers between devices, per_device(): incoming = lax.all_to_all(outgoing, ('x', 'y', 'c'), 0, 0, tiled=True)  10.4 us
    all_to_all x1, waiting for transfers between devices, per_device(): incoming = lax.all_to_all(outgoing, ('x', 'y', 'c'), 0, 0, tiled=True)  9.58 us
    all_to_all x1, blocking collectives, per_device(): lax.all_to_all(owned.reshape(NJ, TOK // NJ, COLS), 'j', 0, 0, tiled=True)  9.12 us
    all_to_all x1, starting transfers between devices, per_device(): own = lax.all_to_all(kv, 'y', 0, 0, tiled=True).reshape(NY * TOK, COLS)  7.23 us
    ppermute x3, starting transfers between devices, per_device(): lax.ppermute(queries, 'x', [(i, i - s) for i in range(s, NX)])  6.49 us
  transfers between devices with their start and end apart: 9, of which 6 were waited for; matrix products, arithmetic and copies ran while one was open for 1% of the time, Pallas kernels for 4%

profile of v3, /device:TPU:6, one launch (start us, length us, event | category | flops | bytes accessed | tf_op | source)
XLA Modules:
  0.0 149.9 jit_solution(17429299081986423881)
XLA Ops:
  0.0 1.9 %prepare.1 = bf16[8,192,256]{2,1,0:T(8,128)(2,1)} custom-call(s32[1]{0:T(128)} %bitcast.2.head, bf16[192,768]{1,0:T(8,128)(2,1)} %k_ref.1, bf16[192,768]{1,0:T(8,128)(2,1)} %v_ref.1), custom_call_target="tpu_custom_call" | custom-call | tf_op jit(solution)/shard_map/prepare/pallas_call | solution.py:246
  1.9 7.2 %all-to-all-start = ((bf16[8,192,256]{2,1,0:T(8,128)(2,1)}), bf16[8,192,256]{2,1,0:T(8,128)(2,1)S(1)}, u32[]{:S(2)}, u32[]{:S(2)}) async-start(bf16[8,192,256]{2,1,0:T(8,128)(2,1)} %prepare.1), calls=%async_computation | async-start | bytes 1572864 | tf_op jit(solution)/shard_map/all_to_all | solution.py:257
  9.1 4.3 %collective-permute-start.4 = (bf16[256,4096]{1,0:T(8,128)(2,1)}, bf16[256,4096]{1,0:T(8,128)(2,1)}, u32[]{:S(2)}, u32[]{:S(2)}) collective-permute-start(bf16[256,4096]{1,0:T(8,128)(2,1)} %w0.1), channel_id=1, source_target_pairs={{0,1},{1,2},{2,0},{12,14},{13,12},{14,13},{3,4},{4,5},{5,3},{15,17... | collective-permute-start | bytes 6291464 | tf_op jit(solution)/shard_map/ppermute | solution.py:244
  13.4 18.8 %all-to-all-done = bf16[8,192,256]{2,1,0:T(8,128)(2,1)S(1)} async-done(((bf16[8,192,256]{2,1,0:T(8,128)(2,1)}), bf16[8,192,256]{2,1,0:T(8,128)(2,1)S(1)}, u32[]{:S(2)}, u32[]{:S(2)}) %all-to-all-start) | async-done | bytes 786464 | tf_op jit(solution)/shard_map/all_to_all | solution.py:257
  32.2 1.9 %collective-permute-start.3 = (bf16[1536,256]{1,0:T(8,128)(2,1)S(1)}, bf16[1536,256]{1,0:T(8,128)(2,1)S(1)}, u32[]{:S(2)}, u32[]{:S(2)}) collective-permute-start(bf16[1536,256]{1,0:T(8,128)(2,1)S(1)} %bitcast.25), channel_id=1, source_target_pairs={{0,12},{12,0},{1,13},{13,1},{2,14},{14,2},{3,15},{15,3},{4,16},{16... | collective-permute-start | bytes 2359304 | tf_op jit(solution)/shard_map/ppermute | solution.py:259
  34.1 3.3 %collective-permute-start.1 = (bf16[192,256]{1,0:T(8,128)(2,1)S(1)}, bf16[192,256]{1,0:T(8,128)(2,1)S(1)}, u32[]{:S(2)}, u32[]{:S(2)}) collective-permute-start(bf16[192,256]{1,0:T(8,128)(2,1)S(1)} %copy-done.2), channel_id=1, source_target_pairs={{384,0},{576,192},{385,1},{577,193},{386,2},{578,194},{387,3},{579... | collective-permute-start | bytes 294920 | tf_op jit(solution)/shard_map/ppermute | solution.py:258
  37.5 1.9 %collective-permute-start = (bf16[192,256]{1,0:T(8,128)(2,1)S(1)}, bf16[192,256]{1,0:T(8,128)(2,1)S(1)}, u32[]{:S(2)}, u32[]{:S(2)}) collective-permute-start(bf16[192,256]{1,0:T(8,128)(2,1)S(1)} %copy-done.2), channel_id=1, source_target_pairs={{192,0},{384,192},{576,384},{193,1},{385,193},{577,385},{194,2},{3... | collective-permute-start | bytes 294920 | tf_op jit(solution)/shard_map/ppermute | solution.py:258
  39.3 1.3 collective-permute-start.2
  40.6 0.0 collective-permute-done.1.refs_2_
  40.7 1.6 %collective-permute-done.refs_1_ = bf16[192,256]{1,0:T(8,128)(2,1)S(1)} collective-permute-done((bf16[192,256]{1,0:T(8,128)(2,1)S(1)}, bf16[192,256]{1,0:T(8,128)(2,1)S(1)}, u32[]{:S(2)}, u32[]{:S(2)}) %collective-permute-start) | collective-permute-done | bytes 98336 | tf_op jit(solution)/shard_map/ppermute | solution.py:258
  42.3 0.8 collective-permute-done.2.refs_3_
  43.1 0.0 collective-permute-done.3.refs_5_
  43.1 2.8 %shard_map.75 = bf16[4,144,384]{2,1,0:T(8,128)(2,1)} custom-call(s32[24]{0:T(128)} %lengths.1, bf16[192,256]{1,0:T(8,128)(2,1)} %refs_0_.1, bf16[192,256]{1,0:T(8,128)(2,1)S(1)} %collective-permute-done.refs_1_, bf16[192,256]{1,0:T(8,128)(2,1)S(1)} %collective-permute-done.1.refs_2_, bf16[192,256]{1,0:T(8,128)(2,1)S(1)} %collective-permute-done.2.refs_3_, ...), custom_call_target="tpu_custom_call" | custom-call | tf_op jit(solution)/shard_map/pallas_call | solution.py:261
  45.8 15.0 %collective-permute-done.4.w1 = bf16[256,4096]{1,0:T(8,128)(2,1)} collective-permute-done((bf16[256,4096]{1,0:T(8,128)(2,1)}, bf16[256,4096]{1,0:T(8,128)(2,1)}, u32[]{:S(2)}, u32[]{:S(2)}) %collective-permute-start.4) | collective-permute-done | bytes 2097184 | tf_op jit(solution)/shard_map/ppermute | solution.py:244
  60.8 1.9 %collective-permute-start.5 = (bf16[256,4096]{1,0:T(8,128)(2,1)}, bf16[256,4096]{1,0:T(8,128)(2,1)S(1)}, u32[]{:S(2)}, u32[]{:S(2)}) collective-permute-start(bf16[256,4096]{1,0:T(8,128)(2,1)} %collective-permute-done.4.w1), channel_id=1, source_target_pairs={{0,12},{12,0},{1,13},{13,1},{2,14},{14,2},{3,15},{15,3},{4,16},{16... | collective-permute-start | bytes 6291464 | tf_op jit(solution)/shard_map/ppermute | solution.py:290
  62.7 4.8 %all-to-all-start.1 = ((bf16[4,144,384]{2,1,0:T(8,128)(2,1)}), bf16[4,144,384]{2,1,0:T(8,128)(2,1)S(1)}, u32[]{:S(2)}, u32[]{:S(2)}) async-start(bf16[4,144,384]{2,1,0:T(8,128)(2,1)} %shard_map.75), calls=%async_computation.1 | async-start | bytes 884736 | tf_op jit(solution)/shard_map/all_to_all | solution.py:273
  67.5 0.1 dynamic_slice.3
  67.6 0.8 copy.8.col_ref
  68.4 1.1 shard_map.74.placement
  69.5 5.2 %all-to-all-done.1.part_ref = bf16[4,144,384]{2,1,0:T(8,128)(2,1)S(1)} async-done(((bf16[4,144,384]{2,1,0:T(8,128)(2,1)}), bf16[4,144,384]{2,1,0:T(8,128)(2,1)S(1)}, u32[]{:S(2)}, u32[]{:S(2)}) %all-to-all-start.1) | async-done | bytes 442400 | tf_op jit(solution)/shard_map/all_to_all | solution.py:273
  74.7 1.1 shard_map.76
  75.8 10.4 %all-to-all-start.2 = ((bf16[64,6,256]{2,1,0:T(8,128)(2,1)}), bf16[64,6,256]{2,1,0:T(8,128)(2,1)S(1)}, u32[]{:S(2)}, u32[]{:S(2)}) async-start(bf16[64,6,256]{2,1,0:T(8,128)(2,1)} %shard_map.76), calls=%async_computation.2 | async-start | bytes 524288 | tf_op jit(solution)/shard_map/all_to_all | solution.py:282
  86.2 0.7 reshape.29.owner_ref
  86.9 1.2 shard_map.73.chooser
  88.2 9.6 %all-to-all-done.2 = bf16[64,6,256]{2,1,0:T(8,128)(2,1)S(1)} async-done(((bf16[64,6,256]{2,1,0:T(8,128)(2,1)}), bf16[64,6,256]{2,1,0:T(8,128)(2,1)S(1)}, u32[]{:S(2)}, u32[]{:S(2)}) %all-to-all-start.2) | async-done | bytes 196640 | tf_op jit(solution)/shard_map/all_to_all | solution.py:282
  97.7 0.1 reshape.34.in_ref
  97.8 0.2 shard_map.77
  98.0 0.0 collective-permute-done.5.w2
  98.0 9.1 %all_to_all.25.x_ref = bf16[3,64,256]{2,1,0:T(8,128)(2,1)S(1)} all-to-all(bf16[3,64,256]{2,1,0:T(8,128)(2,1)S(1)} %bitcast.27), channel_id=1, replica_groups=mesh['x'=4,'y'=8,'c'=2,'q'=4,'j'=3] {'j'}, dimensions={0} | all-to-all | bytes 196608 | tf_op jit(solution)/shard_map/all_to_all | solution.py:292
  107.2 5.0 %project.1 = bf16[4,16,4096]{2,1,0:T(8,128)(2,1)} custom-call(bf16[3,64,256]{2,1,0:T(8,128)(2,1)S(1)} %all_to_all.25.x_ref, bf16[256,4096]{1,0:T(8,128)(2,1)} %w0.1, bf16[256,4096]{1,0:T(8,128)(2,1)} %collective-permute-done.4.w1, bf16[256,4096]{1,0:T(8,128)(2,1)} %copy-done), custom_call_target="tpu_custom_call" | custom-call | tf_op jit(solution)/shard_map/project/pallas_call | solution.py:296
  112.1 37.0 %all_to_all.26 = bf16[4,16,4096]{2,1,0:T(8,128)(2,1)S(1)} all-to-all(bf16[4,16,4096]{2,1,0:T(8,128)(2,1)} %project.1), channel_id=1, replica_groups=mesh['x'=4,'y'=8,'c'=2,'q'=4,'j'=3] {'q'}, dimensions={0} | all-to-all | bytes 1048576 | tf_op jit(solution)/shard_map/all_to_all | solution.py:304
  149.1 0.7 fusion
  (10 shorter events, 0.0 us)
Async XLA Ops:
  0.0 34.1 %copy-start.2 = (bf16[192,256]{1,0:T(8,128)(2,1)S(1)}, bf16[192,256]{1,0:T(8,128)(2,1)}, u32[]{:S(2)}) copy-start(bf16[192,256]{1,0:T(8,128)(2,1)} %refs_0_.1) | copy-start | bytes 294916
  1.9 65.7 %copy-start.3 = (s32[12288]{0:T(1024)S(1)}, s32[12288]{0:T(1024)}, u32[]{:S(2)}) copy-start(s32[12288]{0:T(1024)} %param.11) | copy-start | bytes 147460
  1.9 30.3 %all-to-all-start = ((bf16[8,192,256]{2,1,0:T(8,128)(2,1)}), bf16[8,192,256]{2,1,0:T(8,128)(2,1)S(1)}, u32[]{:S(2)}, u32[]{:S(2)}) async-start(bf16[8,192,256]{2,1,0:T(8,128)(2,1)} %prepare.1), calls=%async_computation | async-start | bytes 1572864 | tf_op jit(solution)/shard_map/all_to_all | solution.py:257
  9.1 51.7 %collective-permute-start.4 = (bf16[256,4096]{1,0:T(8,128)(2,1)}, bf16[256,4096]{1,0:T(8,128)(2,1)}, u32[]{:S(2)}, u32[]{:S(2)}) collective-permute-start(bf16[256,4096]{1,0:T(8,128)(2,1)} %w0.1), channel_id=1, source_target_pairs={{0,1},{1,2},{2,0},{12,14},{13,12},{14,13},{3,4},{4,5},{5,3},{15,17... | collective-permute-start | bytes 6291464 | tf_op jit(solution)/shard_map/ppermute | solution.py:244
  32.2 10.9 %collective-permute-start.3 = (bf16[1536,256]{1,0:T(8,128)(2,1)S(1)}, bf16[1536,256]{1,0:T(8,128)(2,1)S(1)}, u32[]{:S(2)}, u32[]{:S(2)}) collective-permute-start(bf16[1536,256]{1,0:T(8,128)(2,1)S(1)} %bitcast.25), channel_id=1, source_target_pairs={{0,12},{12,0},{1,13},{13,1},{2,14},{14,2},{3,15},{15,3},{4,16},{16... | collective-permute-start | bytes 2359304 | tf_op jit(solution)/shard_map/ppermute | solution.py:259
  34.1 6.5 %collective-permute-start.1 = (bf16[192,256]{1,0:T(8,128)(2,1)S(1)}, bf16[192,256]{1,0:T(8,128)(2,1)S(1)}, u32[]{:S(2)}, u32[]{:S(2)}) collective-permute-start(bf16[192,256]{1,0:T(8,128)(2,1)S(1)} %copy-done.2), channel_id=1, source_target_pairs={{384,0},{576,192},{385,1},{577,193},{386,2},{578,194},{387,3},{579... | collective-permute-start | bytes 294920 | tf_op jit(solution)/shard_map/ppermute | solution.py:258
  37.5 4.8 %collective-permute-start = (bf16[192,256]{1,0:T(8,128)(2,1)S(1)}, bf16[192,256]{1,0:T(8,128)(2,1)S(1)}, u32[]{:S(2)}, u32[]{:S(2)}) collective-permute-start(bf16[192,256]{1,0:T(8,128)(2,1)S(1)} %copy-done.2), channel_id=1, source_target_pairs={{192,0},{384,192},{576,384},{193,1},{385,193},{577,385},{194,2},{3... | collective-permute-start | bytes 294920 | tf_op jit(solution)/shard_map/ppermute | solution.py:258
  39.3 3.7 %collective-permute-start.2 = (bf16[192,256]{1,0:T(8,128)(2,1)S(1)}, bf16[192,256]{1,0:T(8,128)(2,1)S(1)}, u32[]{:S(2)}, u32[]{:S(2)}) collective-permute-start(bf16[192,256]{1,0:T(8,128)(2,1)S(1)} %copy-done.2), channel_id=1, source_target_pairs={{576,0},{577,1},{578,2},{579,3},{580,4},{581,5},{582,6},{583,7},{5... | collective-permute-start | bytes 294920 | tf_op jit(solution)/shard_map/ppermute | solution.py:258
  60.8 37.2 %collective-permute-start.5 = (bf16[256,4096]{1,0:T(8,128)(2,1)}, bf16[256,4096]{1,0:T(8,128)(2,1)S(1)}, u32[]{:S(2)}, u32[]{:S(2)}) collective-permute-start(bf16[256,4096]{1,0:T(8,128)(2,1)} %collective-permute-done.4.w1), channel_id=1, source_target_pairs={{0,12},{12,0},{1,13},{13,1},{2,14},{14,2},{3,15},{15,3},{4,16},{16... | collective-permute-start | bytes 6291464 | tf_op jit(solution)/shard_map/ppermute | solution.py:290
  62.7 12.0 %all-to-all-start.1 = ((bf16[4,144,384]{2,1,0:T(8,128)(2,1)}), bf16[4,144,384]{2,1,0:T(8,128)(2,1)S(1)}, u32[]{:S(2)}, u32[]{:S(2)}) async-start(bf16[4,144,384]{2,1,0:T(8,128)(2,1)} %shard_map.75), calls=%async_computation.1 | async-start | bytes 884736 | tf_op jit(solution)/shard_map/all_to_all | solution.py:273
  67.6 0.8 copy-start.4
  75.8 21.9 %all-to-all-start.2 = ((bf16[64,6,256]{2,1,0:T(8,128)(2,1)}), bf16[64,6,256]{2,1,0:T(8,128)(2,1)S(1)}, u32[]{:S(2)}, u32[]{:S(2)}) async-start(bf16[64,6,256]{2,1,0:T(8,128)(2,1)} %shard_map.76), calls=%async_computation.2 | async-start | bytes 524288 | tf_op jit(solution)/shard_map/all_to_all | solution.py:282
  98.0 9.1 %copy-start = (bf16[256,4096]{1,0:T(8,128)(2,1)}, bf16[256,4096]{1,0:T(8,128)(2,1)S(1)}, u32[]{:S(2)}) copy-start(bf16[256,4096]{1,0:T(8,128)(2,1)S(1)} %collective-permute-done.5.w2) | copy-start | bytes 6291460
  107.2 42.0 %copy-start.1 = (bf16[16,4096]{1,0:T(8,128)(2,1)S(1)}, bf16[16,4096]{1,0:T(8,128)(2,1)}, u32[]{:S(2)}) copy-start(bf16[16,4096]{1,0:T(8,128)(2,1)} %param.13) | copy-start | bytes 393220

commit v4 on v3

--- a/solution.py
+++ b/solution.py
@@ -13,11 +13,10 @@
 HEADS_HERE = 2
 COLS = HEADS_HERE * HEAD
 QROWS = HEADS_HERE * TOK
-SLOTS = 6
-PADDED = 8
 OUT = TOK // (NQ * NJ)
 N_DC = NX * NY * NC
-SLOT_TOTAL = N_DC * SLOTS
+PADDED = 8
+SLOT_TOTAL = N_DC * PADDED
 CHUNK_SLABS = 4
 CHUNK = CHUNK_SLABS * TOK
 PART = HEAD + 16
@@ -135,7 +134,7 @@
     same = (col_ref[...] == target) & earlier
     rank = jnp.sum(same.astype(jnp.int32), axis=0, keepdims=True)
     slot = target * PADDED + rank
-    ids = lax.broadcasted_iota(jnp.int32, (N_DC * PADDED, TOK), 0)
+    ids = lax.broadcasted_iota(jnp.int32, (SLOT_TOTAL, TOK), 0)
     out_ref[...] = (ids == slot).astype(jnp.float32).astype(jnp.bfloat16)
 
 
@@ -158,8 +157,7 @@
             NT,
             preferred_element_type=jnp.float32,
         )
-        rows = rows.reshape(N_DC, PADDED, HEAD)[:, :SLOTS, :]
-        out_ref[:, :, h * HEAD : (h + 1) * HEAD] = rows.astype(jnp.bfloat16)
+        out_ref[:, h * HEAD : (h + 1) * HEAD] = rows.astype(jnp.bfloat16)
 
 
 def choose_kernel(owner_ref, out_ref):
@@ -176,11 +174,11 @@
     ).astype(jnp.bfloat16)
     src = lax.broadcasted_iota(jnp.int32, (N_DC, SLOT_TOTAL), 0)
     slot = lax.broadcasted_iota(jnp.int32, (N_DC, SLOT_TOTAL), 1)
-    inside = (slot >= src * SLOTS) & (slot < (src + 1) * SLOTS)
+    inside = (slot >= src * PADDED) & (slot < (src + 1) * PADDED)
     spread = inside.astype(jnp.float32).astype(jnp.bfloat16)
     count = jnp.dot(count, spread, preferred_element_type=jnp.float32)[:1]
     first = jnp.dot(first, spread, preferred_element_type=jnp.float32)[:1]
-    k = (slot[:1] % SLOTS).astype(jnp.float32)
+    k = (slot[:1] % PADDED).astype(jnp.float32)
     g = jnp.where(k < count, first + k, -1.0).astype(jnp.int32)
     at = lax.broadcasted_iota(jnp.int32, (TOK, 1), 0)
     part = (at >= 64).astype(jnp.int32) + (at >= 128).astype(jnp.int32)
@@ -198,9 +196,11 @@
 def project_kernel(x_ref, w0, w1, w2, out_ref):
     c, j = lax.axis_index("c"), lax.axis_index("j")
     total = jnp.dot(x_ref[j], w0[...], preferred_element_type=jnp.float32)
-    for w, step in ((w1, 2 - c), (w2, 1 + c)):
-        rows = x_ref[lax.rem(j + step, NJ)]
-        total += jnp.dot(rows, w[...], preferred_element_type=jnp.float32)
+    total += jnp.dot(x_ref[lax.rem(j + 2 - c, NJ)], w1[...], preferred_element_type=jnp.float32)
+    width = w0.shape[1]
+    columns = pl.ds(pl.multiple_of(pl.program_id(0) * width, width), width)
+    far = x_ref[lax.rem(j + 1 + c, NJ)]
+    total += jnp.dot(far, w2[:, columns], preferred_element_type=jnp.float32)
     for n in range(NQ):
         out_ref[n] = total[n * OUT : (n + 1) * OUT].astype(jnp.bfloat16)
 
@@ -269,16 +269,17 @@
             pltpu.VMEM((1, QROWS), jnp.float32),
             pltpu.VMEM((HEAD, QROWS), jnp.float32),
         ],
-    )(lengths, queries, *map(near_core, moved), near_core(own), near_core(other))
+    )(lengths, *map(near_core, (queries, *moved)), near_core(own), near_core(other))
     parts = lax.all_to_all(partial, "x", 0, 0, tiled=True)
 
     targets = lax.dynamic_slice_in_dim(mlp_owner, dc * TOK, TOK, 0)
-    placement = kernel(place_kernel, out_here(N_DC * PADDED, TOK), [vmem(), vmem()])(
+    placement = kernel(place_kernel, out_here(SLOT_TOTAL, TOK), [vmem(), vmem()])(
         targets.reshape(1, TOK), targets.reshape(TOK, 1)
     )
     outgoing = kernel(
-        merge_kernel, out_here(N_DC, SLOTS, COLS), [vmem(), vmem()]
+        merge_kernel, out_here(SLOT_TOTAL, COLS), [vmem(), vmem()]
     )(near_core(placement), near_core(parts))
+    outgoing = outgoing.reshape(N_DC, PADDED, COLS)
     incoming = lax.all_to_all(outgoing, ("x", "y", "c"), 0, 0, tiled=True)
     chooser = kernel(choose_kernel, out_here(TOK, SLOT_TOTAL), [vmem()])(
         mlp_owner.reshape(N_DC, TOK)
@@ -286,7 +287,7 @@
     owned = kernel(collect_kernel, out_here(TOK, COLS), [vmem(), vmem()])(
         near_core(chooser), near_core(incoming.reshape(SLOT_TOTAL, COLS))
     )
-    turned, _ = lax.optimization_barrier((turned, partial))
+    turned, _ = lax.optimization_barrier((turned, outgoing))
     swapped = lax.ppermute(turned, "c", peer)
     owned, swapped = lax.optimization_barrier((owned, swapped))
     shared = lax.all_to_all(owned.reshape(NJ, TOK // NJ, COLS), "j", 0, 0, tiled=True)
@@ -297,10 +298,10 @@
         project_kernel,
         out_shape=jax.ShapeDtypeStruct((NQ, OUT, width), jnp.bfloat16),
         grid=(width // tile,),
-        in_specs=[vmem()] + [pl.BlockSpec((COLS, tile), lambda n: (0, n))] * 3,
+        in_specs=[vmem()] + [pl.BlockSpec((COLS, tile), lambda n: (0, n))] * 2 + [vmem()],
         out_specs=pl.BlockSpec((NQ, OUT, tile), lambda n: (0, 0, n)),
         name="project",
-    )(near_core(shared), out_weight, turned, swapped)
+    )(near_core(shared), out_weight, turned, near_core(swapped))
     blocks = lax.all_to_all(projected, "q", 0, 0, tiled=True)
     total = residual.astype(jnp.float32)
     for n in range(NQ):

time: 151 us -> 140 us (0.927)
  waiting for transfers between devices: 51 us -> 36.1 us
  starting transfers between devices: 37 us -> 41.8 us
    ppermute x1, waiting for transfers between devices: 15 us -> 0.01 us  [per_device(): turned = lax.ppermute(out_weight, ('c', 'j'), around)]
    all_to_all x1, starting transfers between devices: 4.78 us -> 12.9 us  [per_device(): parts = lax.all_to_all(partial, 'x', 0, 0, tiled=True)]
    all_to_all x1, starting transfers between devices: 10.4 us -> 7.04 us  [per_device(): incoming = lax.all_to_all(outgoing, ('x', 'y', 'c'), 0, 0, tiled=True)]
  transfers between devices with their start and end apart: 9 -> 9, of which waited for: 6 -> 5; matrix products, arithmetic and copies ran while one was open for 1% -> 1% of each run, Pallas kernels for 4% -> 4%
where the time goes in v4:
time: 140 us
  blocking collectives  46.6 us (33%)
  starting transfers between devices  41.8 us (30%)
  waiting for transfers between devices  36.1 us (26%)
  Pallas kernels  12.7 us (9%)
  local copies, waits for them, and re-layouts  1.57 us (1%)
    all_to_all x1, blocking collectives, per_device(): blocks = lax.all_to_all(projected, 'q', 0, 0, tiled=True)  36.2 us
    all_to_all x1, waiting for transfers between devices, per_device(): own = lax.all_to_all(kv, 'y', 0, 0, tiled=True).reshape(NY * TOK, COLS)  18.8 us
    all_to_all x1, starting transfers between devices, per_device(): parts = lax.all_to_all(partial, 'x', 0, 0, tiled=True)  12.9 us
    all_to_all x1, blocking collectives, per_device(): lax.all_to_all(owned.reshape(NJ, TOK // NJ, COLS), 'j', 0, 0, tiled=True)  10.5 us
    all_to_all x1, waiting for transfers between devices, per_device(): incoming = lax.all_to_all(outgoing, ('x', 'y', 'c'), 0, 0, tiled=True)  9.58 us
    all_to_all x1, starting transfers between devices, per_device(): own = lax.all_to_all(kv, 'y', 0, 0, tiled=True).reshape(NY * TOK, COLS)  7.23 us
    all_to_all x1, starting transfers between devices, per_device(): incoming = lax.all_to_all(outgoing, ('x', 'y', 'c'), 0, 0, tiled=True)  7.04 us
    ppermute x3, starting transfers between devices, per_device(): lax.ppermute(queries, 'x', [(i, i - s) for i in range(s, NX)])  6.49 us
  transfers between devices with their start and end apart: 9, of which 5 were waited for; matrix products, arithmetic and copies ran while one was open for 1% of the time, Pallas kernels for 4%

profile of v4, /device:TPU:6, one launch (start us, length us, event | category | flops | bytes accessed | tf_op | source)
XLA Modules:
  0.0 139.6 jit_solution(18044777038874002785)
XLA Ops:
  0.0 1.9 %prepare.1 = bf16[8,192,256]{2,1,0:T(8,128)(2,1)} custom-call(s32[1]{0:T(128)} %bitcast.2.head, bf16[192,768]{1,0:T(8,128)(2,1)} %k_ref.1, bf16[192,768]{1,0:T(8,128)(2,1)} %v_ref.1), custom_call_target="tpu_custom_call" | custom-call | tf_op jit(solution)/shard_map/prepare/pallas_call | solution.py:246
  1.9 7.2 %all-to-all-start = ((bf16[8,192,256]{2,1,0:T(8,128)(2,1)}), bf16[8,192,256]{2,1,0:T(8,128)(2,1)S(1)}, u32[]{:S(2)}, u32[]{:S(2)}) async-start(bf16[8,192,256]{2,1,0:T(8,128)(2,1)} %prepare.1), calls=%async_computation | async-start | bytes 1572864 | tf_op jit(solution)/shard_map/all_to_all | solution.py:257
  9.1 4.3 %collective-permute-start.4 = (bf16[256,4096]{1,0:T(8,128)(2,1)}, bf16[256,4096]{1,0:T(8,128)(2,1)}, u32[]{:S(2)}, u32[]{:S(2)}) collective-permute-start(bf16[256,4096]{1,0:T(8,128)(2,1)} %w0.1), channel_id=1, source_target_pairs={{0,1},{1,2},{2,0},{12,14},{13,12},{14,13},{3,4},{4,5},{5,3},{15,17... | collective-permute-start | bytes 6291464 | tf_op jit(solution)/shard_map/ppermute | solution.py:244
  13.4 18.8 %all-to-all-done = bf16[8,192,256]{2,1,0:T(8,128)(2,1)S(1)} async-done(((bf16[8,192,256]{2,1,0:T(8,128)(2,1)}), bf16[8,192,256]{2,1,0:T(8,128)(2,1)S(1)}, u32[]{:S(2)}, u32[]{:S(2)}) %all-to-all-start) | async-done | bytes 786464 | tf_op jit(solution)/shard_map/all_to_all | solution.py:257
  32.2 1.9 %collective-permute-start.3 = (bf16[1536,256]{1,0:T(8,128)(2,1)S(1)}, bf16[1536,256]{1,0:T(8,128)(2,1)S(1)}, u32[]{:S(2)}, u32[]{:S(2)}) collective-permute-start(bf16[1536,256]{1,0:T(8,128)(2,1)S(1)} %bitcast.27), channel_id=1, source_target_pairs={{0,12},{12,0},{1,13},{13,1},{2,14},{14,2},{3,15},{15,3},{4,16},{16... | collective-permute-start | bytes 2359304 | tf_op jit(solution)/shard_map/ppermute | solution.py:259
  34.1 3.3 %collective-permute-start.1 = (bf16[192,256]{1,0:T(8,128)(2,1)S(1)}, bf16[192,256]{1,0:T(8,128)(2,1)S(1)}, u32[]{:S(2)}, u32[]{:S(2)}) collective-permute-start(bf16[192,256]{1,0:T(8,128)(2,1)S(1)} %copy-done), channel_id=1, source_target_pairs={{384,0},{576,192},{385,1},{577,193},{386,2},{578,194},{387,3},{579... | collective-permute-start | bytes 294920 | tf_op jit(solution)/shard_map/ppermute | solution.py:258
  37.5 1.9 %collective-permute-start = (bf16[192,256]{1,0:T(8,128)(2,1)S(1)}, bf16[192,256]{1,0:T(8,128)(2,1)S(1)}, u32[]{:S(2)}, u32[]{:S(2)}) collective-permute-start(bf16[192,256]{1,0:T(8,128)(2,1)S(1)} %copy-done), channel_id=1, source_target_pairs={{192,0},{384,192},{576,384},{193,1},{385,193},{577,385},{194,2},{3... | collective-permute-start | bytes 294920 | tf_op jit(solution)/shard_map/ppermute | solution.py:258
  39.3 1.3 collective-permute-start.2
  40.7 0.0 collective-permute-done.1.refs_2_
  40.7 1.6 %collective-permute-done.refs_1_ = bf16[192,256]{1,0:T(8,128)(2,1)S(1)} collective-permute-done((bf16[192,256]{1,0:T(8,128)(2,1)S(1)}, bf16[192,256]{1,0:T(8,128)(2,1)S(1)}, u32[]{:S(2)}, u32[]{:S(2)}) %collective-permute-start) | collective-permute-done | bytes 98336 | tf_op jit(solution)/shard_map/ppermute | solution.py:258
  42.3 0.8 collective-permute-done.2.refs_3_
  43.1 0.0 collective-permute-done.3.refs_5_
  43.1 2.5 %shard_map.75 = bf16[4,144,384]{2,1,0:T(8,128)(2,1)} custom-call(s32[24]{0:T(128)} %lengths.1, bf16[192,256]{1,0:T(8,128)(2,1)S(1)} %copy-done, bf16[192,256]{1,0:T(8,128)(2,1)S(1)} %collective-permute-done.refs_1_, bf16[192,256]{1,0:T(8,128)(2,1)S(1)} %collective-permute-done.1.refs_2_, bf16[192,256]{1,0:T(8,128)(2,1)S(1)} %collective-permute-done.2.refs_3_, ...), custom_call_target="tpu_custom_call" | custom-call | tf_op jit(solution)/shard_map/pallas_call | solution.py:261
  45.6 12.9 %all-to-all-start.1 = ((bf16[4,144,384]{2,1,0:T(8,128)(2,1)}), bf16[4,144,384]{2,1,0:T(8,128)(2,1)S(1)}, u32[]{:S(2)}, u32[]{:S(2)}) async-start(bf16[4,144,384]{2,1,0:T(8,128)(2,1)} %shard_map.75), calls=%async_computation.1 | async-start | bytes 884736 | tf_op jit(solution)/shard_map/all_to_all | solution.py:273
  58.5 0.1 dynamic_slice.3
  58.6 0.8 copy.8.col_ref
  59.3 0.0 copy-done.3
  59.3 1.1 shard_map.74.placement
  60.5 5.3 %all-to-all-done.1.part_ref = bf16[4,144,384]{2,1,0:T(8,128)(2,1)S(1)} async-done(((bf16[4,144,384]{2,1,0:T(8,128)(2,1)}), bf16[4,144,384]{2,1,0:T(8,128)(2,1)S(1)}, u32[]{:S(2)}, u32[]{:S(2)}) %all-to-all-start.1) | async-done | bytes 442400 | tf_op jit(solution)/shard_map/all_to_all | solution.py:273
  65.7 1.1 shard_map.76
  66.8 0.0 collective-permute-done.4.w1
  66.8 1.9 %collective-permute-start.5 = (bf16[256,4096]{1,0:T(8,128)(2,1)}, bf16[256,4096]{1,0:T(8,128)(2,1)S(1)}, u32[]{:S(2)}, u32[]{:S(2)}) collective-permute-start(bf16[256,4096]{1,0:T(8,128)(2,1)} %collective-permute-done.4.w1), channel_id=1, source_target_pairs={{0,12},{12,0},{1,13},{13,1},{2,14},{14,2},{3,15},{15,3},{4,16},{16... | collective-permute-start | bytes 6291464 | tf_op jit(solution)/shard_map/ppermute | solution.py:291
  68.7 7.0 %all-to-all-start.2 = ((bf16[64,8,256]{2,1,0:T(8,128)(2,1)}), bf16[64,8,256]{2,1,0:T(8,128)(2,1)S(1)}, u32[]{:S(2)}, u32[]{:S(2)}) async-start(bf16[64,8,256]{2,1,0:T(8,128)(2,1)} %bitcast.4), calls=%async_computation.2 | async-start | bytes 524288 | tf_op jit(solution)/shard_map/all_to_all | solution.py:283
  75.8 0.7 reshape.32.owner_ref
  76.5 1.2 shard_map.73.chooser
  77.7 9.6 %all-to-all-done.2 = bf16[64,8,256]{2,1,0:T(8,128)(2,1)S(1)} async-done(((bf16[64,8,256]{2,1,0:T(8,128)(2,1)}), bf16[64,8,256]{2,1,0:T(8,128)(2,1)S(1)}, u32[]{:S(2)}, u32[]{:S(2)}) %all-to-all-start.2) | async-done | bytes 262176 | tf_op jit(solution)/shard_map/all_to_all | solution.py:283
  87.3 0.2 shard_map.77
  87.5 0.0 collective-permute-done.5.w2
  87.5 10.5 %all_to_all.25.x_ref = bf16[3,64,256]{2,1,0:T(8,128)(2,1)S(1)} all-to-all(bf16[3,64,256]{2,1,0:T(8,128)(2,1)S(1)} %bitcast.30), channel_id=1, replica_groups=mesh['x'=4,'y'=8,'c'=2,'q'=4,'j'=3] {'j'}, dimensions={0} | all-to-all | bytes 196608 | tf_op jit(solution)/shard_map/all_to_all | solution.py:293
  98.0 4.6 %project.1 = bf16[4,16,4096]{2,1,0:T(8,128)(2,1)} custom-call(bf16[3,64,256]{2,1,0:T(8,128)(2,1)S(1)} %all_to_all.25.x_ref, bf16[256,4096]{1,0:T(8,128)(2,1)} %w0.1, bf16[256,4096]{1,0:T(8,128)(2,1)} %collective-permute-done.4.w1, bf16[256,4096]{1,0:T(8,128)(2,1)S(1)} %collective-permute-done.5.w2), custom_call_target="tpu_custom_call" | custom-call | tf_op jit(solution)/shard_map/project/pallas_call | solution.py:297
  102.6 36.2 %all_to_all.26 = bf16[4,16,4096]{2,1,0:T(8,128)(2,1)S(1)} all-to-all(bf16[4,16,4096]{2,1,0:T(8,128)(2,1)} %project.1), channel_id=1, replica_groups=mesh['x'=4,'y'=8,'c'=2,'q'=4,'j'=3] {'q'}, dimensions={0} | all-to-all | bytes 1048576 | tf_op jit(solution)/shard_map/all_to_all | solution.py:305
  138.8 0.7 fusion
  (7 shorter events, 0.0 us)
Async XLA Ops:
  0.0 34.1 %copy-start = (bf16[192,256]{1,0:T(8,128)(2,1)S(1)}, bf16[192,256]{1,0:T(8,128)(2,1)}, u32[]{:S(2)}) copy-start(bf16[192,256]{1,0:T(8,128)(2,1)} %refs_0_.1) | copy-start | bytes 294916
  1.9 56.6 %copy-start.2 = (s32[12288]{0:T(1024)S(1)}, s32[12288]{0:T(1024)}, u32[]{:S(2)}) copy-start(s32[12288]{0:T(1024)} %param.11) | copy-start | bytes 147460
  1.9 30.3 %all-to-all-start = ((bf16[8,192,256]{2,1,0:T(8,128)(2,1)}), bf16[8,192,256]{2,1,0:T(8,128)(2,1)S(1)}, u32[]{:S(2)}, u32[]{:S(2)}) async-start(bf16[8,192,256]{2,1,0:T(8,128)(2,1)} %prepare.1), calls=%async_computation | async-start | bytes 1572864 | tf_op jit(solution)/shard_map/all_to_all | solution.py:257
  9.1 57.7 %collective-permute-start.4 = (bf16[256,4096]{1,0:T(8,128)(2,1)}, bf16[256,4096]{1,0:T(8,128)(2,1)}, u32[]{:S(2)}, u32[]{:S(2)}) collective-permute-start(bf16[256,4096]{1,0:T(8,128)(2,1)} %w0.1), channel_id=1, source_target_pairs={{0,1},{1,2},{2,0},{12,14},{13,12},{14,13},{3,4},{4,5},{5,3},{15,17... | collective-permute-start | bytes 6291464 | tf_op jit(solution)/shard_map/ppermute | solution.py:244
  32.2 10.9 %collective-permute-start.3 = (bf16[1536,256]{1,0:T(8,128)(2,1)S(1)}, bf16[1536,256]{1,0:T(8,128)(2,1)S(1)}, u32[]{:S(2)}, u32[]{:S(2)}) collective-permute-start(bf16[1536,256]{1,0:T(8,128)(2,1)S(1)} %bitcast.27), channel_id=1, source_target_pairs={{0,12},{12,0},{1,13},{13,1},{2,14},{14,2},{3,15},{15,3},{4,16},{16... | collective-permute-start | bytes 2359304 | tf_op jit(solution)/shard_map/ppermute | solution.py:259
  34.1 6.5 %collective-permute-start.1 = (bf16[192,256]{1,0:T(8,128)(2,1)S(1)}, bf16[192,256]{1,0:T(8,128)(2,1)S(1)}, u32[]{:S(2)}, u32[]{:S(2)}) collective-permute-start(bf16[192,256]{1,0:T(8,128)(2,1)S(1)} %copy-done), channel_id=1, source_target_pairs={{384,0},{576,192},{385,1},{577,193},{386,2},{578,194},{387,3},{579... | collective-permute-start | bytes 294920 | tf_op jit(solution)/shard_map/ppermute | solution.py:258
  37.5 4.8 %collective-permute-start = (bf16[192,256]{1,0:T(8,128)(2,1)S(1)}, bf16[192,256]{1,0:T(8,128)(2,1)S(1)}, u32[]{:S(2)}, u32[]{:S(2)}) collective-permute-start(bf16[192,256]{1,0:T(8,128)(2,1)S(1)} %copy-done), channel_id=1, source_target_pairs={{192,0},{384,192},{576,384},{193,1},{385,193},{577,385},{194,2},{3... | collective-permute-start | bytes 294920 | tf_op jit(solution)/shard_map/ppermute | solution.py:258
  39.3 3.7 %collective-permute-start.2 = (bf16[192,256]{1,0:T(8,128)(2,1)S(1)}, bf16[192,256]{1,0:T(8,128)(2,1)S(1)}, u32[]{:S(2)}, u32[]{:S(2)}) collective-permute-start(bf16[192,256]{1,0:T(8,128)(2,1)S(1)} %copy-done), channel_id=1, source_target_pairs={{576,0},{577,1},{578,2},{579,3},{580,4},{581,5},{582,6},{583,7},{5... | collective-permute-start | bytes 294920 | tf_op jit(solution)/shard_map/ppermute | solution.py:258
  45.6 20.1 %all-to-all-start.1 = ((bf16[4,144,384]{2,1,0:T(8,128)(2,1)}), bf16[4,144,384]{2,1,0:T(8,128)(2,1)S(1)}, u32[]{:S(2)}, u32[]{:S(2)}) async-start(bf16[4,144,384]{2,1,0:T(8,128)(2,1)} %shard_map.75), calls=%async_computation.1 | async-start | bytes 884736 | tf_op jit(solution)/shard_map/all_to_all | solution.py:273
  58.6 0.8 copy-start.3
  66.8 20.7 %collective-permute-start.5 = (bf16[256,4096]{1,0:T(8,128)(2,1)}, bf16[256,4096]{1,0:T(8,128)(2,1)S(1)}, u32[]{:S(2)}, u32[]{:S(2)}) collective-permute-start(bf16[256,4096]{1,0:T(8,128)(2,1)} %collective-permute-done.4.w1), channel_id=1, source_target_pairs={{0,12},{12,0},{1,13},{13,1},{2,14},{14,2},{3,15},{15,3},{4,16},{16... | collective-permute-start | bytes 6291464 | tf_op jit(solution)/shard_map/ppermute | solution.py:291
  68.7 18.6 %all-to-all-start.2 = ((bf16[64,8,256]{2,1,0:T(8,128)(2,1)}), bf16[64,8,256]{2,1,0:T(8,128)(2,1)S(1)}, u32[]{:S(2)}, u32[]{:S(2)}) async-start(bf16[64,8,256]{2,1,0:T(8,128)(2,1)} %bitcast.4), calls=%async_computation.2 | async-start | bytes 524288 | tf_op jit(solution)/shard_map/all_to_all | solution.py:283
  98.0 40.8 %copy-start.1 = (bf16[16,4096]{1,0:T(8,128)(2,1)S(1)}, bf16[16,4096]{1,0:T(8,128)(2,1)}, u32[]{:S(2)}) copy-start(bf16[16,4096]{1,0:T(8,128)(2,1)} %param.13) | copy-start | bytes 393220

commit v5 on v4

--- a/solution.py
+++ b/solution.py
@@ -17,8 +17,8 @@
 N_DC = NX * NY * NC
 PADDED = 8
 SLOT_TOTAL = N_DC * PADDED
-CHUNK_SLABS = 4
-CHUNK = CHUNK_SLABS * TOK
+PIECE = TOK // NX
+CHUNK = NY * PIECE
 PART = HEAD + 16
 LOG2E = 1.4426950408889634
 SCALE2 = HEAD**-0.5 * LOG2E
@@ -40,15 +40,8 @@
         q_all[s] = q_ref[...]
     x, y, c = (lax.axis_index(a) for a in ("x", "y", "c"))
 
-    def empty(xs, carry):
-        out_ref[xs, :HEAD, :] = jnp.zeros((HEAD, QROWS), jnp.bfloat16)
-        rows = lax.broadcasted_iota(jnp.int32, (PART - HEAD, QROWS), 0)
-        out_ref[xs, HEAD:, :] = jnp.where(rows == 0, FLOOR, 0.0).astype(jnp.bfloat16)
-        return carry
-
-    lax.fori_loop(0, x, empty, 0)
-
-    def slab(xs, carry):
+    def slab(turn, carry):
+        xs = lax.rem(x + turn, NX)
         p0 = (xs * (NY * NC) + y * NC + c) * TOK
         last = p0 + TOK - 1
         lane = lax.broadcasted_iota(jnp.int32, (1, QROWS), 1)
@@ -62,8 +55,8 @@
             start = jnp.where(pos >= end, end, start)
             first_start = jnp.where(p0 >= end, end, first_start)
             last_start = jnp.where(last >= end, end, last_start)
-        q_s[:TOK, :] = q_all[xs - x, :, :HEAD]
-        q_s[TOK:, :] = q_all[xs - x, :, HEAD:]
+        q_s[:TOK, :] = q_all[turn, :, :HEAD]
+        q_s[TOK:, :] = q_all[turn, :, HEAD:]
         m_s[...] = jnp.full((1, QROWS), FLOOR, jnp.float32)
         l_s[...] = jnp.zeros((1, QROWS), jnp.float32)
         acc_s[...] = jnp.zeros((HEAD, QROWS), jnp.float32)
@@ -71,8 +64,8 @@
         for ref, core in ((own_ref, c), (peer_ref, 1 - c)):
 
             def chunk(ch, carry, ref=ref, core=core):
-                low = ((x * NY + ch * CHUNK_SLABS) * NC + core) * TOK
-                high = low + (CHUNK_SLABS - 1) * NC * TOK + TOK - 1
+                low = (ch * NY * NC + core) * TOK + x * PIECE
+                high = low + (NY - 1) * NC * TOK + PIECE - 1
                 rows = pl.ds(pl.multiple_of(ch * CHUNK, CHUNK), CHUNK)
 
                 def update(masked):
@@ -83,9 +76,9 @@
                     if masked:
                         at = lax.broadcasted_iota(jnp.int32, (CHUNK, 1), 0)
                         slab_at = jnp.zeros((CHUNK, 1), jnp.int32)
-                        for n in range(1, CHUNK_SLABS):
-                            slab_at += (at >= n * TOK).astype(jnp.int32)
-                        key_pos = low + at + slab_at * ((NC - 1) * TOK)
+                        for n in range(1, NY):
+                            slab_at += (at >= n * PIECE).astype(jnp.int32)
+                        key_pos = low + at + slab_at * (NC * TOK - PIECE)
                         s = jnp.where((key_pos >= start) & (key_pos <= pos), s, NEG)
                     m_old = m_s[...]
                     m_new = jnp.maximum(m_old, round_up(jnp.max(s, axis=0, keepdims=True)))
@@ -113,7 +106,7 @@
 
                 return carry
 
-            lax.fori_loop(0, NY // CHUNK_SLABS, chunk, 0)
+            lax.fori_loop(0, NX, chunk, 0)
 
         out_ref[xs, :HEAD, :] = acc_s[...].astype(jnp.bfloat16)
         total = l_s[...]
@@ -123,7 +116,7 @@
         out_ref[xs, HEAD:, :] = stats.astype(jnp.bfloat16)
         return carry
 
-    lax.fori_loop(x, NX, slab, 0)
+    lax.fori_loop(0, NX, slab, 0)
 
 
 def place_kernel(row_ref, col_ref, out_ref):
@@ -206,9 +199,10 @@
 
 
 def prepare_kernel(head, k_ref, v_ref, kv_ref):
-    for i in range(NY):
-        kv_ref[i, :, :HEAD] = k_ref[...]
-        kv_ref[i, :, HEAD:] = v_ref[...]
+    for i in range(NX * NY):
+        rows = pl.ds(i // NY * PIECE, PIECE)
+        kv_ref[i, :, :HEAD] = k_ref[rows, :]
+        kv_ref[i, :, HEAD:] = v_ref[rows, :]
 
 
 def vmem():
@@ -237,6 +231,9 @@
     tp = lax.axis_index("q") * NJ + lax.axis_index("j")
     dc = (x * NY + y) * NC + c
     peer = [(0, 1), (1, 0)]
+
+    def turn(size, step):
+        return [(i, (i + step) % size) for i in range(size)]
 
     around = [
         (k * NJ + i, k * NJ + (i + 1 + k) % NJ) for k in range(NC) for i in range(NJ)
@@ -245,17 +242,19 @@
     block = pl.BlockSpec((TOK, HEAD), lambda i, head: (0, head[0]))
     kv = pl.pallas_call(
         prepare_kernel,
-        out_shape=jax.ShapeDtypeStruct((NY, TOK, COLS), jnp.bfloat16),
+        out_shape=jax.ShapeDtypeStruct((NX * NY, PIECE, COLS), jnp.bfloat16),
         grid_spec=pltpu.PrefetchScalarGridSpec(
             num_scalar_prefetch=1,
             grid=(1,),
             in_specs=[block, block],
-            out_specs=pl.BlockSpec((NY, TOK, COLS), lambda i, head: (0, 0, 0)),
+            out_specs=pl.BlockSpec((NX * NY, PIECE, COLS), lambda i, head: (0, 0, 0)),
         ),
         name="prepare",
     )((tp * HEADS_HERE // GROUP).reshape(1).astype(jnp.int32), keys, values)
-    own = lax.all_to_all(kv, "y", 0, 0, tiled=True).reshape(NY * TOK, COLS)
-    moved = [lax.ppermute(queries, "x", [(i, i - s) for i in range(s, NX)]) for s in range(1, NX)]
+    own = lax.all_to_all(kv, ("x", "y"), 0, 0, tiled=True).reshape(NY * TOK, COLS)
+    moved = [
+        lax.ppermute(queries, "x", turn(NX, NX - s)) for s in range(1, NX)
+    ]
     other = lax.ppermute(own, "c", peer)
 
     partial = kernel(

time: 140 us -> 151 us (1.079)
  Pallas kernels: 12.7 us -> 22.1 us
  starting transfers between devices: 41.8 us -> 44.7 us
  waiting for transfers between devices: 36.1 us -> 34.4 us
    pallas_call x1, Pallas kernels: 2.53 us -> 12 us  [per_device(): kernel(attend_kernel, out_here(NX, PART, QROWS), [smem()] + [vmem()] * (N...]
    all_to_all x1, starting transfers between devices: 12.9 us -> 5.72 us  [per_device(): parts = lax.all_to_all(partial, 'x', 0, 0, tiled=True)]
    all_to_all x1, starting transfers between devices: 7.23 us -> 13.3 us  [per_device(): lax.all_to_all(kv, ('x', 'y'), 0, 0, tiled=True).reshape(NY * TOK, COLS)]
    ppermute x3, starting transfers between devices: 6.49 us -> 10.1 us  [per_device(): moved = [lax.ppermute(queries, 'x', turn(NX, NX - s)) for s in range(1, NX)]]
    all_to_all x1, waiting for transfers between devices: 18.8 us -> 15.9 us  [per_device(): lax.all_to_all(kv, ('x', 'y'), 0, 0, tiled=True).reshape(NY * TOK, COLS)]
    all_to_all x1, starting transfers between devices: 7.04 us -> 9.44 us  [per_device(): incoming = lax.all_to_all(outgoing, ('x', 'y', 'c'), 0, 0, tiled=True)]
    ppermute x1, starting transfers between devices: 4.27 us -> 1.92 us  [per_device(): turned = lax.ppermute(out_weight, ('c', 'j'), around)]
  transfers between devices with their start and end apart: 9 -> 9, of which waited for: 5 -> 5; matrix products, arithmetic and copies ran while one was open for 1% -> 1% of each run, Pallas kernels for 4% -> 10%
where the time goes in v5:
time: 151 us; the launch traced here: 150 us
  blocking collectives  46.6 us (31%)
  starting transfers between devices  44.7 us (30%)
  waiting for transfers between devices  34.4 us (23%)
  Pallas kernels  22.1 us (15%)
  local copies, waits for them, and re-layouts  1.57 us (1%)
    all_to_all x1, blocking collectives, per_device(): blocks = lax.all_to_all(projected, 'q', 0, 0, tiled=True)  36.3 us
    all_to_all x1, waiting for transfers between devices, per_device(): lax.all_to_all(kv, ('x', 'y'), 0, 0, tiled=True).reshape(NY * TOK, COLS)  15.9 us
    all_to_all x1, starting transfers between devices, per_device(): lax.all_to_all(kv, ('x', 'y'), 0, 0, tiled=True).reshape(NY * TOK, COLS)  13.3 us
    pallas_call x1, Pallas kernels, per_device(): kernel(attend_kernel, out_here(NX, PART, QROWS), [smem()] + [vmem()] * (N...  12 us
    all_to_all x1, blocking collectives, per_device(): lax.all_to_all(owned.reshape(NJ, TOK // NJ, COLS), 'j', 0, 0, tiled=True)  10.3 us
    ppermute x3, starting transfers between devices, per_device(): moved = [lax.ppermute(queries, 'x', turn(NX, NX - s)) for s in range(1, NX)]  10.1 us
    all_to_all x1, waiting for transfers between devices, per_device(): incoming = lax.all_to_all(outgoing, ('x', 'y', 'c'), 0, 0, tiled=True)  9.58 us
    all_to_all x1, starting transfers between devices, per_device(): incoming = lax.all_to_all(outgoing, ('x', 'y', 'c'), 0, 0, tiled=True)  9.44 us
  transfers between devices with their start and end apart: 9, of which 5 were waited for; matrix products, arithmetic and copies ran while one was open for 1% of the time, Pallas kernels for 10%

profile of v5, /device:TPU:6, one launch (start us, length us, event | category | flops | bytes accessed | tf_op | source)
XLA Modules:
  0.0 150.2 jit_solution(12941013268039499675)
XLA Ops:
  0.0 1.9 %prepare.1 = bf16[32,48,256]{2,1,0:T(8,128)(2,1)} custom-call(s32[1]{0:T(128)} %bitcast.2.head, bf16[192,768]{1,0:T(8,128)(2,1)} %k_ref.1, bf16[192,768]{1,0:T(8,128)(2,1)} %v_ref.1), custom_call_target="tpu_custom_call" | custom-call | tf_op jit(solution)/shard_map/prepare/pallas_call | solution.py:243
  1.9 13.3 %all-to-all-start = ((bf16[32,48,256]{2,1,0:T(8,128)(2,1)}), bf16[32,48,256]{2,1,0:T(8,128)(2,1)S(1)}, u32[]{:S(2)}, u32[]{:S(2)}) async-start(bf16[32,48,256]{2,1,0:T(8,128)(2,1)} %prepare.1), calls=%async_computation | async-start | bytes 1572864 | tf_op jit(solution)/shard_map/all_to_all | solution.py:254
  15.2 1.9 %collective-permute-start.4 = (bf16[256,4096]{1,0:T(8,128)(2,1)}, bf16[256,4096]{1,0:T(8,128)(2,1)}, u32[]{:S(2)}, u32[]{:S(2)}) collective-permute-start(bf16[256,4096]{1,0:T(8,128)(2,1)} %w0.1), channel_id=1, source_target_pairs={{0,1},{1,2},{2,0},{12,14},{13,12},{14,13},{3,4},{4,5},{5,3},{15,17... | collective-permute-start | bytes 6291464 | tf_op jit(solution)/shard_map/ppermute | solution.py:241
  17.1 15.9 %all-to-all-done = bf16[32,48,256]{2,1,0:T(8,128)(2,1)S(1)} async-done(((bf16[32,48,256]{2,1,0:T(8,128)(2,1)}), bf16[32,48,256]{2,1,0:T(8,128)(2,1)S(1)}, u32[]{:S(2)}, u32[]{:S(2)}) %all-to-all-start) | async-done | bytes 786464 | tf_op jit(solution)/shard_map/all_to_all | solution.py:254
  33.0 1.9 %collective-permute-start.3 = (bf16[1536,256]{1,0:T(8,128)(2,1)S(1)}, bf16[1536,256]{1,0:T(8,128)(2,1)S(1)}, u32[]{:S(2)}, u32[]{:S(2)}) collective-permute-start(bf16[1536,256]{1,0:T(8,128)(2,1)S(1)} %bitcast.27), channel_id=1, source_target_pairs={{0,12},{12,0},{1,13},{13,1},{2,14},{14,2},{3,15},{15,3},{4,16},{16... | collective-permute-start | bytes 2359304 | tf_op jit(solution)/shard_map/ppermute | solution.py:258
  34.9 3.1 %collective-permute-start.1 = (bf16[192,256]{1,0:T(8,128)(2,1)S(1)}, bf16[192,256]{1,0:T(8,128)(2,1)S(1)}, u32[]{:S(2)}, u32[]{:S(2)}) collective-permute-start(bf16[192,256]{1,0:T(8,128)(2,1)S(1)} %copy-done), channel_id=1, source_target_pairs={{0,384},{192,576},{384,0},{576,192},{1,385},{193,577},{385,1},{577... | collective-permute-start | bytes 294920 | tf_op jit(solution)/shard_map/ppermute | solution.py:256
  38.0 4.1 %collective-permute-start = (bf16[192,256]{1,0:T(8,128)(2,1)S(1)}, bf16[192,256]{1,0:T(8,128)(2,1)S(1)}, u32[]{:S(2)}, u32[]{:S(2)}) collective-permute-start(bf16[192,256]{1,0:T(8,128)(2,1)S(1)} %copy-done), channel_id=1, source_target_pairs={{0,576},{192,0},{384,192},{576,384},{1,577},{193,1},{385,193},{577... | collective-permute-start | bytes 294920 | tf_op jit(solution)/shard_map/ppermute | solution.py:256
  42.1 3.0 %collective-permute-start.2 = (bf16[192,256]{1,0:T(8,128)(2,1)S(1)}, bf16[192,256]{1,0:T(8,128)(2,1)S(1)}, u32[]{:S(2)}, u32[]{:S(2)}) collective-permute-start(bf16[192,256]{1,0:T(8,128)(2,1)S(1)} %copy-done), channel_id=1, source_target_pairs={{0,192},{192,384},{384,576},{576,0},{1,193},{193,385},{385,577},{5... | collective-permute-start | bytes 294920 | tf_op jit(solution)/shard_map/ppermute | solution.py:256
  45.1 0.0 collective-permute-done.1.refs_2_
  45.1 0.9 collective-permute-done.refs_1_
  46.0 2.6 %collective-permute-done.2.refs_3_ = bf16[192,256]{1,0:T(8,128)(2,1)S(1)} collective-permute-done((bf16[192,256]{1,0:T(8,128)(2,1)S(1)}, bf16[192,256]{1,0:T(8,128)(2,1)S(1)}, u32[]{:S(2)}, u32[]{:S(2)}) %collective-permute-start.2) | collective-permute-done | bytes 98336 | tf_op jit(solution)/shard_map/ppermute | solution.py:256
  48.6 0.0 collective-permute-done.3.refs_5_
  48.6 12.0 %shard_map.75 = bf16[4,144,384]{2,1,0:T(8,128)(2,1)} custom-call(s32[24]{0:T(128)} %lengths.1, bf16[192,256]{1,0:T(8,128)(2,1)S(1)} %copy-done, bf16[192,256]{1,0:T(8,128)(2,1)S(1)} %collective-permute-done.refs_1_, bf16[192,256]{1,0:T(8,128)(2,1)S(1)} %collective-permute-done.1.refs_2_, bf16[192,256]{1,0:T(8,128)(2,1)S(1)} %collective-permute-done.2.refs_3_, ...), custom_call_target="tpu_custom_call" | custom-call | tf_op jit(solution)/shard_map/pallas_call | solution.py:260
  60.6 5.7 %all-to-all-start.1 = ((bf16[4,144,384]{2,1,0:T(8,128)(2,1)}), bf16[4,144,384]{2,1,0:T(8,128)(2,1)S(1)}, u32[]{:S(2)}, u32[]{:S(2)}) async-start(bf16[4,144,384]{2,1,0:T(8,128)(2,1)} %shard_map.75), calls=%async_computation.1 | async-start | bytes 884736 | tf_op jit(solution)/shard_map/all_to_all | solution.py:272
  66.3 0.1 dynamic_slice.3
  66.3 0.8 copy.8.col_ref
  67.1 1.1 shard_map.74.placement
  68.2 5.4 %all-to-all-done.1.part_ref = bf16[4,144,384]{2,1,0:T(8,128)(2,1)S(1)} async-done(((bf16[4,144,384]{2,1,0:T(8,128)(2,1)}), bf16[4,144,384]{2,1,0:T(8,128)(2,1)S(1)}, u32[]{:S(2)}, u32[]{:S(2)}) %all-to-all-start.1) | async-done | bytes 442400 | tf_op jit(solution)/shard_map/all_to_all | solution.py:272
  73.6 1.1 shard_map.76
  74.7 0.0 collective-permute-done.4.w1
  74.7 2.3 %collective-permute-start.5 = (bf16[256,4096]{1,0:T(8,128)(2,1)}, bf16[256,4096]{1,0:T(8,128)(2,1)S(1)}, u32[]{:S(2)}, u32[]{:S(2)}) collective-permute-start(bf16[256,4096]{1,0:T(8,128)(2,1)} %collective-permute-done.4.w1), channel_id=1, source_target_pairs={{0,12},{12,0},{1,13},{13,1},{2,14},{14,2},{3,15},{15,3},{4,16},{16... | collective-permute-start | bytes 6291464 | tf_op jit(solution)/shard_map/ppermute | solution.py:290
  77.0 9.4 %all-to-all-start.2 = ((bf16[64,8,256]{2,1,0:T(8,128)(2,1)}), bf16[64,8,256]{2,1,0:T(8,128)(2,1)S(1)}, u32[]{:S(2)}, u32[]{:S(2)}) async-start(bf16[64,8,256]{2,1,0:T(8,128)(2,1)} %bitcast.4), calls=%async_computation.2 | async-start | bytes 524288 | tf_op jit(solution)/shard_map/all_to_all | solution.py:282
  86.5 0.7 reshape.32.owner_ref
  87.2 1.2 shard_map.73.chooser
  88.5 9.6 %all-to-all-done.2 = bf16[64,8,256]{2,1,0:T(8,128)(2,1)S(1)} async-done(((bf16[64,8,256]{2,1,0:T(8,128)(2,1)}), bf16[64,8,256]{2,1,0:T(8,128)(2,1)S(1)}, u32[]{:S(2)}, u32[]{:S(2)}) %all-to-all-start.2) | async-done | bytes 262176 | tf_op jit(solution)/shard_map/all_to_all | solution.py:282
  98.0 0.2 shard_map.77
  98.2 0.0 collective-permute-done.5.w2
  98.2 10.3 %all_to_all.25.x_ref = bf16[3,64,256]{2,1,0:T(8,128)(2,1)S(1)} all-to-all(bf16[3,64,256]{2,1,0:T(8,128)(2,1)S(1)} %bitcast.30), channel_id=1, replica_groups=mesh['x'=4,'y'=8,'c'=2,'q'=4,'j'=3] {'j'}, dimensions={0} | all-to-all | bytes 196608 | tf_op jit(solution)/shard_map/all_to_all | solution.py:292
  108.5 4.6 %project.1 = bf16[4,16,4096]{2,1,0:T(8,128)(2,1)} custom-call(bf16[3,64,256]{2,1,0:T(8,128)(2,1)S(1)} %all_to_all.25.x_ref, bf16[256,4096]{1,0:T(8,128)(2,1)} %w0.1, bf16[256,4096]{1,0:T(8,128)(2,1)} %collective-permute-done.4.w1, bf16[256,4096]{1,0:T(8,128)(2,1)S(1)} %collective-permute-done.5.w2), custom_call_target="tpu_custom_call" | custom-call | tf_op jit(solution)/shard_map/project/pallas_call | solution.py:296
  113.1 36.3 %all_to_all.26 = bf16[4,16,4096]{2,1,0:T(8,128)(2,1)S(1)} all-to-all(bf16[4,16,4096]{2,1,0:T(8,128)(2,1)} %project.1), channel_id=1, replica_groups=mesh['x'=4,'y'=8,'c'=2,'q'=4,'j'=3] {'q'}, dimensions={0} | all-to-all | bytes 1048576 | tf_op jit(solution)/shard_map/all_to_all | solution.py:304
  149.4 0.0 copy-done.1
  149.4 0.7 fusion
  (7 shorter events, 0.0 us)
Async XLA Ops:
  0.0 34.9 %copy-start = (bf16[192,256]{1,0:T(8,128)(2,1)S(1)}, bf16[192,256]{1,0:T(8,128)(2,1)}, u32[]{:S(2)}) copy-start(bf16[192,256]{1,0:T(8,128)(2,1)} %refs_0_.1) | copy-start | bytes 294916
  1.9 64.4 %copy-start.2 = (s32[12288]{0:T(1024)S(1)}, s32[12288]{0:T(1024)}, u32[]{:S(2)}) copy-start(s32[12288]{0:T(1024)} %param.11) | copy-start | bytes 147460
  1.9 31.1 %all-to-all-start = ((bf16[32,48,256]{2,1,0:T(8,128)(2,1)}), bf16[32,48,256]{2,1,0:T(8,128)(2,1)S(1)}, u32[]{:S(2)}, u32[]{:S(2)}) async-start(bf16[32,48,256]{2,1,0:T(8,128)(2,1)} %prepare.1), calls=%async_computation | async-start | bytes 1572864 | tf_op jit(solution)/shard_map/all_to_all | solution.py:254
  15.2 59.6 %collective-permute-start.4 = (bf16[256,4096]{1,0:T(8,128)(2,1)}, bf16[256,4096]{1,0:T(8,128)(2,1)}, u32[]{:S(2)}, u32[]{:S(2)}) collective-permute-start(bf16[256,4096]{1,0:T(8,128)(2,1)} %w0.1), channel_id=1, source_target_pairs={{0,1},{1,2},{2,0},{12,14},{13,12},{14,13},{3,4},{4,5},{5,3},{15,17... | collective-permute-start | bytes 6291464 | tf_op jit(solution)/shard_map/ppermute | solution.py:241
  33.0 15.6 %collective-permute-start.3 = (bf16[1536,256]{1,0:T(8,128)(2,1)S(1)}, bf16[1536,256]{1,0:T(8,128)(2,1)S(1)}, u32[]{:S(2)}, u32[]{:S(2)}) collective-permute-start(bf16[1536,256]{1,0:T(8,128)(2,1)S(1)} %bitcast.27), channel_id=1, source_target_pairs={{0,12},{12,0},{1,13},{13,1},{2,14},{14,2},{3,15},{15,3},{4,16},{16... | collective-permute-start | bytes 2359304 | tf_op jit(solution)/shard_map/ppermute | solution.py:258
  34.9 10.1 %collective-permute-start.1 = (bf16[192,256]{1,0:T(8,128)(2,1)S(1)}, bf16[192,256]{1,0:T(8,128)(2,1)S(1)}, u32[]{:S(2)}, u32[]{:S(2)}) collective-permute-start(bf16[192,256]{1,0:T(8,128)(2,1)S(1)} %copy-done), channel_id=1, source_target_pairs={{0,384},{192,576},{384,0},{576,192},{1,385},{193,577},{385,1},{577... | collective-permute-start | bytes 294920 | tf_op jit(solution)/shard_map/ppermute | solution.py:256
  38.0 8.0 %collective-permute-start = (bf16[192,256]{1,0:T(8,128)(2,1)S(1)}, bf16[192,256]{1,0:T(8,128)(2,1)S(1)}, u32[]{:S(2)}, u32[]{:S(2)}) collective-permute-start(bf16[192,256]{1,0:T(8,128)(2,1)S(1)} %copy-done), channel_id=1, source_target_pairs={{0,576},{192,0},{384,192},{576,384},{1,577},{193,1},{385,193},{577... | collective-permute-start | bytes 294920 | tf_op jit(solution)/shard_map/ppermute | solution.py:256
  42.1 6.5 %collective-permute-start.2 = (bf16[192,256]{1,0:T(8,128)(2,1)S(1)}, bf16[192,256]{1,0:T(8,128)(2,1)S(1)}, u32[]{:S(2)}, u32[]{:S(2)}) collective-permute-start(bf16[192,256]{1,0:T(8,128)(2,1)S(1)} %copy-done), channel_id=1, source_target_pairs={{0,192},{192,384},{384,576},{576,0},{1,193},{193,385},{385,577},{5... | collective-permute-start | bytes 294920 | tf_op jit(solution)/shard_map/ppermute | solution.py:256
  60.6 13.1 %all-to-all-start.1 = ((bf16[4,144,384]{2,1,0:T(8,128)(2,1)}), bf16[4,144,384]{2,1,0:T(8,128)(2,1)S(1)}, u32[]{:S(2)}, u32[]{:S(2)}) async-start(bf16[4,144,384]{2,1,0:T(8,128)(2,1)} %shard_map.75), calls=%async_computation.1 | async-start | bytes 884736 | tf_op jit(solution)/shard_map/all_to_all | solution.py:272
  66.3 0.8 copy-start.3
  74.7 23.5 %collective-permute-start.5 = (bf16[256,4096]{1,0:T(8,128)(2,1)}, bf16[256,4096]{1,0:T(8,128)(2,1)S(1)}, u32[]{:S(2)}, u32[]{:S(2)}) collective-permute-start(bf16[256,4096]{1,0:T(8,128)(2,1)} %collective-permute-done.4.w1), channel_id=1, source_target_pairs={{0,12},{12,0},{1,13},{13,1},{2,14},{14,2},{3,15},{15,3},{4,16},{16... | collective-permute-start | bytes 6291464 | tf_op jit(solution)/shard_map/ppermute | solution.py:290
  77.0 21.0 %all-to-all-start.2 = ((bf16[64,8,256]{2,1,0:T(8,128)(2,1)}), bf16[64,8,256]{2,1,0:T(8,128)(2,1)S(1)}, u32[]{:S(2)}, u32[]{:S(2)}) async-start(bf16[64,8,256]{2,1,0:T(8,128)(2,1)} %bitcast.4), calls=%async_computation.2 | async-start | bytes 524288 | tf_op jit(solution)/shard_map/all_to_all | solution.py:282
  108.5 40.9 %copy-start.1 = (bf16[16,4096]{1,0:T(8,128)(2,1)S(1)}, bf16[16,4096]{1,0:T(8,128)(2,1)}, u32[]{:S(2)}) copy-start(bf16[16,4096]{1,0:T(8,128)(2,1)} %param.13) | copy-start | bytes 393220

commit v6 on v4

--- a/solution.py
+++ b/solution.py
@@ -68,14 +68,14 @@
         l_s[...] = jnp.zeros((1, QROWS), jnp.float32)
         acc_s[...] = jnp.zeros((HEAD, QROWS), jnp.float32)
 
-        for ref, core in ((own_ref, c), (peer_ref, 1 - c)):
-
-            def chunk(ch, carry, ref=ref, core=core):
-                low = ((x * NY + ch * CHUNK_SLABS) * NC + core) * TOK
-                high = low + (CHUNK_SLABS - 1) * NC * TOK + TOK - 1
-                rows = pl.ds(pl.multiple_of(ch * CHUNK, CHUNK), CHUNK)
-
-                def update(masked):
+        def chunk(ch, carry):
+            low = (x * NY + ch * CHUNK_SLABS) * NC * TOK
+            high = low + CHUNK_SLABS * NC * TOK - 1
+            rows = pl.ds(pl.multiple_of(ch * CHUNK, CHUNK), CHUNK)
+
+            def update(masked):
+                pieces = []
+                for ref, core in ((own_ref, c), (peer_ref, 1 - c)):
                     s = lax.dot_general(
                         ref[rows, :HEAD], q_s[...], NT, preferred_element_type=jnp.float32
                     )
@@ -85,35 +85,42 @@
                         slab_at = jnp.zeros((CHUNK, 1), jnp.int32)
                         for n in range(1, CHUNK_SLABS):
                             slab_at += (at >= n * TOK).astype(jnp.int32)
-                        key_pos = low + at + slab_at * ((NC - 1) * TOK)
+                        key_pos = low + core * TOK + at + slab_at * ((NC - 1) * TOK)
                         s = jnp.where((key_pos >= start) & (key_pos <= pos), s, NEG)
-                    m_old = m_s[...]
-                    m_new = jnp.maximum(m_old, round_up(jnp.max(s, axis=0, keepdims=True)))
+                    pieces.append(s)
+                m_old = m_s[...]
+                top = [jnp.max(s, axis=0, keepdims=True) for s in pieces]
+                m_new = jnp.maximum(m_old, round_up(jnp.maximum(top[0], top[1])))
+                fix = jnp.exp2(m_old - m_new)
+                m_s[...] = m_new
+                total = l_s[...] * fix
+                mixed = acc_s[...] * fix
+                for s, ref in zip(pieces, (own_ref, peer_ref)):
                     w = jnp.exp2(s - m_new)
-                    fix = jnp.exp2(m_old - m_new)
-                    m_s[...] = m_new
-                    l_s[...] = l_s[...] * fix + jnp.sum(w, axis=0, keepdims=True)
-                    acc_s[...] = acc_s[...] * fix + lax.dot_general(
+                    total = total + jnp.sum(w, axis=0, keepdims=True)
+                    mixed = mixed + lax.dot_general(
                         ref[rows, HEAD:],
                         w.astype(jnp.bfloat16),
                         TN,
                         preferred_element_type=jnp.float32,
                     )
-
-                needed = (low <= last) & (high >= first_start)
-                whole = (high <= p0) & (low >= last_start)
-
-                @pl.when(needed & whole)
-                def _():
-                    update(False)
-
-                @pl.when(needed & jnp.logical_not(whole))
-                def _():
-                    update(True)
-
-                return carry
-
-            lax.fori_loop(0, NY // CHUNK_SLABS, chunk, 0)
+                l_s[...] = total
+                acc_s[...] = mixed
+
+            needed = (low <= last) & (high >= first_start)
+            whole = (high <= p0) & (low >= last_start)
+
+            @pl.when(needed & whole)
+            def _():
+                update(False)
+
+            @pl.when(needed & jnp.logical_not(whole))
+            def _():
+                update(True)
+
+            return carry
+
+        lax.fori_loop(0, NY // CHUNK_SLABS, chunk, 0)
 
         out_ref[xs, :HEAD, :] = acc_s[...].astype(jnp.bfloat16)
         total = l_s[...]

time: 140 us -> 138 us (0.986)
  starting transfers between devices: 41.8 us -> 39.9 us
  transfers between devices with their start and end apart: 9 -> 9, of which waited for: 5 -> 5; matrix products, arithmetic and copies ran while one was open for 1% -> 1% of each run, Pallas kernels for 4% -> 5%
where the time goes in v6:
time: 138 us; the launch traced here: 137 us
  blocking collectives  46.5 us (34%)
  starting transfers between devices  39.9 us (29%)
  waiting for transfers between devices  35.2 us (26%)
  Pallas kernels  13.1 us (9%)
  local copies, waits for them, and re-layouts  1.57 us (1%)
    all_to_all x1, blocking collectives, per_device(): blocks = lax.all_to_all(projected, 'q', 0, 0, tiled=True)  36.2 us
    all_to_all x1, waiting for transfers between devices, per_device(): own = lax.all_to_all(kv, 'y', 0, 0, tiled=True).reshape(NY * TOK, COLS)  18.8 us
    all_to_all x1, starting transfers between devices, per_device(): parts = lax.all_to_all(partial, 'x', 0, 0, tiled=True)  11.7 us
    all_to_all x1, blocking collectives, per_device(): lax.all_to_all(owned.reshape(NJ, TOK // NJ, COLS), 'j', 0, 0, tiled=True)  10.4 us
    all_to_all x1, waiting for transfers between devices, per_device(): incoming = lax.all_to_all(outgoing, ('x', 'y', 'c'), 0, 0, tiled=True)  9.58 us
    all_to_all x1, starting transfers between devices, per_device(): own = lax.all_to_all(kv, 'y', 0, 0, tiled=True).reshape(NY * TOK, COLS)  7.23 us
    ppermute x3, starting transfers between devices, per_device(): lax.ppermute(queries, 'x', [(i, i - s) for i in range(s, NX)])  6.49 us
    all_to_all x1, starting transfers between devices, per_device(): incoming = lax.all_to_all(outgoing, ('x', 'y', 'c'), 0, 0, tiled=True)  6.45 us
  transfers between devices with their start and end apart: 9, of which 5 were waited for; matrix products, arithmetic and copies ran while one was open for 1% of the time, Pallas kernels for 5%

profile of v6, /device:TPU:6, one launch (start us, length us, event | category | flops | bytes accessed | tf_op | source)
XLA Modules:
  0.0 137.2 jit_solution(330801388181509445)
XLA Ops:
  0.0 1.9 %prepare.1 = bf16[8,192,256]{2,1,0:T(8,128)(2,1)} custom-call(s32[1]{0:T(128)} %bitcast.2.head, bf16[192,768]{1,0:T(8,128)(2,1)} %k_ref.1, bf16[192,768]{1,0:T(8,128)(2,1)} %v_ref.1), custom_call_target="tpu_custom_call" | custom-call | tf_op jit(solution)/shard_map/prepare/pallas_call | solution.py:253
  1.9 7.2 %all-to-all-start = ((bf16[8,192,256]{2,1,0:T(8,128)(2,1)}), bf16[8,192,256]{2,1,0:T(8,128)(2,1)S(1)}, u32[]{:S(2)}, u32[]{:S(2)}) async-start(bf16[8,192,256]{2,1,0:T(8,128)(2,1)} %prepare.1), calls=%async_computation | async-start | bytes 1572864 | tf_op jit(solution)/shard_map/all_to_all | solution.py:264
  9.1 4.3 %collective-permute-start.4 = (bf16[256,4096]{1,0:T(8,128)(2,1)}, bf16[256,4096]{1,0:T(8,128)(2,1)}, u32[]{:S(2)}, u32[]{:S(2)}) collective-permute-start(bf16[256,4096]{1,0:T(8,128)(2,1)} %w0.1), channel_id=1, source_target_pairs={{0,1},{1,2},{2,0},{12,14},{13,12},{14,13},{3,4},{4,5},{5,3},{15,17... | collective-permute-start | bytes 6291464 | tf_op jit(solution)/shard_map/ppermute | solution.py:251
  13.4 18.8 %all-to-all-done = bf16[8,192,256]{2,1,0:T(8,128)(2,1)S(1)} async-done(((bf16[8,192,256]{2,1,0:T(8,128)(2,1)}), bf16[8,192,256]{2,1,0:T(8,128)(2,1)S(1)}, u32[]{:S(2)}, u32[]{:S(2)}) %all-to-all-start) | async-done | bytes 786464 | tf_op jit(solution)/shard_map/all_to_all | solution.py:264
  32.2 1.9 %collective-permute-start.3 = (bf16[1536,256]{1,0:T(8,128)(2,1)S(1)}, bf16[1536,256]{1,0:T(8,128)(2,1)S(1)}, u32[]{:S(2)}, u32[]{:S(2)}) collective-permute-start(bf16[1536,256]{1,0:T(8,128)(2,1)S(1)} %bitcast.27), channel_id=1, source_target_pairs={{0,12},{12,0},{1,13},{13,1},{2,14},{14,2},{3,15},{15,3},{4,16},{16... | collective-permute-start | bytes 2359304 | tf_op jit(solution)/shard_map/ppermute | solution.py:266
  34.1 3.3 %collective-permute-start.1 = (bf16[192,256]{1,0:T(8,128)(2,1)S(1)}, bf16[192,256]{1,0:T(8,128)(2,1)S(1)}, u32[]{:S(2)}, u32[]{:S(2)}) collective-permute-start(bf16[192,256]{1,0:T(8,128)(2,1)S(1)} %copy-done), channel_id=1, source_target_pairs={{384,0},{576,192},{385,1},{577,193},{386,2},{578,194},{387,3},{579... | collective-permute-start | bytes 294920 | tf_op jit(solution)/shard_map/ppermute | solution.py:265
  37.5 1.9 %collective-permute-start = (bf16[192,256]{1,0:T(8,128)(2,1)S(1)}, bf16[192,256]{1,0:T(8,128)(2,1)S(1)}, u32[]{:S(2)}, u32[]{:S(2)}) collective-permute-start(bf16[192,256]{1,0:T(8,128)(2,1)S(1)} %copy-done), channel_id=1, source_target_pairs={{192,0},{384,192},{576,384},{193,1},{385,193},{577,385},{194,2},{3... | collective-permute-start | bytes 294920 | tf_op jit(solution)/shard_map/ppermute | solution.py:265
  39.3 1.3 collective-permute-start.2
  40.7 0.0 collective-permute-done.1.refs_2_
  40.7 1.6 %collective-permute-done.refs_1_ = bf16[192,256]{1,0:T(8,128)(2,1)S(1)} collective-permute-done((bf16[192,256]{1,0:T(8,128)(2,1)S(1)}, bf16[192,256]{1,0:T(8,128)(2,1)S(1)}, u32[]{:S(2)}, u32[]{:S(2)}) %collective-permute-start) | collective-permute-done | bytes 98336 | tf_op jit(solution)/shard_map/ppermute | solution.py:265
  42.3 0.8 collective-permute-done.2.refs_3_
  43.1 0.0 collective-permute-done.3.refs_5_
  43.1 3.0 %shard_map.75 = bf16[4,144,384]{2,1,0:T(8,128)(2,1)} custom-call(s32[24]{0:T(128)} %lengths.1, bf16[192,256]{1,0:T(8,128)(2,1)S(1)} %copy-done, bf16[192,256]{1,0:T(8,128)(2,1)S(1)} %collective-permute-done.refs_1_, bf16[192,256]{1,0:T(8,128)(2,1)S(1)} %collective-permute-done.1.refs_2_, bf16[192,256]{1,0:T(8,128)(2,1)S(1)} %collective-permute-done.2.refs_3_, ...), custom_call_target="tpu_custom_call" | custom-call | tf_op jit(solution)/shard_map/pallas_call | solution.py:268
  46.1 11.7 %all-to-all-start.1 = ((bf16[4,144,384]{2,1,0:T(8,128)(2,1)}), bf16[4,144,384]{2,1,0:T(8,128)(2,1)S(1)}, u32[]{:S(2)}, u32[]{:S(2)}) async-start(bf16[4,144,384]{2,1,0:T(8,128)(2,1)} %shard_map.75), calls=%async_computation.1 | async-start | bytes 884736 | tf_op jit(solution)/shard_map/all_to_all | solution.py:280
  57.8 0.1 dynamic_slice.3
  57.8 0.8 copy.8.col_ref
  58.6 1.1 shard_map.74.placement
  59.7 4.4 %all-to-all-done.1.part_ref = bf16[4,144,384]{2,1,0:T(8,128)(2,1)S(1)} async-done(((bf16[4,144,384]{2,1,0:T(8,128)(2,1)}), bf16[4,144,384]{2,1,0:T(8,128)(2,1)S(1)}, u32[]{:S(2)}, u32[]{:S(2)}) %all-to-all-start.1) | async-done | bytes 442400 | tf_op jit(solution)/shard_map/all_to_all | solution.py:280
  64.1 1.1 shard_map.76
  65.2 0.0 collective-permute-done.4.w1
  65.2 1.9 %collective-permute-start.5 = (bf16[256,4096]{1,0:T(8,128)(2,1)}, bf16[256,4096]{1,0:T(8,128)(2,1)S(1)}, u32[]{:S(2)}, u32[]{:S(2)}) collective-permute-start(bf16[256,4096]{1,0:T(8,128)(2,1)} %collective-permute-done.4.w1), channel_id=1, source_target_pairs={{0,12},{12,0},{1,13},{13,1},{2,14},{14,2},{3,15},{15,3},{4,16},{16... | collective-permute-start | bytes 6291464 | tf_op jit(solution)/shard_map/ppermute | solution.py:298
  67.1 6.5 %all-to-all-start.2 = ((bf16[64,8,256]{2,1,0:T(8,128)(2,1)}), bf16[64,8,256]{2,1,0:T(8,128)(2,1)S(1)}, u32[]{:S(2)}, u32[]{:S(2)}) async-start(bf16[64,8,256]{2,1,0:T(8,128)(2,1)} %bitcast.4), calls=%async_computation.2 | async-start | bytes 524288 | tf_op jit(solution)/shard_map/all_to_all | solution.py:290
  73.6 0.7 reshape.32.owner_ref
  74.3 1.2 shard_map.73.chooser
  75.5 9.6 %all-to-all-done.2 = bf16[64,8,256]{2,1,0:T(8,128)(2,1)S(1)} async-done(((bf16[64,8,256]{2,1,0:T(8,128)(2,1)}), bf16[64,8,256]{2,1,0:T(8,128)(2,1)S(1)}, u32[]{:S(2)}, u32[]{:S(2)}) %all-to-all-start.2) | async-done | bytes 262176 | tf_op jit(solution)/shard_map/all_to_all | solution.py:290
  85.1 0.2 shard_map.77
  85.3 0.0 collective-permute-done.5.w2
  85.3 10.4 %all_to_all.25.x_ref = bf16[3,64,256]{2,1,0:T(8,128)(2,1)S(1)} all-to-all(bf16[3,64,256]{2,1,0:T(8,128)(2,1)S(1)} %bitcast.30), channel_id=1, replica_groups=mesh['x'=4,'y'=8,'c'=2,'q'=4,'j'=3] {'j'}, dimensions={0} | all-to-all | bytes 196608 | tf_op jit(solution)/shard_map/all_to_all | solution.py:300
  95.7 4.6 %project.1 = bf16[4,16,4096]{2,1,0:T(8,128)(2,1)} custom-call(bf16[3,64,256]{2,1,0:T(8,128)(2,1)S(1)} %all_to_all.25.x_ref, bf16[256,4096]{1,0:T(8,128)(2,1)} %w0.1, bf16[256,4096]{1,0:T(8,128)(2,1)} %collective-permute-done.4.w1, bf16[256,4096]{1,0:T(8,128)(2,1)S(1)} %collective-permute-done.5.w2), custom_call_target="tpu_custom_call" | custom-call | tf_op jit(solution)/shard_map/project/pallas_call | solution.py:304
  100.3 36.2 %all_to_all.26 = bf16[4,16,4096]{2,1,0:T(8,128)(2,1)S(1)} all-to-all(bf16[4,16,4096]{2,1,0:T(8,128)(2,1)} %project.1), channel_id=1, replica_groups=mesh['x'=4,'y'=8,'c'=2,'q'=4,'j'=3] {'q'}, dimensions={0} | all-to-all | bytes 1048576 | tf_op jit(solution)/shard_map/all_to_all | solution.py:312
  136.5 0.0 copy-done.1
  136.5 0.7 fusion
  (7 shorter events, 0.0 us)
Async XLA Ops:
  0.0 34.1 %copy-start = (bf16[192,256]{1,0:T(8,128)(2,1)S(1)}, bf16[192,256]{1,0:T(8,128)(2,1)}, u32[]{:S(2)}) copy-start(bf16[192,256]{1,0:T(8,128)(2,1)} %refs_0_.1) | copy-start | bytes 294916
  1.9 55.9 %copy-start.2 = (s32[12288]{0:T(1024)S(1)}, s32[12288]{0:T(1024)}, u32[]{:S(2)}) copy-start(s32[12288]{0:T(1024)} %param.11) | copy-start | bytes 147460
  1.9 30.3 %all-to-all-start = ((bf16[8,192,256]{2,1,0:T(8,128)(2,1)}), bf16[8,192,256]{2,1,0:T(8,128)(2,1)S(1)}, u32[]{:S(2)}, u32[]{:S(2)}) async-start(bf16[8,192,256]{2,1,0:T(8,128)(2,1)} %prepare.1), calls=%async_computation | async-start | bytes 1572864 | tf_op jit(solution)/shard_map/all_to_all | solution.py:264
  9.1 56.1 %collective-permute-start.4 = (bf16[256,4096]{1,0:T(8,128)(2,1)}, bf16[256,4096]{1,0:T(8,128)(2,1)}, u32[]{:S(2)}, u32[]{:S(2)}) collective-permute-start(bf16[256,4096]{1,0:T(8,128)(2,1)} %w0.1), channel_id=1, source_target_pairs={{0,1},{1,2},{2,0},{12,14},{13,12},{14,13},{3,4},{4,5},{5,3},{15,17... | collective-permute-start | bytes 6291464 | tf_op jit(solution)/shard_map/ppermute | solution.py:251
  32.2 10.9 %collective-permute-start.3 = (bf16[1536,256]{1,0:T(8,128)(2,1)S(1)}, bf16[1536,256]{1,0:T(8,128)(2,1)S(1)}, u32[]{:S(2)}, u32[]{:S(2)}) collective-permute-start(bf16[1536,256]{1,0:T(8,128)(2,1)S(1)} %bitcast.27), channel_id=1, source_target_pairs={{0,12},{12,0},{1,13},{13,1},{2,14},{14,2},{3,15},{15,3},{4,16},{16... | collective-permute-start | bytes 2359304 | tf_op jit(solution)/shard_map/ppermute | solution.py:266
  34.1 6.5 %collective-permute-start.1 = (bf16[192,256]{1,0:T(8,128)(2,1)S(1)}, bf16[192,256]{1,0:T(8,128)(2,1)S(1)}, u32[]{:S(2)}, u32[]{:S(2)}) collective-permute-start(bf16[192,256]{1,0:T(8,128)(2,1)S(1)} %copy-done), channel_id=1, source_target_pairs={{384,0},{576,192},{385,1},{577,193},{386,2},{578,194},{387,3},{579... | collective-permute-start | bytes 294920 | tf_op jit(solution)/shard_map/ppermute | solution.py:265
  37.5 4.8 %collective-permute-start = (bf16[192,256]{1,0:T(8,128)(2,1)S(1)}, bf16[192,256]{1,0:T(8,128)(2,1)S(1)}, u32[]{:S(2)}, u32[]{:S(2)}) collective-permute-start(bf16[192,256]{1,0:T(8,128)(2,1)S(1)} %copy-done), channel_id=1, source_target_pairs={{192,0},{384,192},{576,384},{193,1},{385,193},{577,385},{194,2},{3... | collective-permute-start | bytes 294920 | tf_op jit(solution)/shard_map/ppermute | solution.py:265
  39.3 3.7 %collective-permute-start.2 = (bf16[192,256]{1,0:T(8,128)(2,1)S(1)}, bf16[192,256]{1,0:T(8,128)(2,1)S(1)}, u32[]{:S(2)}, u32[]{:S(2)}) collective-permute-start(bf16[192,256]{1,0:T(8,128)(2,1)S(1)} %copy-done), channel_id=1, source_target_pairs={{576,0},{577,1},{578,2},{579,3},{580,4},{581,5},{582,6},{583,7},{5... | collective-permute-start | bytes 294920 | tf_op jit(solution)/shard_map/ppermute | solution.py:265
  46.1 18.0 %all-to-all-start.1 = ((bf16[4,144,384]{2,1,0:T(8,128)(2,1)}), bf16[4,144,384]{2,1,0:T(8,128)(2,1)S(1)}, u32[]{:S(2)}, u32[]{:S(2)}) async-start(bf16[4,144,384]{2,1,0:T(8,128)(2,1)} %shard_map.75), calls=%async_computation.1 | async-start | bytes 884736 | tf_op jit(solution)/shard_map/all_to_all | solution.py:280
  57.8 0.8 copy-start.3
  65.2 20.1 %collective-permute-start.5 = (bf16[256,4096]{1,0:T(8,128)(2,1)}, bf16[256,4096]{1,0:T(8,128)(2,1)S(1)}, u32[]{:S(2)}, u32[]{:S(2)}) collective-permute-start(bf16[256,4096]{1,0:T(8,128)(2,1)} %collective-permute-done.4.w1), channel_id=1, source_target_pairs={{0,12},{12,0},{1,13},{13,1},{2,14},{14,2},{3,15},{15,3},{4,16},{16... | collective-permute-start | bytes 6291464 | tf_op jit(solution)/shard_map/ppermute | solution.py:298
  67.1 18.0 %all-to-all-start.2 = ((bf16[64,8,256]{2,1,0:T(8,128)(2,1)}), bf16[64,8,256]{2,1,0:T(8,128)(2,1)S(1)}, u32[]{:S(2)}, u32[]{:S(2)}) async-start(bf16[64,8,256]{2,1,0:T(8,128)(2,1)} %bitcast.4), calls=%async_computation.2 | async-start | bytes 524288 | tf_op jit(solution)/shard_map/all_to_all | solution.py:290
  95.7 40.8 %copy-start.1 = (bf16[16,4096]{1,0:T(8,128)(2,1)S(1)}, bf16[16,4096]{1,0:T(8,128)(2,1)}, u32[]{:S(2)}) copy-start(bf16[16,4096]{1,0:T(8,128)(2,1)} %param.13) | copy-start | bytes 393220

commit v7 on v6

--- a/solution.py
+++ b/solution.py
@@ -26,6 +26,7 @@
 FLOOR = -1e9
 
 
+SMALL = pltpu.CompilerParams(vmem_limit_bytes=24 << 20)
 NT = (((1,), (1,)), ((), ()))
 TN = (((0,), (0,)), ((), ()))
 
@@ -207,9 +208,9 @@
     width = w0.shape[1]
     columns = pl.ds(pl.multiple_of(pl.program_id(0) * width, width), width)
     far = x_ref[lax.rem(j + 1 + c, NJ)]
-    total += jnp.dot(far, w2[:, columns], preferred_element_type=jnp.float32)
+    total += jnp.dot(far, w2[...], preferred_element_type=jnp.float32)
     for n in range(NQ):
-        out_ref[n] = total[n * OUT : (n + 1) * OUT].astype(jnp.bfloat16)
+        out_ref[n, :, columns] = total[n * OUT : (n + 1) * OUT].astype(jnp.bfloat16)
 
 
 def prepare_kernel(head, k_ref, v_ref, kv_ref):
@@ -236,7 +237,9 @@
 
 def kernel(body, shapes, in_specs, **more):
     outs = [vmem() for _ in shapes] if isinstance(shapes, list) else vmem()
-    return pl.pallas_call(body, out_shape=shapes, in_specs=in_specs, out_specs=outs, **more)
+    return pl.pallas_call(
+        body, out_shape=shapes, in_specs=in_specs, out_specs=outs, compiler_params=SMALL, **more
+    )
 
 
 def per_device(queries, keys, values, lengths, mlp_owner, out_weight, residual):
@@ -300,15 +303,16 @@
     shared = lax.all_to_all(owned.reshape(NJ, TOK // NJ, COLS), "j", 0, 0, tiled=True)
 
     width = out_weight.shape[1]
-    tile = 1024
+    tile = 2048
     projected = pl.pallas_call(
         project_kernel,
-        out_shape=jax.ShapeDtypeStruct((NQ, OUT, width), jnp.bfloat16),
+        out_shape=out_here(NQ, OUT, width),
         grid=(width // tile,),
-        in_specs=[vmem()] + [pl.BlockSpec((COLS, tile), lambda n: (0, n))] * 2 + [vmem()],
-        out_specs=pl.BlockSpec((NQ, OUT, tile), lambda n: (0, 0, n)),
+        in_specs=[vmem()] + [pl.BlockSpec((COLS, tile), lambda n: (0, n))] * 3,
+        out_specs=vmem(),
         name="project",
-    )(near_core(shared), out_weight, turned, near_core(swapped))
+        compiler_params=SMALL,
+    )(near_core(shared), out_weight, turned, swapped)
     blocks = lax.all_to_all(projected, "q", 0, 0, tiled=True)
     total = residual.astype(jnp.float32)
     for n in range(NQ):

time: 138 us -> 136 us (0.986)
  Pallas kernels: 13.1 us -> 9.75 us
  waiting for transfers between devices: 35.2 us -> 38.2 us
    pallas_call x1, Pallas kernels: 4.62 us -> 2.96 us  [per_device(): pl.pallas_call(project_kernel, out_shape=out_here(NQ, OUT, width), grid=(...]
    all_to_all x1, waiting for transfers between devices: 4.38 us -> 5.91 us  [per_device(): parts = lax.all_to_all(partial, 'x', 0, 0, tiled=True)]
    all_to_all x1, waiting for transfers between devices: 9.58 us -> 11 us  [per_device(): incoming = lax.all_to_all(outgoing, ('x', 'y', 'c'), 0, 0, tiled=True)]
  transfers between devices with their start and end apart: 9 -> 9, of which waited for: 5 -> 5; matrix products, arithmetic and copies ran while one was open for 1% -> 0% of each run, Pallas kernels for 5% -> 4%
where the time goes in v7:
time: 136 us; the launch traced here: 135 us
  blocking collectives  46.4 us (34%)
  starting transfers between devices  40 us (29%)
  waiting for transfers between devices  38.2 us (28%)
  Pallas kernels  9.75 us (7%)
    all_to_all x1, blocking collectives, per_device(): blocks = lax.all_to_all(projected, 'q', 0, 0, tiled=True)  36 us
    all_to_all x1, waiting for transfers between devices, per_device(): own = lax.all_to_all(kv, 'y', 0, 0, tiled=True).reshape(NY * TOK, COLS)  18.8 us
    all_to_all x1, starting transfers between devices, per_device(): parts = lax.all_to_all(partial, 'x', 0, 0, tiled=True)  11.7 us
    all_to_all x1, waiting for transfers between devices, per_device(): incoming = lax.all_to_all(outgoing, ('x', 'y', 'c'), 0, 0, tiled=True)  11 us
    all_to_all x1, blocking collectives, per_device(): lax.all_to_all(owned.reshape(NJ, TOK // NJ, COLS), 'j', 0, 0, tiled=True)  10.4 us
    all_to_all x1, starting transfers between devices, per_device(): own = lax.all_to_all(kv, 'y', 0, 0, tiled=True).reshape(NY * TOK, COLS)  7.23 us
    ppermute x3, starting transfers between devices, per_device(): lax.ppermute(queries, 'x', [(i, i - s) for i in range(s, NX)])  6.49 us
    all_to_all x1, starting transfers between devices, per_device(): incoming = lax.all_to_all(outgoing, ('x', 'y', 'c'), 0, 0, tiled=True)  6.45 us
  transfers between devices with their start and end apart: 9, of which 5 were waited for; matrix products, arithmetic and copies ran while one was open for 0% of the time, Pallas kernels for 4%

profile of v7, /device:TPU:6, one launch (start us, length us, event | category | flops | bytes accessed | tf_op | source)
XLA Modules:
  0.0 135.5 jit_solution(9811101178066526566)
XLA Ops:
  0.0 2.0 %prepare.1 = bf16[8,192,256]{2,1,0:T(8,128)(2,1)} custom-call(s32[1]{0:T(128)} %bitcast.2.head, bf16[192,768]{1,0:T(8,128)(2,1)} %k_ref.1, bf16[192,768]{1,0:T(8,128)(2,1)} %v_ref.1), custom_call_target="tpu_custom_call" | custom-call | tf_op jit(solution)/shard_map/prepare/pallas_call | solution.py:256
  2.0 7.2 %all-to-all-start = ((bf16[8,192,256]{2,1,0:T(8,128)(2,1)}), bf16[8,192,256]{2,1,0:T(8,128)(2,1)S(1)}, u32[]{:S(2)}, u32[]{:S(2)}) async-start(bf16[8,192,256]{2,1,0:T(8,128)(2,1)} %prepare.1), calls=%async_computation | async-start | bytes 1572864 | tf_op jit(solution)/shard_map/all_to_all | solution.py:267
  9.2 0.0 copy-done
  9.3 4.3 %collective-permute-start.4 = (bf16[256,4096]{1,0:T(8,128)(2,1)S(1)}, bf16[256,4096]{1,0:T(8,128)(2,1)}, u32[]{:S(2)}, u32[]{:S(2)}) collective-permute-start(bf16[256,4096]{1,0:T(8,128)(2,1)S(1)} %copy-done), channel_id=1, source_target_pairs={{0,1},{1,2},{2,0},{12,14},{13,12},{14,13},{3,4},{4,5},{5,3},{15,17... | collective-permute-start | bytes 6291464 | tf_op jit(solution)/shard_map/ppermute | solution.py:254
  13.5 18.8 %all-to-all-done = bf16[8,192,256]{2,1,0:T(8,128)(2,1)S(1)} async-done(((bf16[8,192,256]{2,1,0:T(8,128)(2,1)}), bf16[8,192,256]{2,1,0:T(8,128)(2,1)S(1)}, u32[]{:S(2)}, u32[]{:S(2)}) %all-to-all-start) | async-done | bytes 786464 | tf_op jit(solution)/shard_map/all_to_all | solution.py:267
  32.4 1.9 %collective-permute-start.3 = (bf16[1536,256]{1,0:T(8,128)(2,1)S(1)}, bf16[1536,256]{1,0:T(8,128)(2,1)S(1)}, u32[]{:S(2)}, u32[]{:S(2)}) collective-permute-start(bf16[1536,256]{1,0:T(8,128)(2,1)S(1)} %bitcast.27), channel_id=1, source_target_pairs={{0,12},{12,0},{1,13},{13,1},{2,14},{14,2},{3,15},{15,3},{4,16},{16... | collective-permute-start | bytes 2359304 | tf_op jit(solution)/shard_map/ppermute | solution.py:269
  34.3 3.3 %collective-permute-start.1 = (bf16[192,256]{1,0:T(8,128)(2,1)S(1)}, bf16[192,256]{1,0:T(8,128)(2,1)S(1)}, u32[]{:S(2)}, u32[]{:S(2)}) collective-permute-start(bf16[192,256]{1,0:T(8,128)(2,1)S(1)} %copy-done.1), channel_id=1, source_target_pairs={{384,0},{576,192},{385,1},{577,193},{386,2},{578,194},{387,3},{579... | collective-permute-start | bytes 294920 | tf_op jit(solution)/shard_map/ppermute | solution.py:268
  37.6 1.9 %collective-permute-start = (bf16[192,256]{1,0:T(8,128)(2,1)S(1)}, bf16[192,256]{1,0:T(8,128)(2,1)S(1)}, u32[]{:S(2)}, u32[]{:S(2)}) collective-permute-start(bf16[192,256]{1,0:T(8,128)(2,1)S(1)} %copy-done.1), channel_id=1, source_target_pairs={{192,0},{384,192},{576,384},{193,1},{385,193},{577,385},{194,2},{3... | collective-permute-start | bytes 294920 | tf_op jit(solution)/shard_map/ppermute | solution.py:268
  39.5 1.3 collective-permute-start.2
  40.8 0.0 collective-permute-done.1.refs_2_
  40.8 1.6 %collective-permute-done.refs_1_ = bf16[192,256]{1,0:T(8,128)(2,1)S(1)} collective-permute-done((bf16[192,256]{1,0:T(8,128)(2,1)S(1)}, bf16[192,256]{1,0:T(8,128)(2,1)S(1)}, u32[]{:S(2)}, u32[]{:S(2)}) %collective-permute-start) | collective-permute-done | bytes 98336 | tf_op jit(solution)/shard_map/ppermute | solution.py:268
  42.4 0.8 collective-permute-done.2.refs_3_
  43.2 0.0 collective-permute-done.3.refs_5_
  43.2 2.9 %shard_map.75 = bf16[4,144,384]{2,1,0:T(8,128)(2,1)} custom-call(s32[24]{0:T(128)S(1)} %copy-done.2, bf16[192,256]{1,0:T(8,128)(2,1)S(1)} %copy-done.1, bf16[192,256]{1,0:T(8,128)(2,1)S(1)} %collective-permute-done.refs_1_, bf16[192,256]{1,0:T(8,128)(2,1)S(1)} %collective-permute-done.1.refs_2_, bf16[192,256]{1,0:T(8,128)(2,1)S(1)} %collective-permute-done.2.refs_3_, ...), custom_call_target="tpu_custom_call" | custom-call | tf_op jit(solution)/shard_map/pallas_call | solution.py:271
  46.1 11.7 %all-to-all-start.1 = ((bf16[4,144,384]{2,1,0:T(8,128)(2,1)}), bf16[4,144,384]{2,1,0:T(8,128)(2,1)S(1)}, u32[]{:S(2)}, u32[]{:S(2)}) async-start(bf16[4,144,384]{2,1,0:T(8,128)(2,1)} %shard_map.75), calls=%async_computation.1 | async-start | bytes 884736 | tf_op jit(solution)/shard_map/all_to_all | solution.py:283
  57.8 0.1 dynamic_slice.3
  57.9 0.1 copy.8.col_ref
  58.0 0.2 shard_map.74.placement
  58.3 5.9 %all-to-all-done.1.part_ref = bf16[4,144,384]{2,1,0:T(8,128)(2,1)S(1)} async-done(((bf16[4,144,384]{2,1,0:T(8,128)(2,1)}), bf16[4,144,384]{2,1,0:T(8,128)(2,1)S(1)}, u32[]{:S(2)}, u32[]{:S(2)}) %all-to-all-start.1) | async-done | bytes 442400 | tf_op jit(solution)/shard_map/all_to_all | solution.py:283
  64.2 1.1 shard_map.76
  65.3 0.0 collective-permute-done.4.w1
  65.3 1.9 %collective-permute-start.5 = (bf16[256,4096]{1,0:T(8,128)(2,1)}, bf16[256,4096]{1,0:T(8,128)(2,1)}, u32[]{:S(2)}, u32[]{:S(2)}) collective-permute-start(bf16[256,4096]{1,0:T(8,128)(2,1)} %collective-permute-done.4.w1), channel_id=1, source_target_pairs={{0,12},{12,0},{1,13},{13,1},{2,14},{14,2},{3,15},{15,3},{4,16},{16... | collective-permute-start | bytes 6291464 | tf_op jit(solution)/shard_map/ppermute | solution.py:301
  67.2 6.5 %all-to-all-start.2 = ((bf16[64,8,256]{2,1,0:T(8,128)(2,1)}), bf16[64,8,256]{2,1,0:T(8,128)(2,1)S(1)}, u32[]{:S(2)}, u32[]{:S(2)}) async-start(bf16[64,8,256]{2,1,0:T(8,128)(2,1)} %bitcast.4), calls=%async_computation.2 | async-start | bytes 524288 | tf_op jit(solution)/shard_map/all_to_all | solution.py:293
  73.6 0.1 reshape.32.owner_ref
  73.7 0.4 shard_map.73.chooser
  74.1 11.0 %all-to-all-done.2 = bf16[64,8,256]{2,1,0:T(8,128)(2,1)S(1)} async-done(((bf16[64,8,256]{2,1,0:T(8,128)(2,1)}), bf16[64,8,256]{2,1,0:T(8,128)(2,1)S(1)}, u32[]{:S(2)}, u32[]{:S(2)}) %all-to-all-start.2) | async-done | bytes 262176 | tf_op jit(solution)/shard_map/all_to_all | solution.py:293
  85.2 0.2 shard_map.77
  85.4 0.0 collective-permute-done.5.w2
  85.4 10.4 %all_to_all.25.x_ref = bf16[3,64,256]{2,1,0:T(8,128)(2,1)S(1)} all-to-all(bf16[3,64,256]{2,1,0:T(8,128)(2,1)S(1)} %bitcast.30), channel_id=1, replica_groups=mesh['x'=4,'y'=8,'c'=2,'q'=4,'j'=3] {'j'}, dimensions={0} | all-to-all | bytes 196608 | tf_op jit(solution)/shard_map/all_to_all | solution.py:303
  95.8 3.0 %project.1 = bf16[4,16,4096]{2,1,0:T(8,128)(2,1)S(1)} custom-call(bf16[3,64,256]{2,1,0:T(8,128)(2,1)S(1)} %all_to_all.25.x_ref, bf16[256,4096]{1,0:T(8,128)(2,1)S(1)} %copy-done, bf16[256,4096]{1,0:T(8,128)(2,1)} %collective-permute-done.4.w1, bf16[256,4096]{1,0:T(8,128)(2,1)} %collective-permute-done.5.w2), custom_call_target="tpu_custom_call" | custom-call | tf_op jit(solution)/shard_map/project/pallas_call | solution.py:307
  98.8 36.0 %all_to_all.26 = bf16[4,16,4096]{2,1,0:T(8,128)(2,1)S(1)} all-to-all(bf16[4,16,4096]{2,1,0:T(8,128)(2,1)S(1)} %project.1), channel_id=1, replica_groups=mesh['x'=4,'y'=8,'c'=2,'q'=4,'j'=3] {'q'}, dimensions={0} | all-to-all | bytes 1048576 | tf_op jit(solution)/shard_map/all_to_all | solution.py:316
  134.7 0.7 fusion
  (9 shorter events, 0.0 us)
Async XLA Ops:
  0.0 9.2 %copy-start = (bf16[256,4096]{1,0:T(8,128)(2,1)S(1)}, bf16[256,4096]{1,0:T(8,128)(2,1)}, u32[]{:S(2)}) copy-start(bf16[256,4096]{1,0:T(8,128)(2,1)} %w0.1) | copy-start | bytes 6291460
  0.0 34.3 %copy-start.1 = (bf16[192,256]{1,0:T(8,128)(2,1)S(1)}, bf16[192,256]{1,0:T(8,128)(2,1)}, u32[]{:S(2)}) copy-start(bf16[192,256]{1,0:T(8,128)(2,1)} %refs_0_.1) | copy-start | bytes 294916
  0.0 43.2 %copy-start.2 = (s32[24]{0:T(128)S(1)}, s32[24]{0:T(128)}, u32[]{:S(2)}) copy-start(s32[24]{0:T(128)} %lengths.1) | copy-start | bytes 292
  2.0 55.8 %copy-start.4 = (s32[12288]{0:T(1024)S(1)}, s32[12288]{0:T(1024)}, u32[]{:S(2)}) copy-start(s32[12288]{0:T(1024)} %param.11) | copy-start | bytes 147460
  2.0 30.3 %all-to-all-start = ((bf16[8,192,256]{2,1,0:T(8,128)(2,1)}), bf16[8,192,256]{2,1,0:T(8,128)(2,1)S(1)}, u32[]{:S(2)}, u32[]{:S(2)}) async-start(bf16[8,192,256]{2,1,0:T(8,128)(2,1)} %prepare.1), calls=%async_computation | async-start | bytes 1572864 | tf_op jit(solution)/shard_map/all_to_all | solution.py:267
  9.3 56.0 %collective-permute-start.4 = (bf16[256,4096]{1,0:T(8,128)(2,1)S(1)}, bf16[256,4096]{1,0:T(8,128)(2,1)}, u32[]{:S(2)}, u32[]{:S(2)}) collective-permute-start(bf16[256,4096]{1,0:T(8,128)(2,1)S(1)} %copy-done), channel_id=1, source_target_pairs={{0,1},{1,2},{2,0},{12,14},{13,12},{14,13},{3,4},{4,5},{5,3},{15,17... | collective-permute-start | bytes 6291464 | tf_op jit(solution)/shard_map/ppermute | solution.py:254
  32.4 10.9 %collective-permute-start.3 = (bf16[1536,256]{1,0:T(8,128)(2,1)S(1)}, bf16[1536,256]{1,0:T(8,128)(2,1)S(1)}, u32[]{:S(2)}, u32[]{:S(2)}) collective-permute-start(bf16[1536,256]{1,0:T(8,128)(2,1)S(1)} %bitcast.27), channel_id=1, source_target_pairs={{0,12},{12,0},{1,13},{13,1},{2,14},{14,2},{3,15},{15,3},{4,16},{16... | collective-permute-start | bytes 2359304 | tf_op jit(solution)/shard_map/ppermute | solution.py:269
  34.3 6.5 %collective-permute-start.1 = (bf16[192,256]{1,0:T(8,128)(2,1)S(1)}, bf16[192,256]{1,0:T(8,128)(2,1)S(1)}, u32[]{:S(2)}, u32[]{:S(2)}) collective-permute-start(bf16[192,256]{1,0:T(8,128)(2,1)S(1)} %copy-done.1), channel_id=1, source_target_pairs={{384,0},{576,192},{385,1},{577,193},{386,2},{578,194},{387,3},{579... | collective-permute-start | bytes 294920 | tf_op jit(solution)/shard_map/ppermute | solution.py:268
  37.6 4.8 %collective-permute-start = (bf16[192,256]{1,0:T(8,128)(2,1)S(1)}, bf16[192,256]{1,0:T(8,128)(2,1)S(1)}, u32[]{:S(2)}, u32[]{:S(2)}) collective-permute-start(bf16[192,256]{1,0:T(8,128)(2,1)S(1)} %copy-done.1), channel_id=1, source_target_pairs={{192,0},{384,192},{576,384},{193,1},{385,193},{577,385},{194,2},{3... | collective-permute-start | bytes 294920 | tf_op jit(solution)/shard_map/ppermute | solution.py:268
  39.5 3.7 %collective-permute-start.2 = (bf16[192,256]{1,0:T(8,128)(2,1)S(1)}, bf16[192,256]{1,0:T(8,128)(2,1)S(1)}, u32[]{:S(2)}, u32[]{:S(2)}) collective-permute-start(bf16[192,256]{1,0:T(8,128)(2,1)S(1)} %copy-done.1), channel_id=1, source_target_pairs={{576,0},{577,1},{578,2},{579,3},{580,4},{581,5},{582,6},{583,7},{5... | collective-permute-start | bytes 294920 | tf_op jit(solution)/shard_map/ppermute | solution.py:268
  46.1 18.0 %all-to-all-start.1 = ((bf16[4,144,384]{2,1,0:T(8,128)(2,1)}), bf16[4,144,384]{2,1,0:T(8,128)(2,1)S(1)}, u32[]{:S(2)}, u32[]{:S(2)}) async-start(bf16[4,144,384]{2,1,0:T(8,128)(2,1)} %shard_map.75), calls=%async_computation.1 | async-start | bytes 884736 | tf_op jit(solution)/shard_map/all_to_all | solution.py:283
  65.3 20.1 %collective-permute-start.5 = (bf16[256,4096]{1,0:T(8,128)(2,1)}, bf16[256,4096]{1,0:T(8,128)(2,1)}, u32[]{:S(2)}, u32[]{:S(2)}) collective-permute-start(bf16[256,4096]{1,0:T(8,128)(2,1)} %collective-permute-done.4.w1), channel_id=1, source_target_pairs={{0,12},{12,0},{1,13},{13,1},{2,14},{14,2},{3,15},{15,3},{4,16},{16... | collective-permute-start | bytes 6291464 | tf_op jit(solution)/shard_map/ppermute | solution.py:301
  67.2 18.0 %all-to-all-start.2 = ((bf16[64,8,256]{2,1,0:T(8,128)(2,1)}), bf16[64,8,256]{2,1,0:T(8,128)(2,1)S(1)}, u32[]{:S(2)}, u32[]{:S(2)}) async-start(bf16[64,8,256]{2,1,0:T(8,128)(2,1)} %bitcast.4), calls=%async_computation.2 | async-start | bytes 524288 | tf_op jit(solution)/shard_map/all_to_all | solution.py:293
  95.8 39.0 %copy-start.3 = (bf16[16,4096]{1,0:T(8,128)(2,1)S(1)}, bf16[16,4096]{1,0:T(8,128)(2,1)}, u32[]{:S(2)}) copy-start(bf16[16,4096]{1,0:T(8,128)(2,1)} %param.13) | copy-start | bytes 393220

commit v8 on v7

--- a/solution.py
+++ b/solution.py
@@ -1,3 +1,5 @@
+import functools
+
 import jax
 import jax.numpy as jnp
 from jax import lax
@@ -35,19 +37,12 @@
     return (v + jnp.abs(v) * 0.0079).astype(jnp.bfloat16).astype(jnp.float32)
 
 
-def attend_kernel(lengths, *refs):
-    q_refs, (own_ref, peer_ref, out_ref, q_all, q_s, m_s, l_s, acc_s) = refs[:NX], refs[NX:]
+def attend_kernel(first, count, lengths, *refs):
+    q_refs, (own_ref, peer_ref), rest = refs[:count], refs[count : count + 2], refs[count + 2 :]
+    out_refs, (q_all, q_s, m_s, l_s, acc_s) = rest[:count], rest[count:]
     for s, q_ref in enumerate(q_refs):
         q_all[s] = q_ref[...]
     x, y, c = (lax.axis_index(a) for a in ("x", "y", "c"))
-
-    def empty(xs, carry):
-        out_ref[xs, :HEAD, :] = jnp.zeros((HEAD, QROWS), jnp.bfloat16)
-        rows = lax.broadcasted_iota(jnp.int32, (PART - HEAD, QROWS), 0)
-        out_ref[xs, HEAD:, :] = jnp.where(rows == 0, FLOOR, 0.0).astype(jnp.bfloat16)
-        return carry
-
-    lax.fori_loop(0, x, empty, 0)
 
     def slab(xs, carry):
         p0 = (xs * (NY * NC) + y * NC + c) * TOK
@@ -63,8 +58,8 @@
             start = jnp.where(pos >= end, end, start)
             first_start = jnp.where(p0 >= end, end, first_start)
             last_start = jnp.where(last >= end, end, last_start)
-        q_s[:TOK, :] = q_all[xs - x, :, :HEAD]
-        q_s[TOK:, :] = q_all[xs - x, :, HEAD:]
+        q_s[:TOK, :] = q_all[xs - x - first, :, :HEAD]
+        q_s[TOK:, :] = q_all[xs - x - first, :, HEAD:]
         m_s[...] = jnp.full((1, QROWS), FLOOR, jnp.float32)
         l_s[...] = jnp.zeros((1, QROWS), jnp.float32)
         acc_s[...] = jnp.zeros((HEAD, QROWS), jnp.float32)
@@ -123,15 +118,20 @@
 
         lax.fori_loop(0, NY // CHUNK_SLABS, chunk, 0)
 
-        out_ref[xs, :HEAD, :] = acc_s[...].astype(jnp.bfloat16)
         total = l_s[...]
         high_part = total.astype(jnp.bfloat16).astype(jnp.float32)
         rows = lax.broadcasted_iota(jnp.int32, (PART - HEAD, QROWS), 0)
         stats = jnp.where(rows == 0, m_s[...], jnp.where(rows == 1, high_part, total - high_part))
-        out_ref[xs, HEAD:, :] = stats.astype(jnp.bfloat16)
+        for n, out_ref in enumerate(out_refs):
+
+            @pl.when(xs - x - first == n)
+            def _(out_ref=out_ref):
+                out_ref[:HEAD, :] = acc_s[...].astype(jnp.bfloat16)
+                out_ref[HEAD:, :] = stats.astype(jnp.bfloat16)
+
         return carry
 
-    lax.fori_loop(x, NX, slab, 0)
+    lax.fori_loop(x + first, jnp.minimum(x + first + count, NX), slab, 0)
 
 
 def place_kernel(row_ref, col_ref, out_ref):
@@ -146,17 +146,21 @@
     out_ref[...] = (ids == slot).astype(jnp.float32).astype(jnp.bfloat16)
 
 
-def merge_kernel(placement, part_ref, out_ref):
-    m = [part_ref[i, HEAD : HEAD + 1, :].astype(jnp.float32) for i in range(NX)]
+def merge_kernel(placement, *refs):
+    part_refs, out_ref = refs[:NX], refs[NX]
+    x = lax.axis_index("x")
+    m = []
+    for s, ref in enumerate(part_refs):
+        m.append(jnp.where(s <= x, ref[HEAD : HEAD + 1, :].astype(jnp.float32), FLOOR))
     top = jnp.maximum(jnp.maximum(m[0], m[1]), jnp.maximum(m[2], m[3]))
     total = jnp.zeros((1, QROWS), jnp.float32)
     mixed = jnp.zeros((HEAD, QROWS), jnp.float32)
-    for i in range(NX):
-        w = jnp.exp2(m[i] - top)
-        part = part_ref[i, HEAD + 1 : HEAD + 2, :].astype(jnp.float32)
-        part = part + part_ref[i, HEAD + 2 : HEAD + 3, :].astype(jnp.float32)
+    for s, ref in enumerate(part_refs):
+        w = jnp.exp2(m[s] - top)
+        part = ref[HEAD + 1 : HEAD + 2, :].astype(jnp.float32)
+        part = part + ref[HEAD + 2 : HEAD + 3, :].astype(jnp.float32)
         total = total + w * part
-        mixed = mixed + w * part_ref[i, :HEAD, :].astype(jnp.float32)
+        mixed = mixed + w * ref[:HEAD, :].astype(jnp.float32)
     attention = (mixed / total).astype(jnp.bfloat16)
     for h in range(HEADS_HERE):
         rows = lax.dot_general(
@@ -268,27 +272,33 @@
     moved = [lax.ppermute(queries, "x", [(i, i - s) for i in range(s, NX)]) for s in range(1, NX)]
     other = lax.ppermute(own, "c", peer)
 
-    partial = kernel(
-        attend_kernel,
-        out_here(NX, PART, QROWS),
-        [smem()] + [vmem()] * (NX + 2),
-        scratch_shapes=[
-            pltpu.VMEM((NX, TOK, COLS), jnp.bfloat16),
-            pltpu.VMEM((QROWS, HEAD), jnp.bfloat16),
-            pltpu.VMEM((1, QROWS), jnp.float32),
-            pltpu.VMEM((1, QROWS), jnp.float32),
-            pltpu.VMEM((HEAD, QROWS), jnp.float32),
-        ],
-    )(lengths, *map(near_core, (queries, *moved)), near_core(own), near_core(other))
-    parts = lax.all_to_all(partial, "x", 0, 0, tiled=True)
+    def attend(first, sent):
+        return kernel(
+            functools.partial(attend_kernel, first, len(sent)),
+            [out_here(PART, QROWS)] * len(sent),
+            [smem()] + [vmem()] * (len(sent) + 2),
+            scratch_shapes=[
+                pltpu.VMEM((len(sent), TOK, COLS), jnp.bfloat16),
+                pltpu.VMEM((QROWS, HEAD), jnp.bfloat16),
+                pltpu.VMEM((1, QROWS), jnp.float32),
+                pltpu.VMEM((1, QROWS), jnp.float32),
+                pltpu.VMEM((HEAD, QROWS), jnp.float32),
+            ],
+        )(lengths, *map(near_core, (*sent, own, other)))
+
+    away = attend(1, moved)
+    arrived = [
+        lax.ppermute(p, "x", [(i, i + s) for i in range(NX - s)]) for s, p in enumerate(away, 1)
+    ]
+    home = attend(0, [queries])
 
     targets = lax.dynamic_slice_in_dim(mlp_owner, dc * TOK, TOK, 0)
     placement = kernel(place_kernel, out_here(SLOT_TOTAL, TOK), [vmem(), vmem()])(
         targets.reshape(1, TOK), targets.reshape(TOK, 1)
     )
     outgoing = kernel(
-        merge_kernel, out_here(SLOT_TOTAL, COLS), [vmem(), vmem()]
-    )(near_core(placement), near_core(parts))
+        merge_kernel, out_here(SLOT_TOTAL, COLS), [vmem()] * (NX + 1)
+    )(*map(near_core, (placement, *home, *arrived)))
     outgoing = outgoing.reshape(N_DC, PADDED, COLS)
     incoming = lax.all_to_all(outgoing, ("x", "y", "c"), 0, 0, tiled=True)
     chooser = kernel(choose_kernel, out_here(TOK, SLOT_TOTAL), [vmem()])(

time: 136 us -> 135 us (level)
  starting transfers between devices: 40 us -> 34.9 us
  waiting for transfers between devices: 38.2 us -> 43.2 us
    all_to_all x1 -> x0, starting transfers between devices: 11.7 us -> none  [per_device(): parts = lax.all_to_all(partial, 'x', 0, 0, tiled=True)]
    ppermute x0 -> x3, waiting for transfers between devices: none -> 10.9 us  [per_device(): lax.ppermute(p, 'x', [(i, i + s) for i in range(NX - s)])]
    all_to_all x1 -> x0, waiting for transfers between devices: 5.91 us -> none  [per_device(): parts = lax.all_to_all(partial, 'x', 0, 0, tiled=True)]
    ppermute x0 -> x3, starting transfers between devices: none -> 3.88 us  [per_device(): lax.ppermute(p, 'x', [(i, i + s) for i in range(NX - s)])]
    all_to_all x1, starting transfers between devices: 6.45 us -> 9.41 us  [per_device(): incoming = lax.all_to_all(outgoing, ('x', 'y', 'c'), 0, 0, tiled=True)]
    pallas_call x2 -> x3, Pallas kernels: 4 us -> 3.8 us  [the longest x2 2.68 us: attend(): kernel(functools.partial(attend_kernel, first, len(sent)), [out_here(PART...]
  transfers between devices with their start and end apart: 9 -> 11, of which waited for: 5 -> 6; matrix products, arithmetic and copies ran while one was open for 0% -> 0% of each run, Pallas kernels for 4% -> 3%
where the time goes in v8:
time: 135 us
  blocking collectives  45.9 us (34%)
  waiting for transfers between devices  43.2 us (32%)
  starting transfers between devices  34.9 us (26%)
  Pallas kernels  9.42 us (7%)
    all_to_all x1, blocking collectives, per_device(): blocks = lax.all_to_all(projected, 'q', 0, 0, tiled=True)  36.8 us
    all_to_all x1, waiting for transfers between devices, per_device(): own = lax.all_to_all(kv, 'y', 0, 0, tiled=True).reshape(NY * TOK, COLS)  18.8 us
    all_to_all x1, waiting for transfers between devices, per_device(): incoming = lax.all_to_all(outgoing, ('x', 'y', 'c'), 0, 0, tiled=True)  11 us
    ppermute x3, waiting for transfers between devices, per_device(): lax.ppermute(p, 'x', [(i, i + s) for i in range(NX - s)])  10.9 us
    all_to_all x1, starting transfers between devices, per_device(): incoming = lax.all_to_all(outgoing, ('x', 'y', 'c'), 0, 0, tiled=True)  9.41 us
    all_to_all x1, blocking collectives, per_device(): lax.all_to_all(owned.reshape(NJ, TOK // NJ, COLS), 'j', 0, 0, tiled=True)  9.12 us
    all_to_all x1, starting transfers between devices, per_device(): own = lax.all_to_all(kv, 'y', 0, 0, tiled=True).reshape(NY * TOK, COLS)  7.1 us
    ppermute x3, starting transfers between devices, per_device(): lax.ppermute(queries, 'x', [(i, i - s) for i in range(s, NX)])  6.47 us
  transfers between devices with their start and end apart: 11, of which 6 were waited for; matrix products, arithmetic and copies ran while one was open for 0% of the time, Pallas kernels for 3%

profile of v8, /device:TPU:6, one launch (start us, length us, event | category | flops | bytes accessed | tf_op | source)
XLA Modules:
  0.0 134.7 jit_solution(14155524339356312478)
XLA Ops:
  0.0 1.8 %prepare.1 = bf16[8,192,256]{2,1,0:T(8,128)(2,1)} custom-call(s32[1]{0:T(128)} %bitcast.2.head, bf16[192,768]{1,0:T(8,128)(2,1)} %k_ref.1, bf16[192,768]{1,0:T(8,128)(2,1)} %v_ref.1), custom_call_target="tpu_custom_call" | custom-call | tf_op jit(solution)/shard_map/prepare/pallas_call | solution.py:260
  1.9 7.1 %all-to-all-start = ((bf16[8,192,256]{2,1,0:T(8,128)(2,1)}), bf16[8,192,256]{2,1,0:T(8,128)(2,1)S(1)}, u32[]{:S(2)}, u32[]{:S(2)}) async-start(bf16[8,192,256]{2,1,0:T(8,128)(2,1)} %prepare.1), calls=%async_computation | async-start | bytes 1572864 | tf_op jit(solution)/shard_map/all_to_all | solution.py:271
  9.0 4.3 %collective-permute-start.7 = (bf16[256,4096]{1,0:T(8,128)(2,1)}, bf16[256,4096]{1,0:T(8,128)(2,1)}, u32[]{:S(2)}, u32[]{:S(2)}) collective-permute-start(bf16[256,4096]{1,0:T(8,128)(2,1)} %w0.1), channel_id=1, source_target_pairs={{0,1},{1,2},{2,0},{12,14},{13,12},{14,13},{3,4},{4,5},{5,3},{15,17... | collective-permute-start | bytes 6291464 | tf_op jit(solution)/shard_map/ppermute | solution.py:258
  13.2 18.8 %all-to-all-done = bf16[8,192,256]{2,1,0:T(8,128)(2,1)S(1)} async-done(((bf16[8,192,256]{2,1,0:T(8,128)(2,1)}), bf16[8,192,256]{2,1,0:T(8,128)(2,1)S(1)}, u32[]{:S(2)}, u32[]{:S(2)}) %all-to-all-start) | async-done | bytes 786464 | tf_op jit(solution)/shard_map/all_to_all | solution.py:271
  32.1 1.9 %collective-permute-start = (bf16[1536,256]{1,0:T(8,128)(2,1)S(1)}, bf16[1536,256]{1,0:T(8,128)(2,1)S(1)}, u32[]{:S(2)}, u32[]{:S(2)}) collective-permute-start(bf16[1536,256]{1,0:T(8,128)(2,1)S(1)} %bitcast.27), channel_id=1, source_target_pairs={{0,12},{12,0},{1,13},{13,1},{2,14},{14,2},{3,15},{15,3},{4,16},{16... | collective-permute-start | bytes 2359304 | tf_op jit(solution)/shard_map/ppermute | solution.py:273
  34.0 2.7 %collective-permute-start.1 = (bf16[192,256]{1,0:T(8,128)(2,1)S(1)}, bf16[192,256]{1,0:T(8,128)(2,1)S(1)}, u32[]{:S(2)}, u32[]{:S(2)}) collective-permute-start(bf16[192,256]{1,0:T(8,128)(2,1)S(1)} %copy-done), channel_id=1, source_target_pairs={{192,0},{384,192},{576,384},{193,1},{385,193},{577,385},{194,2},{3... | collective-permute-start | bytes 294920 | tf_op jit(solution)/shard_map/ppermute | solution.py:272
  36.8 1.3 collective-permute-start.3
  38.1 2.4 %collective-permute-start.2 = (bf16[192,256]{1,0:T(8,128)(2,1)S(1)}, bf16[192,256]{1,0:T(8,128)(2,1)S(1)}, u32[]{:S(2)}, u32[]{:S(2)}) collective-permute-start(bf16[192,256]{1,0:T(8,128)(2,1)S(1)} %copy-done), channel_id=1, source_target_pairs={{384,0},{576,192},{385,1},{577,193},{386,2},{578,194},{387,3},{579... | collective-permute-start | bytes 294920 | tf_op jit(solution)/shard_map/ppermute | solution.py:272
  40.5 2.4 %collective-permute-done.3.refs_2_ = bf16[192,256]{1,0:T(8,128)(2,1)S(1)} collective-permute-done((bf16[192,256]{1,0:T(8,128)(2,1)S(1)}, bf16[192,256]{1,0:T(8,128)(2,1)S(1)}, u32[]{:S(2)}, u32[]{:S(2)}) %collective-permute-start.3) | collective-permute-done | bytes 98336 | tf_op jit(solution)/shard_map/ppermute | solution.py:272
  42.9 0.0 collective-permute-done.2.refs_1_
  42.9 0.6 shard_map.76
  43.5 1.3 collective-permute-start.4
  44.8 1.3 collective-permute-start.5
  46.1 1.3 collective-permute-start.6
  47.4 0.1 dynamic_slice.3
  47.5 0.1 copy.8.col_ref
  47.6 0.2 shard_map.74.placement
  47.8 2.1 %shard_map.75.refs_0_ = bf16[144,384]{1,0:T(8,128)(2,1)S(1)} custom-call(s32[24]{0:T(128)S(1)} %copy-done.1, bf16[192,256]{1,0:T(8,128)(2,1)S(1)} %copy-done, bf16[1536,256]{1,0:T(8,128)(2,1)S(1)} %bitcast.29, bf16[1536,256]{1,0:T(8,128)(2,1)S(1)} %collective-permute-done.refs_2_.refs_4_), custom_call_target="tpu_custom_call" | custom-call | tf_op jit(solution)/shard_map/pallas_call | solution.py:276
  50.0 0.6 collective-permute-done.4.refs_1_
  50.5 8.1 %collective-permute-done.5.refs_2_ = bf16[144,384]{1,0:T(8,128)(2,1)S(1)} collective-permute-done((bf16[144,384]{1,0:T(8,128)(2,1)S(1)}, bf16[144,384]{1,0:T(8,128)(2,1)S(1)}, u32[]{:S(2)}, u32[]{:S(2)}) %collective-permute-start.5) | collective-permute-done | bytes 110624 | tf_op jit(solution)/shard_map/ppermute | solution.py:291
  58.6 2.3 %collective-permute-done.6.refs_3_ = bf16[144,384]{1,0:T(8,128)(2,1)S(1)} collective-permute-done((bf16[144,384]{1,0:T(8,128)(2,1)S(1)}, bf16[144,384]{1,0:T(8,128)(2,1)S(1)}, u32[]{:S(2)}, u32[]{:S(2)}) %collective-permute-start.6) | collective-permute-done | bytes 110624 | tf_op jit(solution)/shard_map/ppermute | solution.py:291
  60.9 1.1 shard_map.77
  62.0 1.9 %collective-permute-start.8 = (bf16[256,4096]{1,0:T(8,128)(2,1)}, bf16[256,4096]{1,0:T(8,128)(2,1)S(1)}, u32[]{:S(2)}, u32[]{:S(2)}) collective-permute-start(bf16[256,4096]{1,0:T(8,128)(2,1)} %collective-permute-done.7.w1), channel_id=1, source_target_pairs={{0,12},{12,0},{1,13},{13,1},{2,14},{14,2},{3,15},{15,3},{4,16},{16... | collective-permute-start | bytes 6291464 | tf_op jit(solution)/shard_map/ppermute | solution.py:311
  63.9 9.4 %all-to-all-start.1 = ((bf16[64,8,256]{2,1,0:T(8,128)(2,1)}), bf16[64,8,256]{2,1,0:T(8,128)(2,1)S(1)}, u32[]{:S(2)}, u32[]{:S(2)}) async-start(bf16[64,8,256]{2,1,0:T(8,128)(2,1)} %bitcast.4), calls=%async_computation.1 | async-start | bytes 524288 | tf_op jit(solution)/shard_map/all_to_all | solution.py:303
  73.4 0.1 reshape.32.owner_ref
  73.4 0.4 shard_map.73.chooser
  73.9 11.0 %all-to-all-done.1 = bf16[64,8,256]{2,1,0:T(8,128)(2,1)S(1)} async-done(((bf16[64,8,256]{2,1,0:T(8,128)(2,1)}), bf16[64,8,256]{2,1,0:T(8,128)(2,1)S(1)}, u32[]{:S(2)}, u32[]{:S(2)}) %all-to-all-start.1) | async-done | bytes 262176 | tf_op jit(solution)/shard_map/all_to_all | solution.py:303
  84.9 0.2 shard_map.78
  85.1 9.1 %all_to_all.20.x_ref = bf16[3,64,256]{2,1,0:T(8,128)(2,1)S(1)} all-to-all(bf16[3,64,256]{2,1,0:T(8,128)(2,1)S(1)} %bitcast.31), channel_id=1, replica_groups=mesh['x'=4,'y'=8,'c'=2,'q'=4,'j'=3] {'j'}, dimensions={0} | all-to-all | bytes 196608 | tf_op jit(solution)/shard_map/all_to_all | solution.py:313
  94.2 2.9 %project.1 = bf16[4,16,4096]{2,1,0:T(8,128)(2,1)S(1)} custom-call(bf16[3,64,256]{2,1,0:T(8,128)(2,1)S(1)} %all_to_all.20.x_ref, bf16[256,4096]{1,0:T(8,128)(2,1)} %w0.1, bf16[256,4096]{1,0:T(8,128)(2,1)} %collective-permute-done.7.w1, bf16[256,4096]{1,0:T(8,128)(2,1)S(1)} %collective-permute-done.8.w2), custom_call_target="tpu_custom_call" | custom-call | tf_op jit(solution)/shard_map/project/pallas_call | solution.py:317
  97.2 36.8 %all_to_all.21 = bf16[4,16,4096]{2,1,0:T(8,128)(2,1)S(1)} all-to-all(bf16[4,16,4096]{2,1,0:T(8,128)(2,1)S(1)} %project.1), channel_id=1, replica_groups=mesh['x'=4,'y'=8,'c'=2,'q'=4,'j'=3] {'q'}, dimensions={0} | all-to-all | bytes 1048576 | tf_op jit(solution)/shard_map/all_to_all | solution.py:326
  134.0 0.7 fusion
  (12 shorter events, 0.0 us)
Async XLA Ops:
  0.0 34.0 %copy-start = (bf16[192,256]{1,0:T(8,128)(2,1)S(1)}, bf16[192,256]{1,0:T(8,128)(2,1)}, u32[]{:S(2)}) copy-start(bf16[192,256]{1,0:T(8,128)(2,1)} %refs_0_.1) | copy-start | bytes 294916
  0.0 42.9 %copy-start.1 = (s32[24]{0:T(128)S(1)}, s32[24]{0:T(128)}, u32[]{:S(2)}) copy-start(s32[24]{0:T(128)} %lengths.3) | copy-start | bytes 292
  0.0 47.4 %copy-start.3 = (s32[12288]{0:T(1024)S(1)}, s32[12288]{0:T(1024)}, u32[]{:S(2)}) copy-start(s32[12288]{0:T(1024)} %param.11) | copy-start | bytes 147460
  1.9 30.2 %all-to-all-start = ((bf16[8,192,256]{2,1,0:T(8,128)(2,1)}), bf16[8,192,256]{2,1,0:T(8,128)(2,1)S(1)}, u32[]{:S(2)}, u32[]{:S(2)}) async-start(bf16[8,192,256]{2,1,0:T(8,128)(2,1)} %prepare.1), calls=%async_computation | async-start | bytes 1572864 | tf_op jit(solution)/shard_map/all_to_all | solution.py:271
  9.0 53.1 %collective-permute-start.7 = (bf16[256,4096]{1,0:T(8,128)(2,1)}, bf16[256,4096]{1,0:T(8,128)(2,1)}, u32[]{:S(2)}, u32[]{:S(2)}) collective-permute-start(bf16[256,4096]{1,0:T(8,128)(2,1)} %w0.1), channel_id=1, source_target_pairs={{0,1},{1,2},{2,0},{12,14},{13,12},{14,13},{3,4},{4,5},{5,3},{15,17... | collective-permute-start | bytes 6291464 | tf_op jit(solution)/shard_map/ppermute | solution.py:258
  32.1 10.8 %collective-permute-start = (bf16[1536,256]{1,0:T(8,128)(2,1)S(1)}, bf16[1536,256]{1,0:T(8,128)(2,1)S(1)}, u32[]{:S(2)}, u32[]{:S(2)}) collective-permute-start(bf16[1536,256]{1,0:T(8,128)(2,1)S(1)} %bitcast.27), channel_id=1, source_target_pairs={{0,12},{12,0},{1,13},{13,1},{2,14},{14,2},{3,15},{15,3},{4,16},{16... | collective-permute-start | bytes 2359304 | tf_op jit(solution)/shard_map/ppermute | solution.py:273
  34.0 6.5 %collective-permute-start.1 = (bf16[192,256]{1,0:T(8,128)(2,1)S(1)}, bf16[192,256]{1,0:T(8,128)(2,1)S(1)}, u32[]{:S(2)}, u32[]{:S(2)}) collective-permute-start(bf16[192,256]{1,0:T(8,128)(2,1)S(1)} %copy-done), channel_id=1, source_target_pairs={{192,0},{384,192},{576,384},{193,1},{385,193},{577,385},{194,2},{3... | collective-permute-start | bytes 294920 | tf_op jit(solution)/shard_map/ppermute | solution.py:272
  36.8 6.1 %collective-permute-start.3 = (bf16[192,256]{1,0:T(8,128)(2,1)S(1)}, bf16[192,256]{1,0:T(8,128)(2,1)S(1)}, u32[]{:S(2)}, u32[]{:S(2)}) collective-permute-start(bf16[192,256]{1,0:T(8,128)(2,1)S(1)} %copy-done), channel_id=1, source_target_pairs={{576,0},{577,1},{578,2},{579,3},{580,4},{581,5},{582,6},{583,7},{5... | collective-permute-start | bytes 294920 | tf_op jit(solution)/shard_map/ppermute | solution.py:272
  38.1 4.9 %collective-permute-start.2 = (bf16[192,256]{1,0:T(8,128)(2,1)S(1)}, bf16[192,256]{1,0:T(8,128)(2,1)S(1)}, u32[]{:S(2)}, u32[]{:S(2)}) collective-permute-start(bf16[192,256]{1,0:T(8,128)(2,1)S(1)} %copy-done), channel_id=1, source_target_pairs={{384,0},{576,192},{385,1},{577,193},{386,2},{578,194},{387,3},{579... | collective-permute-start | bytes 294920 | tf_op jit(solution)/shard_map/ppermute | solution.py:272
  43.5 7.1 %collective-permute-start.4 = (bf16[144,384]{1,0:T(8,128)(2,1)S(1)}, bf16[144,384]{1,0:T(8,128)(2,1)S(1)}, u32[]{:S(2)}, u32[]{:S(2)}) collective-permute-start(bf16[144,384]{1,0:T(8,128)(2,1)S(1)} %get-tuple-element.11), channel_id=1, source_target_pairs={{0,192},{192,384},{384,576},{1,193},{193,385},{385,577},{2,194},{1... | collective-permute-start | bytes 331784 | tf_op jit(solution)/shard_map/ppermute | solution.py:291
  44.8 13.8 %collective-permute-start.5 = (bf16[144,384]{1,0:T(8,128)(2,1)S(1)}, bf16[144,384]{1,0:T(8,128)(2,1)S(1)}, u32[]{:S(2)}, u32[]{:S(2)}) collective-permute-start(bf16[144,384]{1,0:T(8,128)(2,1)S(1)} %get-tuple-element.12), channel_id=1, source_target_pairs={{0,384},{192,576},{1,385},{193,577},{2,386},{194,578},{3,387},{195... | collective-permute-start | bytes 331784 | tf_op jit(solution)/shard_map/ppermute | solution.py:291
  46.1 14.8 %collective-permute-start.6 = (bf16[144,384]{1,0:T(8,128)(2,1)S(1)}, bf16[144,384]{1,0:T(8,128)(2,1)S(1)}, u32[]{:S(2)}, u32[]{:S(2)}) collective-permute-start(bf16[144,384]{1,0:T(8,128)(2,1)S(1)} %get-tuple-element.13), channel_id=1, source_target_pairs={{0,576},{1,577},{2,578},{3,579},{4,580},{5,581},{6,582},{7,583},{8... | collective-permute-start | bytes 331784 | tf_op jit(solution)/shard_map/ppermute | solution.py:291
  62.0 23.1 %collective-permute-start.8 = (bf16[256,4096]{1,0:T(8,128)(2,1)}, bf16[256,4096]{1,0:T(8,128)(2,1)S(1)}, u32[]{:S(2)}, u32[]{:S(2)}) collective-permute-start(bf16[256,4096]{1,0:T(8,128)(2,1)} %collective-permute-done.7.w1), channel_id=1, source_target_pairs={{0,12},{12,0},{1,13},{13,1},{2,14},{14,2},{3,15},{15,3},{4,16},{16... | collective-permute-start | bytes 6291464 | tf_op jit(solution)/shard_map/ppermute | solution.py:311
  63.9 21.0 %all-to-all-start.1 = ((bf16[64,8,256]{2,1,0:T(8,128)(2,1)}), bf16[64,8,256]{2,1,0:T(8,128)(2,1)S(1)}, u32[]{:S(2)}, u32[]{:S(2)}) async-start(bf16[64,8,256]{2,1,0:T(8,128)(2,1)} %bitcast.4), calls=%async_computation.1 | async-start | bytes 524288 | tf_op jit(solution)/shard_map/all_to_all | solution.py:303
  94.2 39.7 %copy-start.2 = (bf16[16,4096]{1,0:T(8,128)(2,1)S(1)}, bf16[16,4096]{1,0:T(8,128)(2,1)}, u32[]{:S(2)}) copy-start(bf16[16,4096]{1,0:T(8,128)(2,1)} %param.13) | copy-start | bytes 393220

commit v9 on v8

--- a/solution.py
+++ b/solution.py
@@ -37,15 +37,12 @@
     return (v + jnp.abs(v) * 0.0079).astype(jnp.bfloat16).astype(jnp.float32)
 
 
-def attend_kernel(first, count, lengths, *refs):
-    q_refs, (own_ref, peer_ref), rest = refs[:count], refs[count : count + 2], refs[count + 2 :]
-    out_refs, (q_all, q_s, m_s, l_s, acc_s) = rest[:count], rest[count:]
-    for s, q_ref in enumerate(q_refs):
-        q_all[s] = q_ref[...]
-    x, y, c = (lax.axis_index(a) for a in ("x", "y", "c"))
-
-    def slab(xs, carry):
-        p0 = (xs * (NY * NC) + y * NC + c) * TOK
+def attend_group(lengths, slabs, q_refs, own_ref, peer_ref, out_refs, q_s, m_s, l_s, acc_s):
+    x, c = lax.axis_index("x"), lax.axis_index("c")
+    count = len(slabs)
+    info = []
+    for n, (at_slab, q_ref) in enumerate(zip(slabs, q_refs)):
+        p0 = at_slab * TOK
         last = p0 + TOK - 1
         lane = lax.broadcasted_iota(jnp.int32, (1, QROWS), 1)
         pos = p0 + jnp.where(lane >= TOK, lane - TOK, lane)
@@ -58,80 +55,105 @@
             start = jnp.where(pos >= end, end, start)
             first_start = jnp.where(p0 >= end, end, first_start)
             last_start = jnp.where(last >= end, end, last_start)
-        q_s[:TOK, :] = q_all[xs - x - first, :, :HEAD]
-        q_s[TOK:, :] = q_all[xs - x - first, :, HEAD:]
-        m_s[...] = jnp.full((1, QROWS), FLOOR, jnp.float32)
-        l_s[...] = jnp.zeros((1, QROWS), jnp.float32)
-        acc_s[...] = jnp.zeros((HEAD, QROWS), jnp.float32)
-
-        def chunk(ch, carry):
-            low = (x * NY + ch * CHUNK_SLABS) * NC * TOK
-            high = low + CHUNK_SLABS * NC * TOK - 1
-            rows = pl.ds(pl.multiple_of(ch * CHUNK, CHUNK), CHUNK)
-
-            def update(masked):
-                pieces = []
-                for ref, core in ((own_ref, c), (peer_ref, 1 - c)):
-                    s = lax.dot_general(
-                        ref[rows, :HEAD], q_s[...], NT, preferred_element_type=jnp.float32
-                    )
-                    s = s * SCALE2
-                    if masked:
-                        at = lax.broadcasted_iota(jnp.int32, (CHUNK, 1), 0)
-                        slab_at = jnp.zeros((CHUNK, 1), jnp.int32)
-                        for n in range(1, CHUNK_SLABS):
-                            slab_at += (at >= n * TOK).astype(jnp.int32)
-                        key_pos = low + core * TOK + at + slab_at * ((NC - 1) * TOK)
-                        s = jnp.where((key_pos >= start) & (key_pos <= pos), s, NEG)
-                    pieces.append(s)
-                m_old = m_s[...]
-                top = [jnp.max(s, axis=0, keepdims=True) for s in pieces]
-                m_new = jnp.maximum(m_old, round_up(jnp.maximum(top[0], top[1])))
-                fix = jnp.exp2(m_old - m_new)
-                m_s[...] = m_new
-                total = l_s[...] * fix
-                mixed = acc_s[...] * fix
-                for s, ref in zip(pieces, (own_ref, peer_ref)):
-                    w = jnp.exp2(s - m_new)
-                    total = total + jnp.sum(w, axis=0, keepdims=True)
-                    mixed = mixed + lax.dot_general(
-                        ref[rows, HEAD:],
-                        w.astype(jnp.bfloat16),
-                        TN,
-                        preferred_element_type=jnp.float32,
-                    )
-                l_s[...] = total
-                acc_s[...] = mixed
-
+        info.append((p0, last, pos, start, first_start, last_start))
+        q_s[n * QROWS : n * QROWS + TOK, :] = q_ref[:, :HEAD]
+        q_s[n * QROWS + TOK : (n + 1) * QROWS, :] = q_ref[:, HEAD:]
+    lanes = count * QROWS
+    m_s[:, :lanes] = jnp.full((1, lanes), FLOOR, jnp.float32)
+    l_s[:, :lanes] = jnp.zeros((1, lanes), jnp.float32)
+    acc_s[:, :lanes] = jnp.zeros((HEAD, lanes), jnp.float32)
+
+    def chunk(ch, carry):
+        low = (x * NY + ch * CHUNK_SLABS) * NC * TOK
+        high = low + CHUNK_SLABS * NC * TOK - 1
+        rows = pl.ds(pl.multiple_of(ch * CHUNK, CHUNK), CHUNK)
+
+        def update(here, pos=None, start=None):
+            pieces = []
+            for ref, core in ((own_ref, c), (peer_ref, 1 - c)):
+                s = lax.dot_general(
+                    ref[rows, :HEAD], q_s[here, :], NT, preferred_element_type=jnp.float32
+                )
+                s = s * SCALE2
+                if pos is not None:
+                    at = lax.broadcasted_iota(jnp.int32, (CHUNK, 1), 0)
+                    slab_at = jnp.zeros((CHUNK, 1), jnp.int32)
+                    for n in range(1, CHUNK_SLABS):
+                        slab_at += (at >= n * TOK).astype(jnp.int32)
+                    key_pos = low + core * TOK + at + slab_at * ((NC - 1) * TOK)
+                    s = jnp.where((key_pos >= start) & (key_pos <= pos), s, NEG)
+                pieces.append(s)
+            m_old = m_s[:, here]
+            top = [jnp.max(s, axis=0, keepdims=True) for s in pieces]
+            m_new = jnp.maximum(m_old, round_up(jnp.maximum(top[0], top[1])))
+            fix = jnp.exp2(m_old - m_new)
+            m_s[:, here] = m_new
+            total = l_s[:, here] * fix
+            mixed = acc_s[:, here] * fix
+            for s, ref in zip(pieces, (own_ref, peer_ref)):
+                w = jnp.exp2(s - m_new)
+                total = total + jnp.sum(w, axis=0, keepdims=True)
+                mixed = mixed + lax.dot_general(
+                    ref[rows, HEAD:],
+                    w.astype(jnp.bfloat16),
+                    TN,
+                    preferred_element_type=jnp.float32,
+                )
+            l_s[:, here] = total
+            acc_s[:, here] = mixed
+
+        flags = []
+        together = jnp.bool_(count > 1)
+        for p0, last, pos, start, first_start, last_start in info:
             needed = (low <= last) & (high >= first_start)
             whole = (high <= p0) & (low >= last_start)
-
-            @pl.when(needed & whole)
+            flags.append((needed, whole))
+            together = together & needed & whole
+        if count > 1:
+
+            @pl.when(together)
             def _():
-                update(False)
-
-            @pl.when(needed & jnp.logical_not(whole))
-            def _():
-                update(True)
-
-            return carry
-
-        lax.fori_loop(0, NY // CHUNK_SLABS, chunk, 0)
-
-        total = l_s[...]
+                update(slice(0, lanes))
+
+        for n, (needed, whole) in enumerate(flags):
+            here = slice(n * QROWS, (n + 1) * QROWS)
+            alone = needed & jnp.logical_not(together)
+
+            @pl.when(alone & whole)
+            def _(here=here):
+                update(here)
+
+            @pl.when(alone & jnp.logical_not(whole))
+            def _(here=here, n=n):
+                update(here, info[n][2], info[n][3])
+
+        return carry
+
+    lax.fori_loop(0, NY // CHUNK_SLABS, chunk, 0)
+
+    for n, out_ref in enumerate(out_refs):
+        here = slice(n * QROWS, (n + 1) * QROWS)
+        out_ref[:HEAD, :] = acc_s[:, here].astype(jnp.bfloat16)
+        total = l_s[:, here]
         high_part = total.astype(jnp.bfloat16).astype(jnp.float32)
         rows = lax.broadcasted_iota(jnp.int32, (PART - HEAD, QROWS), 0)
-        stats = jnp.where(rows == 0, m_s[...], jnp.where(rows == 1, high_part, total - high_part))
-        for n, out_ref in enumerate(out_refs):
-
-            @pl.when(xs - x - first == n)
-            def _(out_ref=out_ref):
-                out_ref[:HEAD, :] = acc_s[...].astype(jnp.bfloat16)
-                out_ref[HEAD:, :] = stats.astype(jnp.bfloat16)
-
-        return carry
-
-    lax.fori_loop(x + first, jnp.minimum(x + first + count, NX), slab, 0)
+        stats = jnp.where(
+            rows == 0, m_s[:, here], jnp.where(rows == 1, high_part, total - high_part)
+        )
+        out_ref[HEAD:, :] = stats.astype(jnp.bfloat16)
+
+
+def attend_kernel(first, groups, lengths, *refs):
+    count = sum(groups)
+    q_refs, key_refs, rest = refs[:count], refs[count : count + 2], refs[count + 2 :]
+    out_refs, scratch = rest[:count], rest[count:]
+    x, y, c = (lax.axis_index(a) for a in ("x", "y", "c"))
+    at = 0
+    for size in groups:
+        part = slice(at, at + size)
+        slabs = [(x + first + n) * (NY * NC) + y * NC + c for n in range(at, at + size)]
+        attend_group(lengths, slabs, q_refs[part], *key_refs, out_refs[part], *scratch)
+        at += size
 
 
 def place_kernel(row_ref, col_ref, out_ref):
@@ -217,10 +239,18 @@
         out_ref[n, :, columns] = total[n * OUT : (n + 1) * OUT].astype(jnp.bfloat16)
 
 
-def prepare_kernel(head, k_ref, v_ref, kv_ref):
+def prepare_kernel(k_ref, v_ref, kv_ref, sems):
+    tp = lax.axis_index("q") * NJ + lax.axis_index("j")
+    at = pl.ds(pl.multiple_of(tp * HEADS_HERE // GROUP * HEAD, HEAD), HEAD)
+    copies = []
     for i in range(NY):
-        kv_ref[i, :, :HEAD] = k_ref[...]
-        kv_ref[i, :, HEAD:] = v_ref[...]
+        for n, ref in enumerate((k_ref, v_ref)):
+            to = kv_ref.at[i, :, pl.ds(n * HEAD, HEAD)]
+            copies.append(pltpu.make_async_copy(ref.at[:, at], to, sems.at[i, n]))
+    for copy in copies:
+        copy.start()
+    for copy in copies:
+        copy.wait()
 
 
 def vmem():
@@ -248,7 +278,6 @@
 
 def per_device(queries, keys, values, lengths, mlp_owner, out_weight, residual):
     x, y, c = lax.axis_index("x"), lax.axis_index("y"), lax.axis_index("c")
-    tp = lax.axis_index("q") * NJ + lax.axis_index("j")
     dc = (x * NY + y) * NC + c
     peer = [(0, 1), (1, 0)]
 
@@ -256,41 +285,37 @@
         (k * NJ + i, k * NJ + (i + 1 + k) % NJ) for k in range(NC) for i in range(NJ)
     ]
     turned = lax.ppermute(out_weight, ("c", "j"), around)
-    block = pl.BlockSpec((TOK, HEAD), lambda i, head: (0, head[0]))
     kv = pl.pallas_call(
         prepare_kernel,
         out_shape=jax.ShapeDtypeStruct((NY, TOK, COLS), jnp.bfloat16),
-        grid_spec=pltpu.PrefetchScalarGridSpec(
-            num_scalar_prefetch=1,
-            grid=(1,),
-            in_specs=[block, block],
-            out_specs=pl.BlockSpec((NY, TOK, COLS), lambda i, head: (0, 0, 0)),
-        ),
+        in_specs=[pl.BlockSpec(memory_space=pltpu.HBM)] * 2,
+        out_specs=pl.BlockSpec(memory_space=pltpu.HBM),
+        scratch_shapes=[pltpu.SemaphoreType.DMA((NY, 2))],
         name="prepare",
-    )((tp * HEADS_HERE // GROUP).reshape(1).astype(jnp.int32), keys, values)
+    )(keys, values)
     own = lax.all_to_all(kv, "y", 0, 0, tiled=True).reshape(NY * TOK, COLS)
     moved = [lax.ppermute(queries, "x", [(i, i - s) for i in range(s, NX)]) for s in range(1, NX)]
     other = lax.ppermute(own, "c", peer)
 
-    def attend(first, sent):
+    def attend(first, sent, groups):
+        lanes = max(groups) * QROWS
         return kernel(
-            functools.partial(attend_kernel, first, len(sent)),
+            functools.partial(attend_kernel, first, groups),
             [out_here(PART, QROWS)] * len(sent),
             [smem()] + [vmem()] * (len(sent) + 2),
             scratch_shapes=[
-                pltpu.VMEM((len(sent), TOK, COLS), jnp.bfloat16),
-                pltpu.VMEM((QROWS, HEAD), jnp.bfloat16),
-                pltpu.VMEM((1, QROWS), jnp.float32),
-                pltpu.VMEM((1, QROWS), jnp.float32),
-                pltpu.VMEM((HEAD, QROWS), jnp.float32),
+                pltpu.VMEM((lanes, HEAD), jnp.bfloat16),
+                pltpu.VMEM((1, lanes), jnp.float32),
+                pltpu.VMEM((1, lanes), jnp.float32),
+                pltpu.VMEM((HEAD, lanes), jnp.float32),
             ],
         )(lengths, *map(near_core, (*sent, own, other)))
 
-    away = attend(1, moved)
+    away = attend(1, moved, (2, 1))
     arrived = [
         lax.ppermute(p, "x", [(i, i + s) for i in range(NX - s)]) for s, p in enumerate(away, 1)
     ]
-    home = attend(0, [queries])
+    home = attend(0, [queries], (1,))
 
     targets = lax.dynamic_slice_in_dim(mlp_owner, dc * TOK, TOK, 0)
     placement = kernel(place_kernel, out_here(SLOT_TOTAL, TOK), [vmem(), vmem()])(

time: 135 us -> 158 us (1.17)
  Pallas kernels: 9.42 us -> 33 us
    pallas_call x1, Pallas kernels: 1.85 us -> 25.1 us  [per_device(): pl.pallas_call(prepare_kernel, out_shape=jax.ShapeDtypeStruct((NY, TOK, C...]
where the time goes in v9:
time: 158 us
  blocking collectives  45.9 us (29%)
  waiting for transfers between devices  42.4 us (27%)
  starting transfers between devices  35.5 us (22%)
  Pallas kernels  33 us (21%)
    all_to_all x1, blocking collectives, per_device(): blocks = lax.all_to_all(projected, 'q', 0, 0, tiled=True)  36.8 us
    pallas_call x1, Pallas kernels, per_device(): pl.pallas_call(prepare_kernel, out_shape=jax.ShapeDtypeStruct((NY, TOK, C...  25.1 us
    all_to_all x1, waiting for transfers between devices, per_device(): own = lax.all_to_all(kv, 'y', 0, 0, tiled=True).reshape(NY * TOK, COLS)  18.8 us
    all_to_all x1, waiting for transfers between devices, per_device(): incoming = lax.all_to_all(outgoing, ('x', 'y', 'c'), 0, 0, tiled=True)  11 us
    ppermute x3, waiting for transfers between devices, per_device(): lax.ppermute(p, 'x', [(i, i + s) for i in range(NX - s)])  10.1 us
    all_to_all x1, starting transfers between devices, per_device(): incoming = lax.all_to_all(outgoing, ('x', 'y', 'c'), 0, 0, tiled=True)  9.77 us
    all_to_all x1, blocking collectives, per_device(): lax.all_to_all(owned.reshape(NJ, TOK // NJ, COLS), 'j', 0, 0, tiled=True)  9.12 us
    all_to_all x1, starting transfers between devices, per_device(): own = lax.all_to_all(kv, 'y', 0, 0, tiled=True).reshape(NY * TOK, COLS)  7.11 us
  transfers between devices with their start and end apart: 11, of which 6 were waited for; matrix products, arithmetic and copies ran while one was open for 0% of the time, Pallas kernels for 3%

profile of v9, /device:TPU:6, one launch (start us, length us, event | category | flops | bytes accessed | tf_op | source)
XLA Modules:
  0.0 158.0 jit_solution(17368610602701140107)
XLA Ops:
  0.0 25.1 %prepare.1 = bf16[8,192,256]{2,1,0:T(8,128)(2,1)} custom-call(bf16[192,768]{1,0:T(8,128)(2,1)} %k_ref.1, bf16[192,768]{1,0:T(8,128)(2,1)} %v_ref.1), custom_call_target="tpu_custom_call" | custom-call | tf_op jit(solution)/shard_map/prepare/pallas_call | solution.py:288
  25.1 7.1 %all-to-all-start = ((bf16[8,192,256]{2,1,0:T(8,128)(2,1)}), bf16[8,192,256]{2,1,0:T(8,128)(2,1)S(1)}, u32[]{:S(2)}, u32[]{:S(2)}) async-start(bf16[8,192,256]{2,1,0:T(8,128)(2,1)} %prepare.1), calls=%async_computation | async-start | bytes 1572864 | tf_op jit(solution)/shard_map/all_to_all | solution.py:296
  32.2 4.3 %collective-permute-start.7 = (bf16[256,4096]{1,0:T(8,128)(2,1)}, bf16[256,4096]{1,0:T(8,128)(2,1)}, u32[]{:S(2)}, u32[]{:S(2)}) collective-permute-start(bf16[256,4096]{1,0:T(8,128)(2,1)} %w0.1), channel_id=1, source_target_pairs={{0,1},{1,2},{2,0},{12,14},{13,12},{14,13},{3,4},{4,5},{5,3},{15,17... | collective-permute-start | bytes 6291464 | tf_op jit(solution)/shard_map/ppermute | solution.py:287
  36.5 18.8 %all-to-all-done = bf16[8,192,256]{2,1,0:T(8,128)(2,1)S(1)} async-done(((bf16[8,192,256]{2,1,0:T(8,128)(2,1)}), bf16[8,192,256]{2,1,0:T(8,128)(2,1)S(1)}, u32[]{:S(2)}, u32[]{:S(2)}) %all-to-all-start) | async-done | bytes 786464 | tf_op jit(solution)/shard_map/all_to_all | solution.py:296
  55.3 1.9 %collective-permute-start = (bf16[1536,256]{1,0:T(8,128)(2,1)S(1)}, bf16[1536,256]{1,0:T(8,128)(2,1)S(1)}, u32[]{:S(2)}, u32[]{:S(2)}) collective-permute-start(bf16[1536,256]{1,0:T(8,128)(2,1)S(1)} %bitcast.26), channel_id=1, source_target_pairs={{0,12},{12,0},{1,13},{13,1},{2,14},{14,2},{3,15},{15,3},{4,16},{16... | collective-permute-start | bytes 2359304 | tf_op jit(solution)/shard_map/ppermute | solution.py:298
  57.3 2.7 %collective-permute-start.1 = (bf16[192,256]{1,0:T(8,128)(2,1)S(1)}, bf16[192,256]{1,0:T(8,128)(2,1)S(1)}, u32[]{:S(2)}, u32[]{:S(2)}) collective-permute-start(bf16[192,256]{1,0:T(8,128)(2,1)S(1)} %copy-done), channel_id=1, source_target_pairs={{192,0},{384,192},{576,384},{193,1},{385,193},{577,385},{194,2},{3... | collective-permute-start | bytes 294920 | tf_op jit(solution)/shard_map/ppermute | solution.py:297
  60.0 1.3 collective-permute-start.3
  61.3 2.4 %collective-permute-start.2 = (bf16[192,256]{1,0:T(8,128)(2,1)S(1)}, bf16[192,256]{1,0:T(8,128)(2,1)S(1)}, u32[]{:S(2)}, u32[]{:S(2)}) collective-permute-start(bf16[192,256]{1,0:T(8,128)(2,1)S(1)} %copy-done), channel_id=1, source_target_pairs={{384,0},{576,192},{385,1},{577,193},{386,2},{578,194},{387,3},{579... | collective-permute-start | bytes 294920 | tf_op jit(solution)/shard_map/ppermute | solution.py:297
  63.8 2.4 %collective-permute-done.3.refs_2_ = bf16[192,256]{1,0:T(8,128)(2,1)S(1)} collective-permute-done((bf16[192,256]{1,0:T(8,128)(2,1)S(1)}, bf16[192,256]{1,0:T(8,128)(2,1)S(1)}, u32[]{:S(2)}, u32[]{:S(2)}) %collective-permute-start.3) | collective-permute-done | bytes 98336 | tf_op jit(solution)/shard_map/ppermute | solution.py:297
  66.1 0.0 collective-permute-done.2.refs_1_
  66.2 0.9 shard_map.76
  67.1 1.3 collective-permute-start.4
  68.4 1.3 collective-permute-start.5
  69.7 1.5 collective-permute-start.6
  71.2 0.1 dynamic_slice.3
  71.2 0.1 copy.8.col_ref
  71.4 0.2 shard_map.74.placement
  71.6 2.1 %shard_map.75.refs_0_ = bf16[144,384]{1,0:T(8,128)(2,1)S(1)} custom-call(s32[24]{0:T(128)S(1)} %copy-done.1, bf16[192,256]{1,0:T(8,128)(2,1)S(1)} %copy-done, bf16[1536,256]{1,0:T(8,128)(2,1)S(1)} %bitcast.28, bf16[1536,256]{1,0:T(8,128)(2,1)S(1)} %collective-permute-done.refs_2_.refs_4_), custom_call_target="tpu_custom_call" | custom-call | tf_op jit(solution)/shard_map/pallas_call | solution.py:302
  73.7 0.3 collective-permute-done.4.refs_1_
  74.0 7.5 %collective-permute-done.5.refs_2_ = bf16[144,384]{1,0:T(8,128)(2,1)S(1)} collective-permute-done((bf16[144,384]{1,0:T(8,128)(2,1)S(1)}, bf16[144,384]{1,0:T(8,128)(2,1)S(1)}, u32[]{:S(2)}, u32[]{:S(2)}) %collective-permute-start.5) | collective-permute-done | bytes 110624 | tf_op jit(solution)/shard_map/ppermute | solution.py:316
  81.5 2.3 %collective-permute-done.6.refs_3_ = bf16[144,384]{1,0:T(8,128)(2,1)S(1)} collective-permute-done((bf16[144,384]{1,0:T(8,128)(2,1)S(1)}, bf16[144,384]{1,0:T(8,128)(2,1)S(1)}, u32[]{:S(2)}, u32[]{:S(2)}) %collective-permute-start.6) | collective-permute-done | bytes 110624 | tf_op jit(solution)/shard_map/ppermute | solution.py:316
  83.8 1.1 shard_map.77
  84.9 1.9 %collective-permute-start.8 = (bf16[256,4096]{1,0:T(8,128)(2,1)}, bf16[256,4096]{1,0:T(8,128)(2,1)S(1)}, u32[]{:S(2)}, u32[]{:S(2)}) collective-permute-start(bf16[256,4096]{1,0:T(8,128)(2,1)} %collective-permute-done.7.w1), channel_id=1, source_target_pairs={{0,12},{12,0},{1,13},{13,1},{2,14},{14,2},{3,15},{15,3},{4,16},{16... | collective-permute-start | bytes 6291464 | tf_op jit(solution)/shard_map/ppermute | solution.py:336
  86.8 9.8 %all-to-all-start.1 = ((bf16[64,8,256]{2,1,0:T(8,128)(2,1)}), bf16[64,8,256]{2,1,0:T(8,128)(2,1)S(1)}, u32[]{:S(2)}, u32[]{:S(2)}) async-start(bf16[64,8,256]{2,1,0:T(8,128)(2,1)} %bitcast.3), calls=%async_computation.1 | async-start | bytes 524288 | tf_op jit(solution)/shard_map/all_to_all | solution.py:328
  96.6 0.1 reshape.29.owner_ref
  96.7 0.4 shard_map.73.chooser
  97.1 11.0 %all-to-all-done.1 = bf16[64,8,256]{2,1,0:T(8,128)(2,1)S(1)} async-done(((bf16[64,8,256]{2,1,0:T(8,128)(2,1)}), bf16[64,8,256]{2,1,0:T(8,128)(2,1)S(1)}, u32[]{:S(2)}, u32[]{:S(2)}) %all-to-all-start.1) | async-done | bytes 262176 | tf_op jit(solution)/shard_map/all_to_all | solution.py:328
  108.2 0.2 shard_map.78
  108.4 9.1 %all_to_all.20.x_ref = bf16[3,64,256]{2,1,0:T(8,128)(2,1)S(1)} all-to-all(bf16[3,64,256]{2,1,0:T(8,128)(2,1)S(1)} %bitcast.30), channel_id=1, replica_groups=mesh['x'=4,'y'=8,'c'=2,'q'=4,'j'=3] {'j'}, dimensions={0} | all-to-all | bytes 196608 | tf_op jit(solution)/shard_map/all_to_all | solution.py:338
  117.5 2.9 %project.1 = bf16[4,16,4096]{2,1,0:T(8,128)(2,1)S(1)} custom-call(bf16[3,64,256]{2,1,0:T(8,128)(2,1)S(1)} %all_to_all.20.x_ref, bf16[256,4096]{1,0:T(8,128)(2,1)} %w0.1, bf16[256,4096]{1,0:T(8,128)(2,1)} %collective-permute-done.7.w1, bf16[256,4096]{1,0:T(8,128)(2,1)S(1)} %collective-permute-done.8.w2), custom_call_target="tpu_custom_call" | custom-call | tf_op jit(solution)/shard_map/project/pallas_call | solution.py:342
  120.4 36.8 %all_to_all.21 = bf16[4,16,4096]{2,1,0:T(8,128)(2,1)S(1)} all-to-all(bf16[4,16,4096]{2,1,0:T(8,128)(2,1)S(1)} %project.1), channel_id=1, replica_groups=mesh['x'=4,'y'=8,'c'=2,'q'=4,'j'=3] {'q'}, dimensions={0} | all-to-all | bytes 1048576 | tf_op jit(solution)/shard_map/all_to_all | solution.py:351
  157.2 0.7 fusion
  (12 shorter events, 0.0 us)
Async XLA Ops:
  0.0 57.3 %copy-start = (bf16[192,256]{1,0:T(8,128)(2,1)S(1)}, bf16[192,256]{1,0:T(8,128)(2,1)}, u32[]{:S(2)}) copy-start(bf16[192,256]{1,0:T(8,128)(2,1)} %refs_0_.1) | copy-start | bytes 294916
  0.0 66.2 %copy-start.1 = (s32[24]{0:T(128)S(1)}, s32[24]{0:T(128)}, u32[]{:S(2)}) copy-start(s32[24]{0:T(128)} %lengths.3) | copy-start | bytes 292
  0.0 71.1 %copy-start.3 = (s32[12288]{0:T(1024)S(1)}, s32[12288]{0:T(1024)}, u32[]{:S(2)}) copy-start(s32[12288]{0:T(1024)} %param.11) | copy-start | bytes 147460
  25.1 30.2 %all-to-all-start = ((bf16[8,192,256]{2,1,0:T(8,128)(2,1)}), bf16[8,192,256]{2,1,0:T(8,128)(2,1)S(1)}, u32[]{:S(2)}, u32[]{:S(2)}) async-start(bf16[8,192,256]{2,1,0:T(8,128)(2,1)} %prepare.1), calls=%async_computation | async-start | bytes 1572864 | tf_op jit(solution)/shard_map/all_to_all | solution.py:296
  32.2 52.7 %collective-permute-start.7 = (bf16[256,4096]{1,0:T(8,128)(2,1)}, bf16[256,4096]{1,0:T(8,128)(2,1)}, u32[]{:S(2)}, u32[]{:S(2)}) collective-permute-start(bf16[256,4096]{1,0:T(8,128)(2,1)} %w0.1), channel_id=1, source_target_pairs={{0,1},{1,2},{2,0},{12,14},{13,12},{14,13},{3,4},{4,5},{5,3},{15,17... | collective-permute-start | bytes 6291464 | tf_op jit(solution)/shard_map/ppermute | solution.py:287
  55.3 10.8 %collective-permute-start = (bf16[1536,256]{1,0:T(8,128)(2,1)S(1)}, bf16[1536,256]{1,0:T(8,128)(2,1)S(1)}, u32[]{:S(2)}, u32[]{:S(2)}) collective-permute-start(bf16[1536,256]{1,0:T(8,128)(2,1)S(1)} %bitcast.26), channel_id=1, source_target_pairs={{0,12},{12,0},{1,13},{13,1},{2,14},{14,2},{3,15},{15,3},{4,16},{16... | collective-permute-start | bytes 2359304 | tf_op jit(solution)/shard_map/ppermute | solution.py:298
  57.3 6.5 %collective-permute-start.1 = (bf16[192,256]{1,0:T(8,128)(2,1)S(1)}, bf16[192,256]{1,0:T(8,128)(2,1)S(1)}, u32[]{:S(2)}, u32[]{:S(2)}) collective-permute-start(bf16[192,256]{1,0:T(8,128)(2,1)S(1)} %copy-done), channel_id=1, source_target_pairs={{192,0},{384,192},{576,384},{193,1},{385,193},{577,385},{194,2},{3... | collective-permute-start | bytes 294920 | tf_op jit(solution)/shard_map/ppermute | solution.py:297
  60.0 6.1 %collective-permute-start.3 = (bf16[192,256]{1,0:T(8,128)(2,1)S(1)}, bf16[192,256]{1,0:T(8,128)(2,1)S(1)}, u32[]{:S(2)}, u32[]{:S(2)}) collective-permute-start(bf16[192,256]{1,0:T(8,128)(2,1)S(1)} %copy-done), channel_id=1, source_target_pairs={{576,0},{577,1},{578,2},{579,3},{580,4},{581,5},{582,6},{583,7},{5... | collective-permute-start | bytes 294920 | tf_op jit(solution)/shard_map/ppermute | solution.py:297
  61.3 4.9 %collective-permute-start.2 = (bf16[192,256]{1,0:T(8,128)(2,1)S(1)}, bf16[192,256]{1,0:T(8,128)(2,1)S(1)}, u32[]{:S(2)}, u32[]{:S(2)}) collective-permute-start(bf16[192,256]{1,0:T(8,128)(2,1)S(1)} %copy-done), channel_id=1, source_target_pairs={{384,0},{576,192},{385,1},{577,193},{386,2},{578,194},{387,3},{579... | collective-permute-start | bytes 294920 | tf_op jit(solution)/shard_map/ppermute | solution.py:297
  67.1 6.9 %collective-permute-start.4 = (bf16[144,384]{1,0:T(8,128)(2,1)S(1)}, bf16[144,384]{1,0:T(8,128)(2,1)S(1)}, u32[]{:S(2)}, u32[]{:S(2)}) collective-permute-start(bf16[144,384]{1,0:T(8,128)(2,1)S(1)} %get-tuple-element.11), channel_id=1, source_target_pairs={{0,192},{192,384},{384,576},{1,193},{193,385},{385,577},{2,194},{1... | collective-permute-start | bytes 331784 | tf_op jit(solution)/shard_map/ppermute | solution.py:316
  68.4 13.2 %collective-permute-start.5 = (bf16[144,384]{1,0:T(8,128)(2,1)S(1)}, bf16[144,384]{1,0:T(8,128)(2,1)S(1)}, u32[]{:S(2)}, u32[]{:S(2)}) collective-permute-start(bf16[144,384]{1,0:T(8,128)(2,1)S(1)} %get-tuple-element.12), channel_id=1, source_target_pairs={{0,384},{192,576},{1,385},{193,577},{2,386},{194,578},{3,387},{195... | collective-permute-start | bytes 331784 | tf_op jit(solution)/shard_map/ppermute | solution.py:316
  69.7 14.1 %collective-permute-start.6 = (bf16[144,384]{1,0:T(8,128)(2,1)S(1)}, bf16[144,384]{1,0:T(8,128)(2,1)S(1)}, u32[]{:S(2)}, u32[]{:S(2)}) collective-permute-start(bf16[144,384]{1,0:T(8,128)(2,1)S(1)} %get-tuple-element.13), channel_id=1, source_target_pairs={{0,576},{1,577},{2,578},{3,579},{4,580},{5,581},{6,582},{7,583},{8... | collective-permute-start | bytes 331784 | tf_op jit(solution)/shard_map/ppermute | solution.py:316
  84.9 23.4 %collective-permute-start.8 = (bf16[256,4096]{1,0:T(8,128)(2,1)}, bf16[256,4096]{1,0:T(8,128)(2,1)S(1)}, u32[]{:S(2)}, u32[]{:S(2)}) collective-permute-start(bf16[256,4096]{1,0:T(8,128)(2,1)} %collective-permute-done.7.w1), channel_id=1, source_target_pairs={{0,12},{12,0},{1,13},{13,1},{2,14},{14,2},{3,15},{15,3},{4,16},{16... | collective-permute-start | bytes 6291464 | tf_op jit(solution)/shard_map/ppermute | solution.py:336
  86.8 21.3 %all-to-all-start.1 = ((bf16[64,8,256]{2,1,0:T(8,128)(2,1)}), bf16[64,8,256]{2,1,0:T(8,128)(2,1)S(1)}, u32[]{:S(2)}, u32[]{:S(2)}) async-start(bf16[64,8,256]{2,1,0:T(8,128)(2,1)} %bitcast.3), calls=%async_computation.1 | async-start | bytes 524288 | tf_op jit(solution)/shard_map/all_to_all | solution.py:328
  117.5 39.7 %copy-start.2 = (bf16[16,4096]{1,0:T(8,128)(2,1)S(1)}, bf16[16,4096]{1,0:T(8,128)(2,1)}, u32[]{:S(2)}) copy-start(bf16[16,4096]{1,0:T(8,128)(2,1)} %param.13) | copy-start | bytes 393220

commit v10 on v9

--- a/solution.py
+++ b/solution.py
@@ -239,18 +239,10 @@
         out_ref[n, :, columns] = total[n * OUT : (n + 1) * OUT].astype(jnp.bfloat16)
 
 
-def prepare_kernel(k_ref, v_ref, kv_ref, sems):
-    tp = lax.axis_index("q") * NJ + lax.axis_index("j")
-    at = pl.ds(pl.multiple_of(tp * HEADS_HERE // GROUP * HEAD, HEAD), HEAD)
-    copies = []
+def prepare_kernel(head, k_ref, v_ref, kv_ref):
     for i in range(NY):
-        for n, ref in enumerate((k_ref, v_ref)):
-            to = kv_ref.at[i, :, pl.ds(n * HEAD, HEAD)]
-            copies.append(pltpu.make_async_copy(ref.at[:, at], to, sems.at[i, n]))
-    for copy in copies:
-        copy.start()
-    for copy in copies:
-        copy.wait()
+        kv_ref[i, :, :HEAD] = k_ref[...]
+        kv_ref[i, :, HEAD:] = v_ref[...]
 
 
 def vmem():
@@ -278,6 +270,7 @@
 
 def per_device(queries, keys, values, lengths, mlp_owner, out_weight, residual):
     x, y, c = lax.axis_index("x"), lax.axis_index("y"), lax.axis_index("c")
+    tp = lax.axis_index("q") * NJ + lax.axis_index("j")
     dc = (x * NY + y) * NC + c
     peer = [(0, 1), (1, 0)]
 
@@ -285,14 +278,18 @@
         (k * NJ + i, k * NJ + (i + 1 + k) % NJ) for k in range(NC) for i in range(NJ)
     ]
     turned = lax.ppermute(out_weight, ("c", "j"), around)
+    block = pl.BlockSpec((TOK, HEAD), lambda i, head: (0, head[0]))
     kv = pl.pallas_call(
         prepare_kernel,
         out_shape=jax.ShapeDtypeStruct((NY, TOK, COLS), jnp.bfloat16),
-        in_specs=[pl.BlockSpec(memory_space=pltpu.HBM)] * 2,
-        out_specs=pl.BlockSpec(memory_space=pltpu.HBM),
-        scratch_shapes=[pltpu.SemaphoreType.DMA((NY, 2))],
+        grid_spec=pltpu.PrefetchScalarGridSpec(
+            num_scalar_prefetch=1,
+            grid=(1,),
+            in_specs=[block, block],
+            out_specs=pl.BlockSpec((NY, TOK, COLS), lambda i, head: (0, 0, 0)),
+        ),
         name="prepare",
-    )(keys, values)
+    )((tp * HEADS_HERE // GROUP).reshape(1).astype(jnp.int32), keys, values)
     own = lax.all_to_all(kv, "y", 0, 0, tiled=True).reshape(NY * TOK, COLS)
     moved = [lax.ppermute(queries, "x", [(i, i - s) for i in range(s, NX)]) for s in range(1, NX)]
     other = lax.ppermute(own, "c", peer)

time: 158 us -> 135 us (0.85)
  Pallas kernels: 33 us -> 9.73 us
    pallas_call x1, Pallas kernels: 25.1 us -> 1.85 us  [per_device(): pl.pallas_call(prepare_kernel, out_shape=jax.ShapeDtypeStruct((NY, TOK, C...]
  transfers between devices with their start and end apart: 11 -> 11, of which waited for: 6 -> 6; matrix products, arithmetic and copies ran while one was open for 0% -> 0% of each run, Pallas kernels for 3% -> 4%
where the time goes in v10:
time: 135 us
  blocking collectives  45.9 us (34%)
  waiting for transfers between devices  42.4 us (31%)
  starting transfers between devices  35.5 us (26%)
  Pallas kernels  9.73 us (7%)
    all_to_all x1, blocking collectives, per_device(): blocks = lax.all_to_all(projected, 'q', 0, 0, tiled=True)  36.8 us
    all_to_all x1, waiting for transfers between devices, per_device(): own = lax.all_to_all(kv, 'y', 0, 0, tiled=True).reshape(NY * TOK, COLS)  18.8 us
    all_to_all x1, waiting for transfers between devices, per_device(): incoming = lax.all_to_all(outgoing, ('x', 'y', 'c'), 0, 0, tiled=True)  11 us
    ppermute x3, waiting for transfers between devices, per_device(): lax.ppermute(p, 'x', [(i, i + s) for i in range(NX - s)])  10.1 us
    all_to_all x1, starting transfers between devices, per_device(): incoming = lax.all_to_all(outgoing, ('x', 'y', 'c'), 0, 0, tiled=True)  9.77 us
    all_to_all x1, blocking collectives, per_device(): lax.all_to_all(owned.reshape(NJ, TOK // NJ, COLS), 'j', 0, 0, tiled=True)  9.13 us
    all_to_all x1, starting transfers between devices, per_device(): own = lax.all_to_all(kv, 'y', 0, 0, tiled=True).reshape(NY * TOK, COLS)  7.1 us
    ppermute x3, starting transfers between devices, per_device(): lax.ppermute(queries, 'x', [(i, i - s) for i in range(s, NX)])  6.47 us
  transfers between devices with their start and end apart: 11, of which 6 were waited for; matrix products, arithmetic and copies ran while one was open for 0% of the time, Pallas kernels for 4%

profile of v10, /device:TPU:6, one launch (start us, length us, event | category | flops | bytes accessed | tf_op | source)
XLA Modules:
  0.0 134.7 jit_solution(9553988155436193957)
XLA Ops:
  0.0 1.8 %prepare.1 = bf16[8,192,256]{2,1,0:T(8,128)(2,1)} custom-call(s32[1]{0:T(128)} %bitcast.2.head, bf16[192,768]{1,0:T(8,128)(2,1)} %k_ref.1, bf16[192,768]{1,0:T(8,128)(2,1)} %v_ref.1), custom_call_target="tpu_custom_call" | custom-call | tf_op jit(solution)/shard_map/prepare/pallas_call | solution.py:282
  1.9 7.1 %all-to-all-start = ((bf16[8,192,256]{2,1,0:T(8,128)(2,1)}), bf16[8,192,256]{2,1,0:T(8,128)(2,1)S(1)}, u32[]{:S(2)}, u32[]{:S(2)}) async-start(bf16[8,192,256]{2,1,0:T(8,128)(2,1)} %prepare.1), calls=%async_computation | async-start | bytes 1572864 | tf_op jit(solution)/shard_map/all_to_all | solution.py:293
  9.0 4.3 %collective-permute-start.7 = (bf16[256,4096]{1,0:T(8,128)(2,1)}, bf16[256,4096]{1,0:T(8,128)(2,1)}, u32[]{:S(2)}, u32[]{:S(2)}) collective-permute-start(bf16[256,4096]{1,0:T(8,128)(2,1)} %w0.1), channel_id=1, source_target_pairs={{0,1},{1,2},{2,0},{12,14},{13,12},{14,13},{3,4},{4,5},{5,3},{15,17... | collective-permute-start | bytes 6291464 | tf_op jit(solution)/shard_map/ppermute | solution.py:280
  13.2 18.8 %all-to-all-done = bf16[8,192,256]{2,1,0:T(8,128)(2,1)S(1)} async-done(((bf16[8,192,256]{2,1,0:T(8,128)(2,1)}), bf16[8,192,256]{2,1,0:T(8,128)(2,1)S(1)}, u32[]{:S(2)}, u32[]{:S(2)}) %all-to-all-start) | async-done | bytes 786464 | tf_op jit(solution)/shard_map/all_to_all | solution.py:293
  32.1 1.9 %collective-permute-start = (bf16[1536,256]{1,0:T(8,128)(2,1)S(1)}, bf16[1536,256]{1,0:T(8,128)(2,1)S(1)}, u32[]{:S(2)}, u32[]{:S(2)}) collective-permute-start(bf16[1536,256]{1,0:T(8,128)(2,1)S(1)} %bitcast.27), channel_id=1, source_target_pairs={{0,12},{12,0},{1,13},{13,1},{2,14},{14,2},{3,15},{15,3},{4,16},{16... | collective-permute-start | bytes 2359304 | tf_op jit(solution)/shard_map/ppermute | solution.py:295
  34.0 2.7 %collective-permute-start.1 = (bf16[192,256]{1,0:T(8,128)(2,1)S(1)}, bf16[192,256]{1,0:T(8,128)(2,1)S(1)}, u32[]{:S(2)}, u32[]{:S(2)}) collective-permute-start(bf16[192,256]{1,0:T(8,128)(2,1)S(1)} %copy-done), channel_id=1, source_target_pairs={{192,0},{384,192},{576,384},{193,1},{385,193},{577,385},{194,2},{3... | collective-permute-start | bytes 294920 | tf_op jit(solution)/shard_map/ppermute | solution.py:294
  36.8 1.3 collective-permute-start.3
  38.1 2.4 %collective-permute-start.2 = (bf16[192,256]{1,0:T(8,128)(2,1)S(1)}, bf16[192,256]{1,0:T(8,128)(2,1)S(1)}, u32[]{:S(2)}, u32[]{:S(2)}) collective-permute-start(bf16[192,256]{1,0:T(8,128)(2,1)S(1)} %copy-done), channel_id=1, source_target_pairs={{384,0},{576,192},{385,1},{577,193},{386,2},{578,194},{387,3},{579... | collective-permute-start | bytes 294920 | tf_op jit(solution)/shard_map/ppermute | solution.py:294
  40.5 2.4 %collective-permute-done.3.refs_2_ = bf16[192,256]{1,0:T(8,128)(2,1)S(1)} collective-permute-done((bf16[192,256]{1,0:T(8,128)(2,1)S(1)}, bf16[192,256]{1,0:T(8,128)(2,1)S(1)}, u32[]{:S(2)}, u32[]{:S(2)}) %collective-permute-start.3) | collective-permute-done | bytes 98336 | tf_op jit(solution)/shard_map/ppermute | solution.py:294
  42.9 0.0 collective-permute-done.2.refs_1_
  42.9 0.9 shard_map.76
  43.8 1.3 collective-permute-start.4
  45.1 1.3 collective-permute-start.5
  46.4 1.5 %collective-permute-start.6 = (bf16[144,384]{1,0:T(8,128)(2,1)S(1)}, bf16[144,384]{1,0:T(8,128)(2,1)S(1)}, u32[]{:S(2)}, u32[]{:S(2)}) collective-permute-start(bf16[144,384]{1,0:T(8,128)(2,1)S(1)} %get-tuple-element.13), channel_id=1, source_target_pairs={{0,576},{1,577},{2,578},{3,579},{4,580},{5,581},{6,582},{7,583},{8... | collective-permute-start | bytes 331784 | tf_op jit(solution)/shard_map/ppermute | solution.py:313
  47.9 0.1 dynamic_slice.3
  48.0 0.1 copy.8.col_ref
  48.1 0.2 shard_map.74.placement
  48.3 2.1 %shard_map.75.refs_0_ = bf16[144,384]{1,0:T(8,128)(2,1)S(1)} custom-call(s32[24]{0:T(128)S(1)} %copy-done.1, bf16[192,256]{1,0:T(8,128)(2,1)S(1)} %copy-done, bf16[1536,256]{1,0:T(8,128)(2,1)S(1)} %bitcast.29, bf16[1536,256]{1,0:T(8,128)(2,1)S(1)} %collective-permute-done.refs_2_.refs_4_), custom_call_target="tpu_custom_call" | custom-call | tf_op jit(solution)/shard_map/pallas_call | solution.py:299
  50.4 0.3 collective-permute-done.4.refs_1_
  50.7 7.6 %collective-permute-done.5.refs_2_ = bf16[144,384]{1,0:T(8,128)(2,1)S(1)} collective-permute-done((bf16[144,384]{1,0:T(8,128)(2,1)S(1)}, bf16[144,384]{1,0:T(8,128)(2,1)S(1)}, u32[]{:S(2)}, u32[]{:S(2)}) %collective-permute-start.5) | collective-permute-done | bytes 110624 | tf_op jit(solution)/shard_map/ppermute | solution.py:313
  58.3 2.3 %collective-permute-done.6.refs_3_ = bf16[144,384]{1,0:T(8,128)(2,1)S(1)} collective-permute-done((bf16[144,384]{1,0:T(8,128)(2,1)S(1)}, bf16[144,384]{1,0:T(8,128)(2,1)S(1)}, u32[]{:S(2)}, u32[]{:S(2)}) %collective-permute-start.6) | collective-permute-done | bytes 110624 | tf_op jit(solution)/shard_map/ppermute | solution.py:313
  60.5 1.1 shard_map.77
  61.7 1.9 %collective-permute-start.8 = (bf16[256,4096]{1,0:T(8,128)(2,1)}, bf16[256,4096]{1,0:T(8,128)(2,1)S(1)}, u32[]{:S(2)}, u32[]{:S(2)}) collective-permute-start(bf16[256,4096]{1,0:T(8,128)(2,1)} %collective-permute-done.7.w1), channel_id=1, source_target_pairs={{0,12},{12,0},{1,13},{13,1},{2,14},{14,2},{3,15},{15,3},{4,16},{16... | collective-permute-start | bytes 6291464 | tf_op jit(solution)/shard_map/ppermute | solution.py:333
  63.6 9.8 %all-to-all-start.1 = ((bf16[64,8,256]{2,1,0:T(8,128)(2,1)}), bf16[64,8,256]{2,1,0:T(8,128)(2,1)S(1)}, u32[]{:S(2)}, u32[]{:S(2)}) async-start(bf16[64,8,256]{2,1,0:T(8,128)(2,1)} %bitcast.4), calls=%async_computation.1 | async-start | bytes 524288 | tf_op jit(solution)/shard_map/all_to_all | solution.py:325
  73.4 0.1 reshape.32.owner_ref
  73.4 0.4 shard_map.73.chooser
  73.9 11.0 %all-to-all-done.1 = bf16[64,8,256]{2,1,0:T(8,128)(2,1)S(1)} async-done(((bf16[64,8,256]{2,1,0:T(8,128)(2,1)}), bf16[64,8,256]{2,1,0:T(8,128)(2,1)S(1)}, u32[]{:S(2)}, u32[]{:S(2)}) %all-to-all-start.1) | async-done | bytes 262176 | tf_op jit(solution)/shard_map/all_to_all | solution.py:325
  84.9 0.2 shard_map.78
  85.1 9.1 %all_to_all.20.x_ref = bf16[3,64,256]{2,1,0:T(8,128)(2,1)S(1)} all-to-all(bf16[3,64,256]{2,1,0:T(8,128)(2,1)S(1)} %bitcast.31), channel_id=1, replica_groups=mesh['x'=4,'y'=8,'c'=2,'q'=4,'j'=3] {'j'}, dimensions={0} | all-to-all | bytes 196608 | tf_op jit(solution)/shard_map/all_to_all | solution.py:335
  94.3 2.9 %project.1 = bf16[4,16,4096]{2,1,0:T(8,128)(2,1)S(1)} custom-call(bf16[3,64,256]{2,1,0:T(8,128)(2,1)S(1)} %all_to_all.20.x_ref, bf16[256,4096]{1,0:T(8,128)(2,1)} %w0.1, bf16[256,4096]{1,0:T(8,128)(2,1)} %collective-permute-done.7.w1, bf16[256,4096]{1,0:T(8,128)(2,1)S(1)} %collective-permute-done.8.w2), custom_call_target="tpu_custom_call" | custom-call | tf_op jit(solution)/shard_map/project/pallas_call | solution.py:339
  97.2 36.8 %all_to_all.21 = bf16[4,16,4096]{2,1,0:T(8,128)(2,1)S(1)} all-to-all(bf16[4,16,4096]{2,1,0:T(8,128)(2,1)S(1)} %project.1), channel_id=1, replica_groups=mesh['x'=4,'y'=8,'c'=2,'q'=4,'j'=3] {'q'}, dimensions={0} | all-to-all | bytes 1048576 | tf_op jit(solution)/shard_map/all_to_all | solution.py:348
  134.0 0.7 fusion
  (12 shorter events, 0.0 us)
Async XLA Ops:
  0.0 34.0 %copy-start = (bf16[192,256]{1,0:T(8,128)(2,1)S(1)}, bf16[192,256]{1,0:T(8,128)(2,1)}, u32[]{:S(2)}) copy-start(bf16[192,256]{1,0:T(8,128)(2,1)} %refs_0_.1) | copy-start | bytes 294916
  0.0 42.9 %copy-start.1 = (s32[24]{0:T(128)S(1)}, s32[24]{0:T(128)}, u32[]{:S(2)}) copy-start(s32[24]{0:T(128)} %lengths.3) | copy-start | bytes 292
  0.0 47.9 %copy-start.3 = (s32[12288]{0:T(1024)S(1)}, s32[12288]{0:T(1024)}, u32[]{:S(2)}) copy-start(s32[12288]{0:T(1024)} %param.11) | copy-start | bytes 147460
  1.9 30.2 %all-to-all-start = ((bf16[8,192,256]{2,1,0:T(8,128)(2,1)}), bf16[8,192,256]{2,1,0:T(8,128)(2,1)S(1)}, u32[]{:S(2)}, u32[]{:S(2)}) async-start(bf16[8,192,256]{2,1,0:T(8,128)(2,1)} %prepare.1), calls=%async_computation | async-start | bytes 1572864 | tf_op jit(solution)/shard_map/all_to_all | solution.py:293
  9.0 52.7 %collective-permute-start.7 = (bf16[256,4096]{1,0:T(8,128)(2,1)}, bf16[256,4096]{1,0:T(8,128)(2,1)}, u32[]{:S(2)}, u32[]{:S(2)}) collective-permute-start(bf16[256,4096]{1,0:T(8,128)(2,1)} %w0.1), channel_id=1, source_target_pairs={{0,1},{1,2},{2,0},{12,14},{13,12},{14,13},{3,4},{4,5},{5,3},{15,17... | collective-permute-start | bytes 6291464 | tf_op jit(solution)/shard_map/ppermute | solution.py:280
  32.1 10.8 %collective-permute-start = (bf16[1536,256]{1,0:T(8,128)(2,1)S(1)}, bf16[1536,256]{1,0:T(8,128)(2,1)S(1)}, u32[]{:S(2)}, u32[]{:S(2)}) collective-permute-start(bf16[1536,256]{1,0:T(8,128)(2,1)S(1)} %bitcast.27), channel_id=1, source_target_pairs={{0,12},{12,0},{1,13},{13,1},{2,14},{14,2},{3,15},{15,3},{4,16},{16... | collective-permute-start | bytes 2359304 | tf_op jit(solution)/shard_map/ppermute | solution.py:295
  34.0 6.5 %collective-permute-start.1 = (bf16[192,256]{1,0:T(8,128)(2,1)S(1)}, bf16[192,256]{1,0:T(8,128)(2,1)S(1)}, u32[]{:S(2)}, u32[]{:S(2)}) collective-permute-start(bf16[192,256]{1,0:T(8,128)(2,1)S(1)} %copy-done), channel_id=1, source_target_pairs={{192,0},{384,192},{576,384},{193,1},{385,193},{577,385},{194,2},{3... | collective-permute-start | bytes 294920 | tf_op jit(solution)/shard_map/ppermute | solution.py:294
  36.8 6.1 %collective-permute-start.3 = (bf16[192,256]{1,0:T(8,128)(2,1)S(1)}, bf16[192,256]{1,0:T(8,128)(2,1)S(1)}, u32[]{:S(2)}, u32[]{:S(2)}) collective-permute-start(bf16[192,256]{1,0:T(8,128)(2,1)S(1)} %copy-done), channel_id=1, source_target_pairs={{576,0},{577,1},{578,2},{579,3},{580,4},{581,5},{582,6},{583,7},{5... | collective-permute-start | bytes 294920 | tf_op jit(solution)/shard_map/ppermute | solution.py:294
  38.1 4.9 %collective-permute-start.2 = (bf16[192,256]{1,0:T(8,128)(2,1)S(1)}, bf16[192,256]{1,0:T(8,128)(2,1)S(1)}, u32[]{:S(2)}, u32[]{:S(2)}) collective-permute-start(bf16[192,256]{1,0:T(8,128)(2,1)S(1)} %copy-done), channel_id=1, source_target_pairs={{384,0},{576,192},{385,1},{577,193},{386,2},{578,194},{387,3},{579... | collective-permute-start | bytes 294920 | tf_op jit(solution)/shard_map/ppermute | solution.py:294
  43.8 6.9 %collective-permute-start.4 = (bf16[144,384]{1,0:T(8,128)(2,1)S(1)}, bf16[144,384]{1,0:T(8,128)(2,1)S(1)}, u32[]{:S(2)}, u32[]{:S(2)}) collective-permute-start(bf16[144,384]{1,0:T(8,128)(2,1)S(1)} %get-tuple-element.11), channel_id=1, source_target_pairs={{0,192},{192,384},{384,576},{1,193},{193,385},{385,577},{2,194},{1... | collective-permute-start | bytes 331784 | tf_op jit(solution)/shard_map/ppermute | solution.py:313
  45.1 13.2 %collective-permute-start.5 = (bf16[144,384]{1,0:T(8,128)(2,1)S(1)}, bf16[144,384]{1,0:T(8,128)(2,1)S(1)}, u32[]{:S(2)}, u32[]{:S(2)}) collective-permute-start(bf16[144,384]{1,0:T(8,128)(2,1)S(1)} %get-tuple-element.12), channel_id=1, source_target_pairs={{0,384},{192,576},{1,385},{193,577},{2,386},{194,578},{3,387},{195... | collective-permute-start | bytes 331784 | tf_op jit(solution)/shard_map/ppermute | solution.py:313
  46.4 14.1 %collective-permute-start.6 = (bf16[144,384]{1,0:T(8,128)(2,1)S(1)}, bf16[144,384]{1,0:T(8,128)(2,1)S(1)}, u32[]{:S(2)}, u32[]{:S(2)}) collective-permute-start(bf16[144,384]{1,0:T(8,128)(2,1)S(1)} %get-tuple-element.13), channel_id=1, source_target_pairs={{0,576},{1,577},{2,578},{3,579},{4,580},{5,581},{6,582},{7,583},{8... | collective-permute-start | bytes 331784 | tf_op jit(solution)/shard_map/ppermute | solution.py:313
  61.7 23.4 %collective-permute-start.8 = (bf16[256,4096]{1,0:T(8,128)(2,1)}, bf16[256,4096]{1,0:T(8,128)(2,1)S(1)}, u32[]{:S(2)}, u32[]{:S(2)}) collective-permute-start(bf16[256,4096]{1,0:T(8,128)(2,1)} %collective-permute-done.7.w1), channel_id=1, source_target_pairs={{0,12},{12,0},{1,13},{13,1},{2,14},{14,2},{3,15},{15,3},{4,16},{16... | collective-permute-start | bytes 6291464 | tf_op jit(solution)/shard_map/ppermute | solution.py:333
  63.6 21.3 %all-to-all-start.1 = ((bf16[64,8,256]{2,1,0:T(8,128)(2,1)}), bf16[64,8,256]{2,1,0:T(8,128)(2,1)S(1)}, u32[]{:S(2)}, u32[]{:S(2)}) async-start(bf16[64,8,256]{2,1,0:T(8,128)(2,1)} %bitcast.4), calls=%async_computation.1 | async-start | bytes 524288 | tf_op jit(solution)/shard_map/all_to_all | solution.py:325
  94.3 39.7 %copy-start.2 = (bf16[16,4096]{1,0:T(8,128)(2,1)S(1)}, bf16[16,4096]{1,0:T(8,128)(2,1)}, u32[]{:S(2)}) copy-start(bf16[16,4096]{1,0:T(8,128)(2,1)} %param.13) | copy-start | bytes 393220
